TPU v7x, 512 devices: a whole 4x4x16 slice. The times are simulated.
512 devices in a mesh: row: 64 (over y, z), col: 8 (over x, core).
Axes of the slice: x: 4, y: 4, z: 16, core: 2. Of those that a mesh axis runs over, the one named last changes fastest.
Arguments:
- sources: bfloat16 [524288, 640], P(('row', 'col')), may hold values from -6 to 6
- tree_perm: int32 [524288], P(('row', 'col')), may hold values from 0 to 524287, as said below
- leaf_blocks: bfloat16 [524288, 512], P(('row', 'col')), may hold values from -0.25 to 0.25
- u_factors: bfloat16 [10, 32, 524288], P(None, None, ('row', 'col')), may hold values from -0.3125 to 0.3125
- v_factors: bfloat16 [10, 32, 524288], P(None, None, ('row', 'col')), as said below
- level_ranks: int32 [10], replicated, may hold values from 16 to 32
Outputs:
- products: bfloat16 [524288, 640], P(('row', 'col'))
Inputs may be any that keep to these rules, and one draw needn't show every extreme that they name: tree_perm is a permutation that maps each aligned block of 1024 positions onto the same block of initial indices. `v_factors`: entries of level l are of the order of the inverse square root of 524288 / 2^l.
All inputs are finite; a program needn't handle non-finite values.
Results may differ from a plain program's by a relative error of at most 0.0037.
Values sent between devices are 32-bit elements; how exact they have to be, the bound alone decides.
No kernel may reach another device: no remote copies, remote signals or barrier semaphores. Data moves between devices by JAX's collectives and lax.ppermute only.
A program may use at most 64 MiB of HBM per device.

v0:
```python
import jax
import jax.numpy as jnp
from jax import lax
from jax.sharding import Mesh
from jax.sharding import PartitionSpec as P

COL = ("col_0", "col_1")
ROW_COL = ("row", "col_0", "col_1")


def partner(x, axis, distance):
    return lax.ppermute(x, axis, [(i, i ^ 1 << distance) for i in range(lax.axis_size(axis))])


def cut_rows(length, count):
    unit = 8 if length >= 8 * count else 1
    return [length // unit * k // count * unit for k in range(1, count)]


def stacked_from(x, axes, order):
    blocks = x
    for k in order:
        blocks = lax.all_gather(blocks, axes[k])
    done = order[::-1]
    back = [done.index(k) for k in range(len(axes))]
    blocks = blocks.transpose(*back, *range(len(axes), blocks.ndim))
    return blocks.reshape(-1, *x.shape)


def laid_out(blocks, dim):
    blocks = jnp.moveaxis(blocks, 0, dim)
    lengths = blocks.shape
    return blocks.reshape(*lengths[:dim], lengths[dim] * lengths[dim + 1], *lengths[dim + 2 :])


def gather_at_once(x, axes, dim):
    split_at = max(range(max(1, x.ndim - 1)), key=lambda d: x.shape[d])
    count, done = (len(axes), [])
    for first, share in enumerate(jnp.split(x, cut_rows(x.shape[split_at], count), axis=split_at)):
        if share.size:
            order = [(first - k) % count for k in range(count)]
            done.append(stacked_from(share, axes, order))
    return laid_out(jnp.concatenate(done, axis=split_at + 1), dim)


def per_device(sources, tree_perm, leaf_blocks, u_factors, v_factors, level_ranks):
    row_count, rhs_count = sources.shape
    leaf_size = leaf_blocks.shape[1]
    level_count, rank_cap, _ = u_factors.shape
    col_size = lax.axis_size(COL)
    col_bits = col_size.bit_length() - 1
    row_bits = lax.axis_size("row").bit_length() - 1
    dev_bits = row_bits + col_bits
    first_row = (lax.axis_index("row") * col_size + lax.axis_index(COL)) * row_count
    local_index = tree_perm - first_row
    ordered = sources[local_index]
    rank_mask = (lax.iota(jnp.int32, rank_cap)[None, :] < level_ranks[:, None]).astype(jnp.float32)
    partial_coef = jnp.einsum(
        "lkn,nr->lkr", v_factors[:dev_bits], ordered, preferred_element_type=jnp.float32
    )
    siblings = [None] * dev_bits
    running = partial_coef
    for bit_pos in range(col_bits):
        finish = dev_bits - 1 - bit_pos
        received = partner(running, COL, bit_pos)
        siblings[finish] = received[finish]
        running = running[:finish] + received[:finish]
    share_width = rhs_count // col_size
    running = lax.dynamic_slice_in_dim(running, lax.axis_index(COL) * share_width, share_width, 2)
    coarse = [None] * row_bits
    for bit_pos in range(row_bits):
        finish = row_bits - 1 - bit_pos
        received = partner(running, "row", bit_pos)
        coarse[finish] = received[finish]
        running = running[:finish] + received[:finish]
    coarse_stack = jnp.stack(coarse)
    coarse_stack = gather_at_once(coarse_stack, COL, 2)
    far_coef = (
        jnp.concatenate([coarse_stack, jnp.stack(siblings[row_bits:])], axis=0)
        * rank_mask[:dev_bits, :, None]
    ).astype(jnp.bfloat16)
    leaf_count = row_count // leaf_size
    result = jnp.einsum(
        "gij,gjr->gir",
        leaf_blocks.reshape(leaf_count, leaf_size, leaf_size),
        ordered.reshape(leaf_count, leaf_size, rhs_count),
        preferred_element_type=jnp.float32,
    ).reshape(row_count, rhs_count)
    result = result + jnp.einsum(
        "lkn,lkr->nr", u_factors[:dev_bits], far_coef, preferred_element_type=jnp.float32
    )
    cluster_rows = row_count >> 9 - dev_bits + 1
    groups = row_count // cluster_rows
    near_coef = jnp.einsum(
        "kgs,gsr->gkr",
        v_factors[9].reshape(rank_cap, groups, cluster_rows),
        ordered.reshape(groups, cluster_rows, rhs_count),
        preferred_element_type=jnp.float32,
    )
    near_coef = near_coef.reshape(groups // 2, 2, rank_cap, rhs_count)[:, ::-1].reshape(
        groups, rank_cap, rhs_count
    )
    near_coef = (near_coef * rank_mask[9][None, :, None]).astype(jnp.bfloat16)
    result = result + jnp.einsum(
        "kgs,gkr->gsr",
        u_factors[9].reshape(rank_cap, groups, cluster_rows),
        near_coef,
        preferred_element_type=jnp.float32,
    ).reshape(row_count, rhs_count)
    return jnp.zeros_like(sources).at[local_index].set(result.astype(jnp.bfloat16))


def solution(mesh):
    torus = Mesh(mesh.devices.reshape(mesh.shape["row"], 4, 2), ("row", "col_0", "col_1"))
    placed = (
        P(ROW_COL, None),
        P(ROW_COL),
        P(ROW_COL, None),
        P(None, None, ROW_COL),
        P(None, None, ROW_COL),
        P(),
    )
    return jax.shard_map(
        per_device, mesh=torus, in_specs=placed, out_specs=P(ROW_COL, None), check_vma=False
    )
```

profile of v0, /device:TPU:1, one launch (start us, length us, event | category | flops | bytes accessed | tf_op | source)
XLA Modules:
  0.0 154.2 jit_solution(17403796162434309323)
XLA Ops:
  1.3 4.0 %gather_fusion = bf16[1024,640]{1,0:T(8,128)(2,1)S(1)} fusion(bf16[1024,640]{1,0:T(8,128)(2,1)S(1)} %copy-done, s32[1024]{0:T(1024)S(1)} %get-tuple-element.5), kind=kCustom, calls=%fused_computation | custom fusion | bytes 2625536 | tf_op jit(solution)/shard_map/gather | solution.py:56
  6.0 8.7 %collective-permute-start = (f32[9,32,640]{2,1,0:T(8,128)S(1)}, f32[9,32,640]{2,1,0:T(8,128)S(1)}, u32[]{:S(2)}, u32[]{:S(2)}) collective-permute-start(f32[9,32,640]{2,1,0:T(8,128)S(1)} %fusion.4), channel_id=1, source_target_pairs={{0,1},{1,0},{2,3},{3,2},{4,5},{5,4},{6,7},{7,6},{8,9},{9,8},{10,11... | collective-permute-start | bytes 2211848 | tf_op jit(solution)/shard_map/ppermute | solution.py:12
  16.7 1.9 %collective-permute-start.1 = (f32[8,32,640]{2,1,0:T(8,128)S(1)}, f32[8,32,640]{2,1,0:T(8,128)S(1)}, u32[]{:S(2)}, u32[]{:S(2)}) collective-permute-start(f32[8,32,640]{2,1,0:T(8,128)S(1)} %slice_add_fusion), channel_id=1, source_target_pairs={{0,2},{1,3},{2,0},{3,1},{4,6},{5,7},{6,4},{7,5},{8,10},{9,11},{10,... | collective-permute-start | bytes 1966088 | tf_op jit(solution)/shard_map/ppermute | solution.py:12
  18.6 15.9 %collective-permute-done.1 = f32[8,32,640]{2,1,0:T(8,128)S(1)} collective-permute-done((f32[8,32,640]{2,1,0:T(8,128)S(1)}, f32[8,32,640]{2,1,0:T(8,128)S(1)}, u32[]{:S(2)}, u32[]{:S(2)}) %collective-permute-start.1) | collective-permute-done | bytes 655392 | tf_op jit(solution)/shard_map/ppermute | solution.py:12
  37.3 14.8 %collective-permute-done.2 = f32[7,32,640]{2,1,0:T(8,128)} collective-permute-done((f32[7,32,640]{2,1,0:T(8,128)S(1)}, f32[7,32,640]{2,1,0:T(8,128)}, u32[]{:S(2)}, u32[]{:S(2)}) %collective-permute-start.2) | collective-permute-done | bytes 573472 | tf_op jit(solution)/shard_map/ppermute | solution.py:12
  53.4 1.9 %collective-permute-start.3 = (f32[6,32,80]{2,1,0:T(8,128)S(1)}, f32[6,32,80]{2,1,0:T(8,128)S(1)}, u32[]{:S(2)}, u32[]{:S(2)}) collective-permute-start(f32[6,32,80]{2,1,0:T(8,128)S(1)} %dynamic-slice_add_fusion), channel_id=1, source_target_pairs={{0,8},{8,0},{16,24},{24,16},{32,40},{40,32},{48,56},{56,48},{64,72... | collective-permute-start | bytes 184328 | tf_op jit(solution)/shard_map/ppermute | solution.py:12
  55.3 2.5 %fusion.20 = f32[2,640,512]{1,2,0:T(8,128)} fusion(bf16[2,512,512]{2,1,0:T(8,128)(2,1)S(1)} %bitcast.49, bf16[2,512,640]{2,1,0:T(8,128)(2,1)S(1)} %bitcast.43), kind=kOutput, calls=%fused_computation.42 | convolution fusion | flops 671088640 | bytes 4980736 | tf_op jit(solution)/shard_map/gij,gjr->gir/dot_general | solution.py:83
  58.8 1.9 %collective-permute-start.4 = (f32[5,32,80]{2,1,0:T(8,128)S(1)}, f32[5,32,80]{2,1,0:T(8,128)S(1)}, u32[]{:S(2)}, u32[]{:S(2)}) collective-permute-start(f32[5,32,80]{2,1,0:T(8,128)S(1)} %slice_add_fusion.2), channel_id=1, source_target_pairs={{0,16},{8,24},{16,0},{24,8},{32,48},{40,56},{48,32},{56,40},{64,80... | collective-permute-start | bytes 153608 | tf_op jit(solution)/shard_map/ppermute | solution.py:12
  61.0 4.7 %collective-permute-done.4 = f32[5,32,80]{2,1,0:T(8,128)S(1)} collective-permute-done((f32[5,32,80]{2,1,0:T(8,128)S(1)}, f32[5,32,80]{2,1,0:T(8,128)S(1)}, u32[]{:S(2)}, u32[]{:S(2)}) %collective-permute-start.4) | collective-permute-done | bytes 51232 | tf_op jit(solution)/shard_map/ppermute | solution.py:12
  65.7 4.9 %collective-permute-start.5 = (f32[4,32,80]{2,1,0:T(8,128)S(1)}, f32[4,32,80]{2,1,0:T(8,128)S(1)}, u32[]{:S(2)}, u32[]{:S(2)}) collective-permute-start(f32[4,32,80]{2,1,0:T(8,128)S(1)} %slice_add_fusion.3), channel_id=1, source_target_pairs={{0,32},{8,40},{16,48},{24,56},{32,0},{40,8},{48,16},{56,24},{64,96... | collective-permute-start | bytes 122888 | tf_op jit(solution)/shard_map/ppermute | solution.py:12
  70.7 5.3 %collective-permute-done.5 = f32[4,32,80]{2,1,0:T(8,128)S(1)} collective-permute-done((f32[4,32,80]{2,1,0:T(8,128)S(1)}, f32[4,32,80]{2,1,0:T(8,128)S(1)}, u32[]{:S(2)}, u32[]{:S(2)}) %collective-permute-start.5) | collective-permute-done | bytes 40992 | tf_op jit(solution)/shard_map/ppermute | solution.py:12
  76.0 10.5 %collective-permute-start.6 = (f32[3,32,80]{2,1,0:T(8,128)S(1)}, f32[3,32,80]{2,1,0:T(8,128)S(1)}, u32[]{:S(2)}, u32[]{:S(2)}) collective-permute-start(f32[3,32,80]{2,1,0:T(8,128)S(1)} %slice_add_fusion.4), channel_id=1, source_target_pairs={{0,64},{8,72},{16,80},{24,88},{32,96},{40,104},{48,112},{56,120},{... | collective-permute-start | bytes 92168 | tf_op jit(solution)/shard_map/ppermute | solution.py:12
  86.6 3.0 %collective-permute-done.6 = f32[3,32,80]{2,1,0:T(8,128)S(1)} collective-permute-done((f32[3,32,80]{2,1,0:T(8,128)S(1)}, f32[3,32,80]{2,1,0:T(8,128)S(1)}, u32[]{:S(2)}, u32[]{:S(2)}) %collective-permute-start.6) | collective-permute-done | bytes 30752 | tf_op jit(solution)/shard_map/ppermute | solution.py:12
  91.6 2.9 %collective-permute-done.7 = f32[2,32,80]{2,1,0:T(8,128)S(1)} collective-permute-done((f32[2,32,80]{2,1,0:T(8,128)S(1)}, f32[2,32,80]{2,1,0:T(8,128)S(1)}, u32[]{:S(2)}, u32[]{:S(2)}) %collective-permute-start.7) | collective-permute-done | bytes 20512 | tf_op jit(solution)/shard_map/ppermute | solution.py:12
  94.5 3.2 %collective-permute-start.8 = (f32[1,32,80]{2,1,0:T(8,128)S(1)}, f32[1,32,80]{2,1,0:T(8,128)S(1)}, u32[]{:S(2)}, u32[]{:S(2)}) collective-permute-start(f32[1,32,80]{2,1,0:T(8,128)S(1)} %slice_add_fusion.6), channel_id=1, source_target_pairs={{0,256},{8,264},{16,272},{24,280},{32,288},{40,296},{48,304},{56,3... | collective-permute-start | bytes 30728 | tf_op jit(solution)/shard_map/ppermute | solution.py:12
  97.8 2.0 %fusion.14 = f32[2,640,512]{1,2,0:T(8,128)} fusion(bf16[2,32,640]{2,1,0:T(8,128)(2,1)S(1)} %multiply_convert_fusion, bf16[32,2,512]{2,1,0:T(2,128)(2,1)S(1)} %reshape_squeeze.7), kind=kOutput, calls=%fused_computation.23 | convolution fusion | flops 41943040 | bytes 2768896 | tf_op jit(solution)/shard_map/kgs,gkr->gsr/dot_general | solution.py:104
  99.8 3.2 %copy.29 = f32[1024,640]{0,1:T(8,128)} copy(f32[1024,640]{1,0:T(8,128)} %bitcast.46) | data formatting | bytes 5242880 | tf_op jit(solution)/shard_map/reshape | solution.py:109
  103.0 3.2 %copy.24 = f32[1024,640]{0,1:T(8,128)} copy(f32[1024,640]{1,0:T(8,128)} %bitcast.45) | data formatting | bytes 5242880 | tf_op jit(solution)/shard_map/reshape | solution.py:88
  107.3 9.1 %all-gather.2 = f32[12,16,80]{2,1,0:T(8,128)S(1)} all-gather(f32[6,16,80]{2,1,0:T(8,128)S(1)} %get-tuple-element.8), channel_id=4, replica_groups=mesh['row'=64,'col_0'=4,'col_1'=2] {'col_1'}, dimensions={0}, use_global_device_ids=true | all-gather | bytes 92160 | tf_op jit(solution)/shard_map/all_gather | solution.py:23
  116.4 10.0 %all-gather = f32[24,16,80]{2,1,0:T(8,128)S(1)} all-gather(f32[6,16,80]{2,1,0:T(8,128)S(1)} %get-tuple-element.7), channel_id=2, replica_groups=mesh['row'=64,'col_0'=4,'col_1'=2] {'col_0'}, dimensions={0}, use_global_device_ids=true | all-gather | bytes 153600 | tf_op jit(solution)/shard_map/all_gather | solution.py:23
  126.4 4.5 %all-gather.1 = f32[8,6,16,80]{3,2,1,0:T(8,128)S(1)} all-gather(f32[4,6,16,80]{3,2,1,0:T(8,128)S(1)} %bitcast.50), channel_id=3, replica_groups=mesh['row'=64,'col_0'=4,'col_1'=2] {'col_1'}, dimensions={0}, use_global_device_ids=true | all-gather | bytes 368640 | tf_op jit(solution)/shard_map/all_gather | solution.py:23
  130.9 10.3 %all-gather.3 = f32[8,6,16,80]{3,2,1,0:T(8,128)S(1)} all-gather(f32[2,6,16,80]{3,2,1,0:T(8,128)S(1)} %bitcast.51), channel_id=5, replica_groups=mesh['row'=64,'col_0'=4,'col_1'=2] {'col_0'}, dimensions={0}, use_global_device_ids=true | all-gather | bytes 307200 | tf_op jit(solution)/shard_map/all_gather | solution.py:23
  142.3 3.7 %fusion.1 = bf16[1024,640]{0,1:T(8,128)(2,1)S(1)} fusion(f32[1024,640]{0,1:T(8,128)} %copy.29, f32[1024,640]{0,1:T(8,128)} %copy.24, bf16[10,32,1024]{2,1,0:T(8,128)(2,1)} %param.9, f32[1,32,640]{2,1,0:T(8,128)S(1)} %slice-done, f32[1,32,640]{2,1,0:T(8,128)S(1)} %slice-done.1, f32[1,32,640]{2,1,0:T(8,128)S(1)} %slice.143, f32[6,32,640]{2,1,0:T(8,128)S(1)} %reshape.36, ...), kind=kOutput, calls=%fused_computation.4 | convolution fusion | flops 380375040 | bytes 7881856 | tf_op jit(solution)/shard_map/lkn,lkr->nr/dot_general | solution.py:89
  147.4 6.8 %scatter_custom_fusion = bf16[1024,640]{1,0:T(8,128)(2,1)} fusion(s32[1024]{0:T(1024)S(1)} %get-tuple-element.6, bf16[1024,640]{1,0:T(8,128)(2,1)} %copy.28, bf16[]{:T(256)} %constant.10.clone.1), kind=kCustom, calls=%fused_computation.13 | custom fusion | bytes 1311232 | tf_op jit(solution)/shard_map/scatter | solution.py:110
  (56 shorter events, 14.6 us)
Async XLA Ops:
  0.0 1.3 copy-start
  1.3 4.0 %copy-start.4 = (bf16[10,32,1024]{2,1,0:T(8,128)(2,1)S(1)}, bf16[10,32,1024]{2,1,0:T(8,128)(2,1)}, u32[]{:S(2)}) copy-start(bf16[10,32,1024]{2,1,0:T(8,128)(2,1)} %param.10) | copy-start | bytes 1966084
  6.0 10.6 %collective-permute-start = (f32[9,32,640]{2,1,0:T(8,128)S(1)}, f32[9,32,640]{2,1,0:T(8,128)S(1)}, u32[]{:S(2)}, u32[]{:S(2)}) collective-permute-start(f32[9,32,640]{2,1,0:T(8,128)S(1)} %fusion.4), channel_id=1, source_target_pairs={{0,1},{1,0},{2,3},{3,2},{4,5},{5,4},{6,7},{7,6},{8,9},{9,8},{10,11... | collective-permute-start | bytes 2211848 | tf_op jit(solution)/shard_map/ppermute | solution.py:12
  16.6 18.0 %copy-start.2 = (f32[9,32,640]{2,1,0:T(8,128)}, f32[9,32,640]{2,1,0:T(8,128)S(1)}, u32[]{:S(2)}) copy-start(f32[9,32,640]{2,1,0:T(8,128)S(1)} %collective-permute-done) | copy-start | bytes 2211844
  16.7 17.8 %collective-permute-start.1 = (f32[8,32,640]{2,1,0:T(8,128)S(1)}, f32[8,32,640]{2,1,0:T(8,128)S(1)}, u32[]{:S(2)}, u32[]{:S(2)}) collective-permute-start(f32[8,32,640]{2,1,0:T(8,128)S(1)} %slice_add_fusion), channel_id=1, source_target_pairs={{0,2},{1,3},{2,0},{3,1},{4,6},{5,7},{6,4},{7,5},{8,10},{9,11},{10,... | collective-permute-start | bytes 1966088 | tf_op jit(solution)/shard_map/ppermute | solution.py:12
  34.5 0.9 copy-start.3
  35.4 16.8 %collective-permute-start.2 = (f32[7,32,640]{2,1,0:T(8,128)S(1)}, f32[7,32,640]{2,1,0:T(8,128)}, u32[]{:S(2)}, u32[]{:S(2)}) collective-permute-start(f32[7,32,640]{2,1,0:T(8,128)S(1)} %slice_add_fusion.1), channel_id=1, source_target_pairs={{0,4},{1,5},{2,6},{3,7},{4,0},{5,1},{6,2},{7,3},{8,12},{9,13},{10,... | collective-permute-start | bytes 1720328 | tf_op jit(solution)/shard_map/ppermute | solution.py:12
  37.3 18.0 %copy-start.1 = (bf16[1024,512]{1,0:T(8,128)(2,1)S(1)}, bf16[1024,512]{1,0:T(8,128)(2,1)}, u32[]{:S(2)}) copy-start(bf16[1024,512]{1,0:T(8,128)(2,1)} %param.8) | copy-start | bytes 3145732
  53.4 5.4 %collective-permute-start.3 = (f32[6,32,80]{2,1,0:T(8,128)S(1)}, f32[6,32,80]{2,1,0:T(8,128)S(1)}, u32[]{:S(2)}, u32[]{:S(2)}) collective-permute-start(f32[6,32,80]{2,1,0:T(8,128)S(1)} %dynamic-slice_add_fusion), channel_id=1, source_target_pairs={{0,8},{8,0},{16,24},{24,16},{32,40},{40,32},{48,56},{56,48},{64,72... | collective-permute-start | bytes 184328 | tf_op jit(solution)/shard_map/ppermute | solution.py:12
  55.3 2.5 %slice-start.2 = ((bf16[10,32,1024]{2,1,0:T(8,128)(2,1)}), bf16[1,32,1024]{2,1,0:T(8,128)(2,1)S(1)}, s32[]{:S(2)}) async-start(bf16[10,32,1024]{2,1,0:T(8,128)(2,1)} %param.10), calls=%async_computation.2 | async-start | bytes 131072 | tf_op jit(solution)/shard_map/slice | solution.py:96
  57.9 12.8 %copy-start.5 = (s32[10]{0:T(128)S(1)}, s32[10]{0:T(128)}, u32[]{:S(2)}) copy-start(s32[10]{0:T(128)} %param.11) | copy-start | bytes 124
  57.9 33.7 %slice-start.3 = ((bf16[10,32,1024]{2,1,0:T(8,128)(2,1)}), bf16[1,32,1024]{2,1,0:T(8,128)(2,1)S(1)}, s32[]{:S(2)}) async-start(bf16[10,32,1024]{2,1,0:T(8,128)(2,1)} %param.9), calls=%async_computation.3 | async-start | bytes 131072 | tf_op jit(solution)/shard_map/slice | solution.py:106
  58.8 7.0 %collective-permute-start.4 = (f32[5,32,80]{2,1,0:T(8,128)S(1)}, f32[5,32,80]{2,1,0:T(8,128)S(1)}, u32[]{:S(2)}, u32[]{:S(2)}) collective-permute-start(f32[5,32,80]{2,1,0:T(8,128)S(1)} %slice_add_fusion.2), channel_id=1, source_target_pairs={{0,16},{8,24},{16,0},{24,8},{32,48},{40,56},{48,32},{56,40},{64,80... | collective-permute-start | bytes 153608 | tf_op jit(solution)/shard_map/ppermute | solution.py:12
  65.7 10.3 %collective-permute-start.5 = (f32[4,32,80]{2,1,0:T(8,128)S(1)}, f32[4,32,80]{2,1,0:T(8,128)S(1)}, u32[]{:S(2)}, u32[]{:S(2)}) collective-permute-start(f32[4,32,80]{2,1,0:T(8,128)S(1)} %slice_add_fusion.3), channel_id=1, source_target_pairs={{0,32},{8,40},{16,48},{24,56},{32,0},{40,8},{48,16},{56,24},{64,96... | collective-permute-start | bytes 122888 | tf_op jit(solution)/shard_map/ppermute | solution.py:12
  76.0 13.5 %collective-permute-start.6 = (f32[3,32,80]{2,1,0:T(8,128)S(1)}, f32[3,32,80]{2,1,0:T(8,128)S(1)}, u32[]{:S(2)}, u32[]{:S(2)}) collective-permute-start(f32[3,32,80]{2,1,0:T(8,128)S(1)} %slice_add_fusion.4), channel_id=1, source_target_pairs={{0,64},{8,72},{16,80},{24,88},{32,96},{40,104},{48,112},{56,120},{... | collective-permute-start | bytes 92168 | tf_op jit(solution)/shard_map/ppermute | solution.py:12
  89.6 4.9 %collective-permute-start.7 = (f32[2,32,80]{2,1,0:T(8,128)S(1)}, f32[2,32,80]{2,1,0:T(8,128)S(1)}, u32[]{:S(2)}, u32[]{:S(2)}) collective-permute-start(f32[2,32,80]{2,1,0:T(8,128)S(1)} %slice_add_fusion.5), channel_id=1, source_target_pairs={{0,128},{8,136},{16,144},{24,152},{32,160},{40,168},{48,176},{56,1... | collective-permute-start | bytes 61448 | tf_op jit(solution)/shard_map/ppermute | solution.py:12
  94.5 12.7 %collective-permute-start.8 = (f32[1,32,80]{2,1,0:T(8,128)S(1)}, f32[1,32,80]{2,1,0:T(8,128)S(1)}, u32[]{:S(2)}, u32[]{:S(2)}) collective-permute-start(f32[1,32,80]{2,1,0:T(8,128)S(1)} %slice_add_fusion.6), channel_id=1, source_target_pairs={{0,256},{8,264},{16,272},{24,280},{32,288},{40,296},{48,304},{56,3... | collective-permute-start | bytes 30728 | tf_op jit(solution)/shard_map/ppermute | solution.py:12
  141.3 0.9 slice-start
  141.4 0.9 slice-start.1
where the time goes:
time: 156 us; the launch traced here: 154 us
  waiting for transfers between devices  49.3 us (32%)
  starting transfers between devices  37 us (24%)
  blocking collectives  33.9 us (22%)
  local copies, waits for them, and re-layouts  23.2 us (15%)
  matrix products  9.2 us (6%)
    ppermute x9, waiting for transfers between devices, partner(): lax.ppermute(x, axis, [(i, i ^ 1 << distance) for i in range(lax.axis_siz...  49.3 us
    ppermute x9, starting transfers between devices, partner(): lax.ppermute(x, axis, [(i, i ^ 1 << distance) for i in range(lax.axis_siz...  37 us
    all_gather x4, blocking collectives, stacked_from(): blocks = lax.all_gather(blocks, axes[k])  33.9 us
    scatter x1, local copies, waits for them, and re-layouts, per_device(): jnp.zeros_like(sources).at[local_index].set(result.astype(jnp.bfloat16))  6.79 us
    gather x1, local copies, waits for them, and re-layouts, per_device(): ordered = sources[local_index]  4.02 us
    dot_general x1, matrix products, per_device(): jnp.einsum('lkn,lkr->nr', u_factors[:dev_bits], far_coef, preferred_eleme...  3.67 us
    reshape x1, local copies, waits for them, and re-layouts, per_device(): result = jnp.einsum('gij,gjr->gir', leaf_blocks.reshape(leaf_count, leaf_...  3.25 us
    reshape x1, local copies, waits for them, and re-layouts, per_device(): result = result + jnp.einsum('kgs,gkr->gsr', u_factors[9].reshape(rank_ca...  3.23 us
  transfers between devices with their start and end apart: 9, of which 8 were waited for; matrix products, arithmetic and copies ran while one was open for 8% of the time, Pallas kernels for 0%

commit v1 on v0

v1 whole, which is shorter than its diff:
```python
import jax
import jax.numpy as jnp
from jax import lax
from jax.experimental import pallas as pl
from jax.experimental.pallas import tpu as pltpu
from jax.sharding import Mesh
from jax.sharding import PartitionSpec as P

AXES = ("y", "zh", "zl", "x", "c")
F32 = jnp.float32
BF16 = jnp.bfloat16
NN = (((1,), (0,)), ((), ()))
NT = (((1,), (1,)), ((), ()))


def dot(a, b, dims=NN):
    return lax.dot_general(a, b, dims, preferred_element_type=F32)


def one_hot_t(perm, first, count):
    n = perm.shape[1]
    j = lax.broadcasted_iota(jnp.int32, (count, n), 0) + first
    return jnp.where(j == perm, 1.0, 0.0).astype(BF16)


def coef_kernel(core, perm_ref, v_ref, s_ref, mine_ref, send_ref, acc):
    n = s_ref.shape[0]
    rank = v_ref.shape[1]
    perm = perm_ref[...] & (n - 1)
    v = v_ref[0:9].reshape(9 * rank, n)
    step = 256
    total = None
    for j in range(0, n, step):
        vp = dot(v, one_hot_t(perm, j, step), NT).astype(BF16)
        part = dot(vp, s_ref[j : j + step, :])
        total = part if total is None else total + part
    half = 4 * rank
    me = core[0]
    mine = pl.ds(pl.multiple_of(me * half, half), half)
    theirs = pl.ds(pl.multiple_of((1 - me) * half, half), half)
    for d in range(acc.shape[0]):
        lanes = slice(d * 128, (d + 1) * 128)
        for level in range(8):
            acc[d, pl.ds(level, rank, stride=8), :] = total[level * rank : (level + 1) * rank, lanes]
        mine_ref[:, lanes] = acc[d, mine, :]
        send_ref[0:half, lanes] = acc[d, theirs, :]
    send_ref[half : half + rank, :] = total[8 * rank : 9 * rank]


def local_kernel(ranks, perm_ref, s_ref, leaf_ref, u_ref, v_ref, near_ref, base_ref, ut_ref, p_ref, pt_ref, ord_ref, lp_ref, uf_ref, us_ref, ue_ref, fe_ref):
    n, _ = s_ref.shape
    leaf = leaf_ref.shape[1]
    rank = u_ref.shape[1]
    perm = perm_ref[...] & (n - 1)
    step = 256
    for j in range(0, n, step):
        pt_ref[j : j + step, :] = one_hot_t(perm, j, step)
    for i in range(0, n, 128):
        column = jnp.broadcast_to(perm[:, i : i + 128], (128, 128)).T
        lane = lax.broadcasted_iota(jnp.int32, (128, 128), 1)
        for j in range(0, n, 128):
            p_ref[i : i + 128, j : j + 128] = jnp.where(column == lane + j, 1.0, 0.0).astype(BF16)

    row = lax.broadcasted_iota(jnp.int32, (rank, n), 0)
    lane_n = lax.broadcasted_iota(jnp.int32, (rank, n), 1)
    for level in range(8):
        kept = jnp.where(row < ranks[level], u_ref[level].astype(F32), 0.0)
        for d in range(n // 128):
            uf_ref[d, pl.ds(level, rank, stride=8), :] = kept[:, d * 128 : (d + 1) * 128]
    for d in range(n // 128):
        us_ref[:, d * 128 : (d + 1) * 128] = uf_ref[d].astype(BF16)
    ue_ref[0:rank, :] = jnp.where(row < ranks[8], u_ref[8].astype(F32), 0.0).astype(BF16)
    last = jnp.where(row < ranks[9], u_ref[9].astype(F32), 0.0)
    ue_ref[rank : 2 * rank, :] = jnp.where(lane_n < leaf, last, 0.0).astype(BF16)
    ue_ref[2 * rank : 3 * rank, :] = jnp.where(lane_n < leaf, 0.0, last).astype(BF16)

    def order(b, _):
        rows = pl.ds(pl.multiple_of(b * step, step), step)
        ord_ref[rows, :] = dot(p_ref[rows, :], s_ref[...]).astype(BF16)
        for g in range(0, n, leaf):
            lp_ref[rows, g : g + leaf] = dot(pt_ref[rows, g : g + leaf], leaf_ref[g : g + leaf, :]).astype(BF16)
        ut_ref[rows, :] = dot(pt_ref[rows, :], us_ref[...], NT).astype(BF16)
        return 0

    lax.fori_loop(0, n // step, order, 0)
    fe_ref[0:rank, :] = near_ref[...].astype(BF16)
    fe_ref[rank : 2 * rank, :] = dot(v_ref[9][:, leaf:], ord_ref[leaf:, :]).astype(BF16)
    fe_ref[2 * rank : 3 * rank, :] = dot(v_ref[9][:, :leaf], ord_ref[:leaf, :]).astype(BF16)

    def apply(b, _):
        rows = pl.ds(pl.multiple_of(b * step, step), step)
        ue = dot(pt_ref[rows, :], ue_ref[...], NT).astype(BF16)
        base_ref[rows, :] = dot(lp_ref[rows, :], ord_ref[...]) + dot(ue, fe_ref[...])
        return 0

    lax.fori_loop(0, n // step, apply, 0)


def level_row(place, p):
    y, zh = place[0], place[1]
    py, pz = p // 4, p % 4
    same = jnp.where(pz == (zh ^ 1), 3, 2)
    return jnp.where(py == y, same, jnp.where(py == (y ^ 1), 1, 0))


def middle_kernel(place, got_ref, out_ref, fine_ref, tot_ref):
    row = lax.broadcasted_iota(jnp.int32, got_ref.shape[1:], 0)
    got = lambda zl, x: got_ref[zl * 4 + x]
    sums = [(got(zl, 0) + got(zl, 1)) + (got(zl, 2) + got(zl, 3)) for zl in range(4)]
    tot_ref[...] = (sums[0] + sums[1]) + (sums[2] + sums[3])
    for zl in range(4):
        low = jnp.where(row == 5, sums[zl ^ 1], sums[zl ^ 2] + sums[zl ^ 3])
        for x in range(4):
            high = jnp.where(row == 7, got(zl, x ^ 1), got(zl, x ^ 2) + got(zl, x ^ 3))
            fine_ref[zl * 4 + x] = jnp.where(row >= 6, high, low)
    for p in range(16):
        out_ref[p] = tot_ref[pl.ds(level_row(place, p), 1), :]


def far_kernel(place, got_ref, fine_ref, out_ref, acc):
    acc[...] = jnp.zeros_like(acc)
    me = place[0] * 4 + place[1]
    for p in range(16):
        at = pl.ds(level_row(place, p), 1)
        acc[at, :] = acc[at, :] + jnp.where(me == p, 0.0, got_ref[p])
    row = lax.broadcasted_iota(jnp.int32, acc.shape, 0)
    far = acc[...]
    for p in range(16):
        out_ref[p] = jnp.where(row < 4, far, fine_ref[p])


def last_kernel(far_ref, ut_ref, base_ref, out_ref, far16):
    @pl.when(pl.program_id(0) == 0)
    def _():
        far16[...] = far_ref[...].astype(BF16)

    out_ref[...] = (base_ref[...] + dot(ut_ref[...], far16[...])).astype(BF16)


SMEM = pl.BlockSpec(memory_space=pltpu.SMEM)
VMEM = pl.BlockSpec(memory_space=pltpu.VMEM)


def shape(dims, dtype=F32):
    return jax.ShapeDtypeStruct(dims, dtype)


def per_device(sources, tree_perm, leaf_blocks, u_factors, v_factors, level_ranks):
    n, rhs = sources.shape
    rank = u_factors.shape[1]
    half = 4 * rank
    core = lax.axis_index("c")
    place = jnp.stack([lax.axis_index("y"), lax.axis_index("zh")])
    perm = tree_perm.reshape(1, n)
    mine, send = pl.pallas_call(
        coef_kernel,
        name="coef",
        in_specs=[SMEM, VMEM, VMEM, VMEM],
        out_specs=[VMEM, VMEM],
        out_shape=[shape((half, rhs)), shape((half + rank, rhs))],
        scratch_shapes=[pltpu.VMEM((rhs // 128, 2 * half, 128), F32)],
    )(core.reshape(1), perm, v_factors, sources)
    pair = lax.all_gather(send, "c")
    other = lax.dynamic_index_in_dim(pair, 1 - core, 0, keepdims=False)
    near = other[half:]
    partial = (mine + other[:half]).reshape(16, 8, rhs)
    base, ut = pl.pallas_call(
        local_kernel,
        name="local",
        in_specs=[SMEM] + [VMEM] * 6,
        out_specs=[VMEM, VMEM],
        out_shape=[shape((n, rhs)), shape((n, 2 * half), BF16)],
        scratch_shapes=[
            pltpu.VMEM((n, n), BF16),
            pltpu.VMEM((n, n), BF16),
            pltpu.VMEM((n, rhs), BF16),
            pltpu.VMEM((n, n), BF16),
            pltpu.VMEM((n // 128, 2 * half, 128), F32),
            pltpu.VMEM((2 * half, n), BF16),
            pltpu.VMEM((3 * rank, n), BF16),
            pltpu.VMEM((3 * rank, rhs), BF16),
        ],
        cost_estimate=pl.CostEstimate(flops=4_600_000_000, bytes_accessed=8_000_000, transcendentals=0),
    )(level_ranks, perm, sources, leaf_blocks, u_factors, v_factors, near)
    got = lax.all_to_all(partial, ("zl", "x"), 0, 0, tiled=True)
    rows, fine = pl.pallas_call(
        middle_kernel,
        name="middle",
        in_specs=[SMEM, VMEM],
        out_specs=[VMEM, VMEM],
        out_shape=[shape((16, 1, rhs)), shape((16, 8, rhs))],
        scratch_shapes=[pltpu.VMEM((8, rhs), F32)],
    )(place, got)
    rows = lax.all_to_all(rows, ("y", "zh"), 0, 0, tiled=True)
    far = pl.pallas_call(
        far_kernel,
        name="far",
        in_specs=[SMEM, VMEM, VMEM],
        out_specs=VMEM,
        out_shape=shape((16, 8, rhs)),
        scratch_shapes=[pltpu.VMEM((8, rhs), F32)],
    )(place, rows, fine)
    far = lax.all_to_all(far, ("zl", "x"), 0, 0, tiled=True)
    far = lax.all_gather(far.reshape(half, rhs), "c", axis=0, tiled=True)
    step = 256
    return pl.pallas_call(
        last_kernel,
        name="last",
        grid=(n // step,),
        in_specs=[
            pl.BlockSpec((2 * half, rhs), lambda i: (0, 0)),
            pl.BlockSpec((step, 2 * half), lambda i: (i, 0)),
            pl.BlockSpec((step, rhs), lambda i: (i, 0)),
        ],
        out_specs=pl.BlockSpec((step, rhs), lambda i: (i, 0)),
        out_shape=shape((n, rhs), BF16),
        scratch_shapes=[pltpu.VMEM((2 * half, rhs), BF16)],
    )(far, ut, base)


def solution(mesh):
    torus = Mesh(mesh.devices.reshape(4, 4, 4, 4, 2), AXES)
    placed = (P(AXES, None), P(AXES), P(AXES, None), P(None, None, AXES), P(None, None, AXES), P())
    return jax.shard_map(
        per_device, mesh=torus, in_specs=placed, out_specs=P(AXES, None), check_vma=False
    )
```

time: 156 us -> 90.1 us (0.58)
  waiting for transfers between devices: 49.3 us -> 10.5 us
  starting transfers between devices: 37 us -> 8.18 us
  Pallas kernels: 0 us -> 26.5 us
  local copies, waits for them, and re-layouts: 23.2 us -> 1.37 us
  matrix products: 9.2 us -> 0 us
  blocking collectives: 33.9 us -> 41.6 us
    ppermute x9 -> x0, waiting for transfers between devices: 49.3 us -> none  [partner(): lax.ppermute(x, axis, [(i, i ^ 1 << distance) for i in range(lax.axis_siz...]
    ppermute x9 -> x0, starting transfers between devices: 37 us -> none  [partner(): lax.ppermute(x, axis, [(i, i ^ 1 << distance) for i in range(lax.axis_siz...]
    all_to_all x0 -> x1, blocking collectives: none -> 27.8 us  [per_device(): rows = lax.all_to_all(rows, ('y', 'zh'), 0, 0, tiled=True)]
    pallas_call x0 -> x5, Pallas kernels: none -> 26.5 us  [the longest x1 13.9 us: per_device(): pl.pallas_call(local_kernel, name='local', in_specs=[SMEM] + [VMEM] * 6,...]
    all_gather x4 -> x2, blocking collectives: 33.9 us -> 13.8 us  [the longest x1 9.18 us: per_device(): pair = lax.all_gather(send, 'c')]
    all_to_all x0 -> x2, waiting for transfers between devices: none -> 10.5 us  [the longest x1 10.5 us: per_device(): got = lax.all_to_all(partial, ('zl', 'x'), 0, 0, tiled=True)]
    dot_general x5 -> x0, matrix products: 9.2 us -> none  [the longest x1 3.67 us: per_device(): jnp.einsum('lkn,lkr->nr', u_factors[:dev_bits], far_coef, preferred_eleme...]
    all_to_all x0 -> x2, starting transfers between devices: none -> 8.18 us  [the longest x1 4.64 us: per_device(): far = lax.all_to_all(far, ('zl', 'x'), 0, 0, tiled=True)]
  transfers between devices with their start and end apart: 9 -> 2, of which waited for: 8 -> 1; matrix products, arithmetic and copies ran while one was open for 8% -> 1% of each run, Pallas kernels for 0% -> 15%
where the time goes in v1:
time: 90.1 us; the launch traced here: 89.6 us
  blocking collectives  41.6 us (46%)
  Pallas kernels  26.5 us (29%)
  waiting for transfers between devices  10.5 us (12%)
  starting transfers between devices  8.18 us (9%)
  other arithmetic  1.38 us (2%)
  local copies, waits for them, and re-layouts  1.37 us (2%)
    all_to_all x1, blocking collectives, per_device(): rows = lax.all_to_all(rows, ('y', 'zh'), 0, 0, tiled=True)  27.8 us
    pallas_call x1, Pallas kernels, per_device(): pl.pallas_call(local_kernel, name='local', in_specs=[SMEM] + [VMEM] * 6,...  13.9 us
    all_to_all x1, waiting for transfers between devices, per_device(): got = lax.all_to_all(partial, ('zl', 'x'), 0, 0, tiled=True)  10.5 us
    all_gather x1, blocking collectives, per_device(): pair = lax.all_gather(send, 'c')  9.18 us
    all_to_all x1, starting transfers between devices, per_device(): far = lax.all_to_all(far, ('zl', 'x'), 0, 0, tiled=True)  4.64 us
    pallas_call x1, Pallas kernels, per_device(): pl.pallas_call(last_kernel, name='last', grid=(n // step,), in_specs=[pl....  4.58 us
    all_gather x1, blocking collectives, per_device(): far = lax.all_gather(far.reshape(half, rhs), 'c', axis=0, tiled=True)  4.58 us
    pallas_call x1, Pallas kernels, per_device(): pl.pallas_call(coef_kernel, name='coef', in_specs=[SMEM, VMEM, VMEM, VMEM...  4.41 us
  transfers between devices with their start and end apart: 2, of which 1 were waited for; matrix products, arithmetic and copies ran while one was open for 1% of the time, Pallas kernels for 15%

profile of v1, /device:TPU:1, one launch (start us, length us, event | category | flops | bytes accessed | tf_op | source)
XLA Modules:
  0.0 89.6 jit_solution(3209659102066773916)
XLA Ops:
  0.0 4.4 %coef.1 = (f32[128,640]{1,0:T(8,128)}, f32[160,640]{1,0:T(8,128)}) custom-call(s32[1]{0:T(128)} %bitcast.2.core, s32[1,1024]{1,0:T(1,128)} %bitcast.19, bf16[10,32,1024]{2,1,0:T(8,128)(2,1)} %v_ref.3, bf16[1024,640]{1,0:T(8,128)(2,1)} %s_ref.3), custom_call_target="tpu_custom_call" | custom-call | tf_op jit(solution)/shard_map/coef/pallas_call | solution.py:155
  4.4 0.0 copy-start.1
  4.4 9.2 %all-gather = f32[320,640]{1,0:T(8,128)S(1)} all-gather(f32[160,640]{1,0:T(8,128)} %get-tuple-element.12), channel_id=2, replica_groups=mesh['y'=4,'zh'=4,'zl'=4,'x'=4,'c'=2] {'c'}, dimensions={0}, use_global_device_ids=true | all-gather | bytes 1228800 | tf_op jit(solution)/shard_map/all_gather | solution.py:163
  13.6 0.0 copy-done.1
  13.6 0.8 fusion.1
  14.4 3.5 %all-to-all-start = ((f32[16,8,640]{2,1,0:T(8,128)}), f32[16,8,640]{2,1,0:T(8,128)S(1)}, u32[]{:S(2)}, u32[]{:S(2)}) async-start(f32[16,8,640]{2,1,0:T(8,128)} %fusion.1), calls=%async_computation | async-start | bytes 655360 | tf_op jit(solution)/shard_map/all_to_all | solution.py:185
  17.9 0.6 pad_add_fusion.place
  18.5 10.5 %all-to-all-done.got_ref = f32[16,8,640]{2,1,0:T(8,128)S(1)} async-done(((f32[16,8,640]{2,1,0:T(8,128)}), f32[16,8,640]{2,1,0:T(8,128)S(1)}, u32[]{:S(2)}, u32[]{:S(2)}) %all-to-all-start) | async-done | bytes 327712 | tf_op jit(solution)/shard_map/all_to_all | solution.py:185
  29.0 0.0 copy-start
  29.0 0.7 copy-done
  29.8 1.8 %middle.1 = (f32[16,1,640]{2,1,0:T(1,128)}, f32[16,8,640]{2,1,0:T(8,128)}) custom-call(s32[2]{0:T(128)} %pad_add_fusion.place, f32[16,8,640]{2,1,0:T(8,128)} %copy-done), custom_call_target="tpu_custom_call" | custom-call | tf_op jit(solution)/shard_map/middle/pallas_call | solution.py:186
  31.5 27.8 %all_to_all.15.got_ref = f32[16,1,640]{2,1,0:T(1,128)} all-to-all(f32[16,1,640]{2,1,0:T(1,128)} %get-tuple-element.13), channel_id=1, replica_groups=mesh['y'=4,'zh'=4,'zl'=4,'x'=4,'c'=2] {'y','zh'}, dimensions={0} | all-to-all | bytes 81920 | tf_op jit(solution)/shard_map/all_to_all | solution.py:194
  59.3 1.9 %far.1 = f32[16,8,640]{2,1,0:T(8,128)} custom-call(s32[2]{0:T(128)} %pad_add_fusion.place, f32[16,1,640]{2,1,0:T(1,128)} %all_to_all.15.got_ref, f32[16,8,640]{2,1,0:T(8,128)} %get-tuple-element.14.fine_ref), custom_call_target="tpu_custom_call" | custom-call | tf_op jit(solution)/shard_map/far/pallas_call | solution.py:195
  61.2 4.6 %all-to-all-start.2 = ((f32[16,8,640]{2,1,0:T(8,128)}), f32[16,8,640]{2,1,0:T(8,128)S(1)}, u32[]{:S(2)}, u32[]{:S(2)}) async-start(f32[16,8,640]{2,1,0:T(8,128)} %far.1), calls=%async_computation.2 | async-start | bytes 655360 | tf_op jit(solution)/shard_map/all_to_all | solution.py:203
  65.9 0.6 dynamic-slice_bitcast_fusion.1.near_ref
  66.5 13.9 %local.1 = (f32[1024,640]{1,0:T(8,128)}, bf16[1024,256]{1,0:T(8,128)(2,1)}) custom-call(s32[10]{0:T(128)} %ranks.1, s32[1,1024]{1,0:T(1,128)} %bitcast.20, bf16[1024,640]{1,0:T(8,128)(2,1)} %s_ref.3, bf16[1024,512]{1,0:T(8,128)(2,1)} %leaf_ref.1, bf16[10,32,1024]{2,1,0:T(8,128)(2,1)} %u_ref.1, bf16[10,32,1024]{2,1,0:T(8,128)(2,1)} %v_ref.3, ...), custom_call_target="tpu_custom_call" | custom-call | flops 4600000000 | bytes 8000000 | tf_op jit(solution)/shard_map/local/pallas_call | solution.py:167
  80.4 0.0 all-to-all-done.2
  80.4 4.6 %all_gather.11.far_ref = f32[256,640]{1,0:T(8,128)} all-gather(f32[128,640]{1,0:T(8,128)S(1)} %bitcast.18), channel_id=1, replica_groups=mesh['y'=4,'zh'=4,'zl'=4,'x'=4,'c'=2] {'c'}, dimensions={0}, use_global_device_ids=true | all-gather | bytes 983040 | tf_op jit(solution)/shard_map/all_gather | solution.py:204
  85.0 4.6 %last.1 = bf16[1024,640]{1,0:T(8,128)(2,1)} custom-call(f32[256,640]{1,0:T(8,128)} %all_gather.11.far_ref, bf16[1024,256]{1,0:T(8,128)(2,1)} %get-tuple-element.15.ut_ref, f32[1024,640]{1,0:T(8,128)} %get-tuple-element.16.base_ref), custom_call_target="tpu_custom_call" | custom-call | tf_op jit(solution)/shard_map/last/pallas_call | solution.py:206
Async XLA Ops:
  4.4 9.2 %copy-start.1 = (f32[128,640]{1,0:T(8,128)S(1)}, f32[128,640]{1,0:T(8,128)}, u32[]{:S(2)}) copy-start(f32[128,640]{1,0:T(8,128)} %get-tuple-element.11) | copy-start | bytes 983044
  14.4 14.7 %all-to-all-start = ((f32[16,8,640]{2,1,0:T(8,128)}), f32[16,8,640]{2,1,0:T(8,128)S(1)}, u32[]{:S(2)}, u32[]{:S(2)}) async-start(f32[16,8,640]{2,1,0:T(8,128)} %fusion.1), calls=%async_computation | async-start | bytes 655360 | tf_op jit(solution)/shard_map/all_to_all | solution.py:185
  29.0 0.7 copy-start
  61.2 19.2 %all-to-all-start.2 = ((f32[16,8,640]{2,1,0:T(8,128)}), f32[16,8,640]{2,1,0:T(8,128)S(1)}, u32[]{:S(2)}, u32[]{:S(2)}) async-start(f32[16,8,640]{2,1,0:T(8,128)} %far.1), calls=%async_computation.2 | async-start | bytes 655360 | tf_op jit(solution)/shard_map/all_to_all | solution.py:203

commit v2 on v1

--- a/solution.py
+++ b/solution.py
@@ -23,15 +23,28 @@
     return jnp.where(j == perm, 1.0, 0.0).astype(BF16)
 
 
-def coef_kernel(core, perm_ref, v_ref, s_ref, mine_ref, send_ref, acc):
+def coef_kernel(core, perm_ref, v_hbm, s_hbm, mine_ref, send_ref, acc, v_ref, s_ref, v_sem, s_sem):
     n = s_ref.shape[0]
-    rank = v_ref.shape[1]
+    levels, rank, _ = v_ref.shape
+    step = 256
+    v_copy = pltpu.make_async_copy(v_hbm.at[0:levels], v_ref, v_sem)
+    v_copy.start()
+    s_copy = [
+        pltpu.make_async_copy(s_hbm.at[j : j + step], s_ref.at[j : j + step], s_sem.at[j // step])
+        for j in range(0, n, step)
+    ]
+    for copy in s_copy:
+        copy.start()
     perm = perm_ref[...] & (n - 1)
-    v = v_ref[0:9].reshape(9 * rank, n)
-    step = 256
+    hot = one_hot_t(perm, 0, step)
+    v_copy.wait()
+    v = v_ref[...].reshape(levels * rank, n)
     total = None
     for j in range(0, n, step):
-        vp = dot(v, one_hot_t(perm, j, step), NT).astype(BF16)
+        vp = dot(v, hot, NT).astype(BF16)
+        if j + step < n:
+            hot = one_hot_t(perm, j + step, step)
+        s_copy[j // step].wait()
         part = dot(vp, s_ref[j : j + step, :])
         total = part if total is None else total + part
     half = 4 * rank
@@ -47,7 +60,7 @@
     send_ref[half : half + rank, :] = total[8 * rank : 9 * rank]
 
 
-def local_kernel(ranks, perm_ref, s_ref, leaf_ref, u_ref, v_ref, near_ref, base_ref, ut_ref, p_ref, pt_ref, ord_ref, lp_ref, uf_ref, us_ref, ue_ref, fe_ref):
+def local_kernel(ranks, core, perm_ref, s_ref, leaf_ref, u_ref, v_ref, pair_ref, _, base_ref, ut_ref, p_ref, pt_ref, ord_ref, lp_ref, uf_ref, us_ref, ue_ref, fe_ref):
     n, _ = s_ref.shape
     leaf = leaf_ref.shape[1]
     rank = u_ref.shape[1]
@@ -83,7 +96,7 @@
         return 0
 
     lax.fori_loop(0, n // step, order, 0)
-    fe_ref[0:rank, :] = near_ref[...].astype(BF16)
+    fe_ref[0:rank, :] = pair_ref[1 - core[0], 4 * rank :, :].astype(BF16)
     fe_ref[rank : 2 * rank, :] = dot(v_ref[9][:, leaf:], ord_ref[leaf:, :]).astype(BF16)
     fe_ref[2 * rank : 3 * rank, :] = dot(v_ref[9][:, :leaf], ord_ref[:leaf, :]).astype(BF16)
 
@@ -117,7 +130,7 @@
         out_ref[p] = tot_ref[pl.ds(level_row(place, p), 1), :]
 
 
-def far_kernel(place, got_ref, fine_ref, out_ref, acc):
+def far_kernel(place, got_ref, fine_ref, _, out_ref, acc):
     acc[...] = jnp.zeros_like(acc)
     me = place[0] * 4 + place[1]
     for p in range(16):
@@ -139,6 +152,11 @@
 
 SMEM = pl.BlockSpec(memory_space=pltpu.SMEM)
 VMEM = pl.BlockSpec(memory_space=pltpu.VMEM)
+ANY = pl.BlockSpec(memory_space=pl.ANY)
+
+
+def grant(mib):
+    return pltpu.CompilerParams(vmem_limit_bytes=mib << 20)
 
 
 def shape(dims, dtype=F32):
@@ -149,25 +167,41 @@
     n, rhs = sources.shape
     rank = u_factors.shape[1]
     half = 4 * rank
-    core = lax.axis_index("c")
+    core = lax.axis_index("c").reshape(1)
     place = jnp.stack([lax.axis_index("y"), lax.axis_index("zh")])
     perm = tree_perm.reshape(1, n)
     mine, send = pl.pallas_call(
         coef_kernel,
         name="coef",
-        in_specs=[SMEM, VMEM, VMEM, VMEM],
+        in_specs=[SMEM, VMEM, ANY, ANY],
         out_specs=[VMEM, VMEM],
         out_shape=[shape((half, rhs)), shape((half + rank, rhs))],
-        scratch_shapes=[pltpu.VMEM((rhs // 128, 2 * half, 128), F32)],
-    )(core.reshape(1), perm, v_factors, sources)
+        scratch_shapes=[
+            pltpu.VMEM((rhs // 128, 2 * half, 128), F32),
+            pltpu.VMEM((9, rank, n), BF16),
+            pltpu.VMEM((n, rhs), BF16),
+            pltpu.SemaphoreType.DMA,
+            pltpu.SemaphoreType.DMA((n // 256,)),
+        ],
+        compiler_params=grant(14),
+    )(core, perm, v_factors, sources)
     pair = lax.all_gather(send, "c")
-    other = lax.dynamic_index_in_dim(pair, 1 - core, 0, keepdims=False)
-    near = other[half:]
+    other = lax.dynamic_index_in_dim(pair, 1 - core[0], 0, keepdims=False)
     partial = (mine + other[:half]).reshape(16, 8, rhs)
+    got = lax.all_to_all(partial, ("zl", "x"), 0, 0, tiled=True)
+    rows, fine = pl.pallas_call(
+        middle_kernel,
+        name="middle",
+        in_specs=[SMEM, VMEM],
+        out_specs=[VMEM, VMEM],
+        out_shape=[shape((16, 1, rhs)), shape((16, 8, rhs))],
+        scratch_shapes=[pltpu.VMEM((8, rhs), F32)],
+        compiler_params=grant(4),
+    )(place, got)
     base, ut = pl.pallas_call(
         local_kernel,
         name="local",
-        in_specs=[SMEM] + [VMEM] * 6,
+        in_specs=[SMEM, SMEM] + [VMEM] * 6 + [ANY],
         out_specs=[VMEM, VMEM],
         out_shape=[shape((n, rhs)), shape((n, 2 * half), BF16)],
         scratch_shapes=[
@@ -180,26 +214,19 @@
             pltpu.VMEM((3 * rank, n), BF16),
             pltpu.VMEM((3 * rank, rhs), BF16),
         ],
+        compiler_params=grant(32),
         cost_estimate=pl.CostEstimate(flops=4_600_000_000, bytes_accessed=8_000_000, transcendentals=0),
-    )(level_ranks, perm, sources, leaf_blocks, u_factors, v_factors, near)
-    got = lax.all_to_all(partial, ("zl", "x"), 0, 0, tiled=True)
-    rows, fine = pl.pallas_call(
-        middle_kernel,
-        name="middle",
-        in_specs=[SMEM, VMEM],
-        out_specs=[VMEM, VMEM],
-        out_shape=[shape((16, 1, rhs)), shape((16, 8, rhs))],
-        scratch_shapes=[pltpu.VMEM((8, rhs), F32)],
-    )(place, got)
+    )(level_ranks, core, perm, sources, leaf_blocks, u_factors, v_factors, pair, fine)
     rows = lax.all_to_all(rows, ("y", "zh"), 0, 0, tiled=True)
     far = pl.pallas_call(
         far_kernel,
         name="far",
-        in_specs=[SMEM, VMEM, VMEM],
+        in_specs=[SMEM, VMEM, VMEM, ANY],
         out_specs=VMEM,
         out_shape=shape((16, 8, rhs)),
         scratch_shapes=[pltpu.VMEM((8, rhs), F32)],
-    )(place, rows, fine)
+        compiler_params=grant(4),
+    )(place, rows, fine, ut)
     far = lax.all_to_all(far, ("zl", "x"), 0, 0, tiled=True)
     far = lax.all_gather(far.reshape(half, rhs), "c", axis=0, tiled=True)
     step = 256
@@ -215,6 +242,7 @@
         out_specs=pl.BlockSpec((step, rhs), lambda i: (i, 0)),
         out_shape=shape((n, rhs), BF16),
         scratch_shapes=[pltpu.VMEM((2 * half, rhs), BF16)],
+        compiler_params=grant(8),
     )(far, ut, base)
 
 

time: 90.1 us -> 85.4 us (0.948)
  blocking collectives: 41.6 us -> 27.9 us
  starting transfers between devices: 8.18 us -> 17.5 us
  Pallas kernels: 26.5 us -> 18.4 us
  local copies, waits for them, and re-layouts: 1.37 us -> 8.95 us
    all_to_all x1, blocking collectives: 27.8 us -> 14.4 us  [per_device(): far = lax.all_to_all(far, ('zl', 'x'), 0, 0, tiled=True)]
    all_to_all x1, starting transfers between devices: 4.64 us -> 14 us  [per_device(): rows = lax.all_to_all(rows, ('y', 'zh'), 0, 0, tiled=True)]
    unnamed x4 -> x22, local copies, waits for them, and re-layouts: 0.73 us -> 8.95 us
    pallas_call x3, Pallas kernels: 20.2 us -> 14.9 us  [the longest x1 11 us: per_device(): pl.pallas_call(local_kernel, name='local', in_specs=[SMEM, SMEM] + [VMEM]...]
    pallas_call x1, Pallas kernels: 4.58 us -> 2.31 us  [per_device(): pl.pallas_call(last_kernel, name='last', grid=(n // step,), in_specs=[pl....]
  transfers between devices with their start and end apart: 2 -> 2, of which waited for: 1 -> 1; matrix products, arithmetic and copies ran while one was open for 1% -> 0% of each run, Pallas kernels for 15% -> 13%
where the time goes in v2:
time: 85.4 us; the launch traced here: 84.8 us
  blocking collectives  27.9 us (33%)
  Pallas kernels  18.4 us (22%)
  starting transfers between devices  17.5 us (20%)
  waiting for transfers between devices  11 us (13%)
  local copies, waits for them, and re-layouts  8.95 us (10%)
    all_to_all x1, blocking collectives, per_device(): far = lax.all_to_all(far, ('zl', 'x'), 0, 0, tiled=True)  14.4 us
    all_to_all x1, starting transfers between devices, per_device(): rows = lax.all_to_all(rows, ('y', 'zh'), 0, 0, tiled=True)  14 us
    all_to_all x1, waiting for transfers between devices, per_device(): got = lax.all_to_all(partial, ('zl', 'x'), 0, 0, tiled=True)  11 us
    pallas_call x1, Pallas kernels, per_device(): pl.pallas_call(local_kernel, name='local', in_specs=[SMEM, SMEM] + [VMEM]...  11 us
    unnamed x22, local copies, waits for them, and re-layouts  8.95 us
    all_gather x1, blocking collectives, per_device(): pair = lax.all_gather(send, 'c')  8.85 us
    all_gather x1, blocking collectives, per_device(): far = lax.all_gather(far.reshape(half, rhs), 'c', axis=0, tiled=True)  4.65 us
    all_to_all x1, starting transfers between devices, per_device(): got = lax.all_to_all(partial, ('zl', 'x'), 0, 0, tiled=True)  3.54 us
  transfers between devices with their start and end apart: 2, of which 1 were waited for; matrix products, arithmetic and copies ran while one was open for 0% of the time, Pallas kernels for 13%

profile of v2, /device:TPU:1, one launch (start us, length us, event | category | flops | bytes accessed | tf_op | source)
XLA Modules:
  0.0 84.8 jit_solution(14275737988105083082)
XLA Ops:
  0.0 1.3 %copy-done.2 = bf16[1024,640]{1,0:T(8,128)(2,1)S(1)} copy-done((bf16[1024,640]{1,0:T(8,128)(2,1)S(1)}, bf16[1024,640]{1,0:T(8,128)(2,1)}, u32[]{:S(2)}) %copy-start.2) | copy-done | bytes 1310744
  1.3 1.1 %copy-done.4 = bf16[10,32,1024]{2,1,0:T(8,128)(2,1)S(1)} copy-done((bf16[10,32,1024]{2,1,0:T(8,128)(2,1)S(1)}, bf16[10,32,1024]{2,1,0:T(8,128)(2,1)}, u32[]{:S(2)}) %copy-start.4) | copy-done | bytes 655384
  2.4 0.7 copy-done.6
  3.1 3.1 %coef.1 = (f32[128,640]{1,0:T(8,128)S(1)}, f32[160,640]{1,0:T(8,128)S(1)}) custom-call(s32[1]{0:T(128)} %bitcast.2.core, s32[1,1024]{1,0:T(1,128)S(1)} %bitcast.16, bf16[10,32,1024]{2,1,0:T(8,128)(2,1)S(1)} %copy-done.4, bf16[1024,640]{1,0:T(8,128)(2,1)S(1)} %copy-done.2), custom_call_target="tpu_custom_call" | custom-call | tf_op jit(solution)/shard_map/coef/pallas_call | solution.py:173
  6.2 8.9 %all-gather = f32[320,640]{1,0:T(8,128)S(1)} all-gather(f32[160,640]{1,0:T(8,128)S(1)} %get-tuple-element.12), channel_id=2, replica_groups=mesh['y'=4,'zh'=4,'zl'=4,'x'=4,'c'=2] {'c'}, dimensions={0}, use_global_device_ids=true | all-gather | bytes 1228800 | tf_op jit(solution)/shard_map/all_gather | solution.py:188
  15.1 0.8 fusion.1
  15.9 3.5 %all-to-all-start = ((f32[16,8,640]{2,1,0:T(8,128)}), f32[16,8,640]{2,1,0:T(8,128)S(1)}, u32[]{:S(2)}, u32[]{:S(2)}) async-start(f32[16,8,640]{2,1,0:T(8,128)} %fusion.1), calls=%async_computation | async-start | bytes 655360 | tf_op jit(solution)/shard_map/all_to_all | solution.py:191
  19.4 0.1 pad_add_fusion.place
  19.5 11.0 %all-to-all-done.got_ref = f32[16,8,640]{2,1,0:T(8,128)S(1)} async-done(((f32[16,8,640]{2,1,0:T(8,128)}), f32[16,8,640]{2,1,0:T(8,128)S(1)}, u32[]{:S(2)}, u32[]{:S(2)}) %all-to-all-start) | async-done | bytes 327712 | tf_op jit(solution)/shard_map/all_to_all | solution.py:191
  30.5 1.2 %middle.1 = (f32[16,1,640]{2,1,0:T(1,128)}, f32[16,8,640]{2,1,0:T(8,128)S(1)}) custom-call(s32[2]{0:T(128)S(1)} %pad_add_fusion.place, f32[16,8,640]{2,1,0:T(8,128)S(1)} %all-to-all-done.got_ref), custom_call_target="tpu_custom_call" | custom-call | tf_op jit(solution)/shard_map/middle/pallas_call | solution.py:192
  31.7 14.0 %all-to-all-start.1 = ((f32[16,1,640]{2,1,0:T(1,128)}), f32[16,1,640]{2,1,0:T(1,128)S(1)}, u32[]{:S(2)}, u32[]{:S(2)}) async-start(f32[16,1,640]{2,1,0:T(1,128)} %get-tuple-element.13), calls=%async_computation.1 | async-start | bytes 81920 | tf_op jit(solution)/shard_map/all_to_all | solution.py:220
  45.8 0.0 copy-done
  45.8 0.0 copy-start.1
  45.8 1.1 %copy-done.1 = f32[320,640]{1,0:T(8,128)S(1)} copy-done((f32[320,640]{1,0:T(8,128)S(1)}, f32[320,640]{1,0:T(8,128)}, u32[]{:S(2)}) %copy-start.1) | copy-done | bytes 819224
  46.9 1.3 %copy-done.3 = bf16[1024,640]{1,0:T(8,128)(2,1)S(1)} copy-done((bf16[1024,640]{1,0:T(8,128)(2,1)S(1)}, bf16[1024,640]{1,0:T(8,128)(2,1)}, u32[]{:S(2)}) %copy-start.3) | copy-done | bytes 1310744
  48.2 1.1 %copy-done.5 = bf16[10,32,1024]{2,1,0:T(8,128)(2,1)S(1)} copy-done((bf16[10,32,1024]{2,1,0:T(8,128)(2,1)S(1)}, bf16[10,32,1024]{2,1,0:T(8,128)(2,1)}, u32[]{:S(2)}) %copy-start.5) | copy-done | bytes 655384
  49.3 1.2 %copy-done.8 = bf16[1024,512]{1,0:T(8,128)(2,1)S(1)} copy-done((bf16[1024,512]{1,0:T(8,128)(2,1)S(1)}, bf16[1024,512]{1,0:T(8,128)(2,1)}, u32[]{:S(2)}) %copy-start.8) | copy-done | bytes 1048600
  50.6 1.1 %copy-done.9 = bf16[10,32,1024]{2,1,0:T(8,128)(2,1)S(1)} copy-done((bf16[10,32,1024]{2,1,0:T(8,128)(2,1)S(1)}, bf16[10,32,1024]{2,1,0:T(8,128)(2,1)}, u32[]{:S(2)}) %copy-start.9) | copy-done | bytes 655384
  51.6 11.0 %local.1 = (f32[1024,640]{1,0:T(8,128)S(1)}, bf16[1024,256]{1,0:T(8,128)(2,1)S(1)}) custom-call(s32[10]{0:T(128)S(1)} %copy-done.10, s32[1]{0:T(128)} %bitcast.2.core, s32[1,1024]{1,0:T(1,128)S(1)} %bitcast.17, bf16[1024,640]{1,0:T(8,128)(2,1)S(1)} %copy-done.3, bf16[1024,512]{1,0:T(8,128)(2,1)S(1)} %copy-done.8, bf16[10,32,1024]{2,1,0:T(8,128)(2,1)S(1)} %copy-done.9, ...), custom_call_target="tpu_custom_call" | custom-call | flops 4600000000 | bytes 8000000 | tf_op jit(solution)/shard_map/local/pallas_call | solution.py:201
  62.7 0.0 all-to-all-done.1.got_ref
  62.7 0.7 far.1
  63.4 14.4 %all_to_all.15 = f32[16,8,640]{2,1,0:T(8,128)S(1)} all-to-all(f32[16,8,640]{2,1,0:T(8,128)S(1)} %far.1), channel_id=1, replica_groups=mesh['y'=4,'zh'=4,'zl'=4,'x'=4,'c'=2] {'zl','x'}, dimensions={0} | all-to-all | bytes 655360 | tf_op jit(solution)/shard_map/all_to_all | solution.py:230
  77.8 4.7 %all_gather.11.far_ref = f32[256,640]{1,0:T(8,128)S(1)} all-gather(f32[128,640]{1,0:T(8,128)S(1)} %bitcast.18), channel_id=1, replica_groups=mesh['y'=4,'zh'=4,'zl'=4,'x'=4,'c'=2] {'c'}, dimensions={0}, use_global_device_ids=true | all-gather | bytes 983040 | tf_op jit(solution)/shard_map/all_gather | solution.py:231
  82.4 2.3 %last.1 = bf16[1024,640]{1,0:T(8,128)(2,1)} custom-call(f32[256,640]{1,0:T(8,128)S(1)} %all_gather.11.far_ref, bf16[1024,256]{1,0:T(8,128)(2,1)S(1)} %get-tuple-element.15._.ut_ref, f32[1024,640]{1,0:T(8,128)S(1)} %get-tuple-element.16.base_ref), custom_call_target="tpu_custom_call" | custom-call | tf_op jit(solution)/shard_map/last/pallas_call | solution.py:233
  (12 shorter events, 0.0 us)
Async XLA Ops:
  0.0 1.3 %copy-start.2 = (bf16[1024,640]{1,0:T(8,128)(2,1)S(1)}, bf16[1024,640]{1,0:T(8,128)(2,1)}, u32[]{:S(2)}) copy-start(bf16[1024,640]{1,0:T(8,128)(2,1)} %s_ref.1) | copy-start | bytes 3932164
  1.3 1.1 %copy-start.4 = (bf16[10,32,1024]{2,1,0:T(8,128)(2,1)S(1)}, bf16[10,32,1024]{2,1,0:T(8,128)(2,1)}, u32[]{:S(2)}) copy-start(bf16[10,32,1024]{2,1,0:T(8,128)(2,1)} %v_ref.1) | copy-start | bytes 1966084
  2.4 0.7 copy-start.6
  15.1 30.7 %copy-start = (f32[320,640]{1,0:T(8,128)}, f32[320,640]{1,0:T(8,128)S(1)}, u32[]{:S(2)}) copy-start(f32[320,640]{1,0:T(8,128)S(1)} %all-gather) | copy-start | bytes 2457604
  15.1 30.7 %copy-start.7 = (s32[1024]{0:T(1024)S(1)}, s32[1024]{0:T(1024)}, u32[]{:S(2)}) copy-start(s32[1024]{0:T(1024)} %param.7) | copy-start | bytes 12292
  15.1 30.7 %copy-start.10 = (s32[10]{0:T(128)S(1)}, s32[10]{0:T(128)}, u32[]{:S(2)}) copy-start(s32[10]{0:T(128)} %ranks.1) | copy-start | bytes 124
  15.9 14.7 %all-to-all-start = ((f32[16,8,640]{2,1,0:T(8,128)}), f32[16,8,640]{2,1,0:T(8,128)S(1)}, u32[]{:S(2)}, u32[]{:S(2)}) async-start(f32[16,8,640]{2,1,0:T(8,128)} %fusion.1), calls=%async_computation | async-start | bytes 655360 | tf_op jit(solution)/shard_map/all_to_all | solution.py:191
  31.7 30.9 %all-to-all-start.1 = ((f32[16,1,640]{2,1,0:T(1,128)}), f32[16,1,640]{2,1,0:T(1,128)S(1)}, u32[]{:S(2)}, u32[]{:S(2)}) async-start(f32[16,1,640]{2,1,0:T(1,128)} %get-tuple-element.13), calls=%async_computation.1 | async-start | bytes 81920 | tf_op jit(solution)/shard_map/all_to_all | solution.py:220
  45.8 1.1 %copy-start.1 = (f32[320,640]{1,0:T(8,128)S(1)}, f32[320,640]{1,0:T(8,128)}, u32[]{:S(2)}) copy-start(f32[320,640]{1,0:T(8,128)} %copy-done) | copy-start | bytes 2457604
  46.9 1.3 %copy-start.3 = (bf16[1024,640]{1,0:T(8,128)(2,1)S(1)}, bf16[1024,640]{1,0:T(8,128)(2,1)}, u32[]{:S(2)}) copy-start(bf16[1024,640]{1,0:T(8,128)(2,1)} %s_ref.1) | copy-start | bytes 3932164
  48.2 1.1 %copy-start.5 = (bf16[10,32,1024]{2,1,0:T(8,128)(2,1)S(1)}, bf16[10,32,1024]{2,1,0:T(8,128)(2,1)}, u32[]{:S(2)}) copy-start(bf16[10,32,1024]{2,1,0:T(8,128)(2,1)} %v_ref.1) | copy-start | bytes 1966084
  49.3 1.2 %copy-start.8 = (bf16[1024,512]{1,0:T(8,128)(2,1)S(1)}, bf16[1024,512]{1,0:T(8,128)(2,1)}, u32[]{:S(2)}) copy-start(bf16[1024,512]{1,0:T(8,128)(2,1)} %leaf_ref.1) | copy-start | bytes 3145732
  50.6 1.1 %copy-start.9 = (bf16[10,32,1024]{2,1,0:T(8,128)(2,1)S(1)}, bf16[10,32,1024]{2,1,0:T(8,128)(2,1)}, u32[]{:S(2)}) copy-start(bf16[10,32,1024]{2,1,0:T(8,128)(2,1)} %u_ref.1) | copy-start | bytes 1966084

commit v3 on v2

--- a/solution.py
+++ b/solution.py
@@ -23,10 +23,12 @@
     return jnp.where(j == perm, 1.0, 0.0).astype(BF16)
 
 
-def coef_kernel(core, perm_ref, v_hbm, s_hbm, mine_ref, send_ref, acc, v_ref, s_ref, v_sem, s_sem):
+def coef_kernel(core, perm_hbm, v_hbm, s_hbm, mine_ref, send_ref, acc, perm_ref, v_ref, s_ref, perm_sem, v_sem, s_sem):
     n = s_ref.shape[0]
     levels, rank, _ = v_ref.shape
     step = 256
+    perm_copy = pltpu.make_async_copy(perm_hbm, perm_ref, perm_sem)
+    perm_copy.start()
     v_copy = pltpu.make_async_copy(v_hbm.at[0:levels], v_ref, v_sem)
     v_copy.start()
     s_copy = [
@@ -35,6 +37,7 @@
     ]
     for copy in s_copy:
         copy.start()
+    perm_copy.wait()
     perm = perm_ref[...] & (n - 1)
     hot = one_hot_t(perm, 0, step)
     v_copy.wait()
@@ -60,10 +63,19 @@
     send_ref[half : half + rank, :] = total[8 * rank : 9 * rank]
 
 
-def local_kernel(ranks, core, perm_ref, s_ref, leaf_ref, u_ref, v_ref, pair_ref, _, base_ref, ut_ref, p_ref, pt_ref, ord_ref, lp_ref, uf_ref, us_ref, ue_ref, fe_ref):
+def local_kernel(
+    ranks, core, perm_hbm, s_hbm, leaf_hbm, u_hbm, v_hbm, pair_ref, _,
+    ord_hbm, lp_hbm, ut_ref, et_ref, fe_ref, token_ref,
+    perm_ref, s_ref, leaf_ref, u_ref, v_ref, p_ref, pt_ref, uf_ref, us_ref, ue_ref, ord_ref, lp_ref, sems, ord_sems, lp_sems,
+):
     n, _ = s_ref.shape
     leaf = leaf_ref.shape[1]
     rank = u_ref.shape[1]
+    pairs = ((perm_hbm, perm_ref), (s_hbm, s_ref), (u_hbm, u_ref), (leaf_hbm, leaf_ref), (v_hbm.at[9], v_ref))
+    copies = [pltpu.make_async_copy(a, b, sems.at[k]) for k, (a, b) in enumerate(pairs)]
+    for copy in copies:
+        copy.start()
+    copies[0].wait()
     perm = perm_ref[...] & (n - 1)
     step = 256
     for j in range(0, n, step):
@@ -73,6 +85,8 @@
         lane = lax.broadcasted_iota(jnp.int32, (128, 128), 1)
         for j in range(0, n, 128):
             p_ref[i : i + 128, j : j + 128] = jnp.where(column == lane + j, 1.0, 0.0).astype(BF16)
+    for copy in copies[1:]:
+        copy.wait()
 
     row = lax.broadcasted_iota(jnp.int32, (rank, n), 0)
     lane_n = lax.broadcasted_iota(jnp.int32, (rank, n), 1)
@@ -87,26 +101,36 @@
     ue_ref[rank : 2 * rank, :] = jnp.where(lane_n < leaf, last, 0.0).astype(BF16)
     ue_ref[2 * rank : 3 * rank, :] = jnp.where(lane_n < leaf, 0.0, last).astype(BF16)
 
+    def kept_copies(b):
+        rows = pl.ds(pl.multiple_of(b * step, step), step)
+        return (
+            pltpu.make_async_copy(ord_ref.at[rows], ord_hbm.at[rows], ord_sems.at[b]),
+            pltpu.make_async_copy(lp_ref.at[rows], lp_hbm.at[rows], lp_sems.at[b]),
+        )
+
     def order(b, _):
         rows = pl.ds(pl.multiple_of(b * step, step), step)
         ord_ref[rows, :] = dot(p_ref[rows, :], s_ref[...]).astype(BF16)
         for g in range(0, n, leaf):
             lp_ref[rows, g : g + leaf] = dot(pt_ref[rows, g : g + leaf], leaf_ref[g : g + leaf, :]).astype(BF16)
         ut_ref[rows, :] = dot(pt_ref[rows, :], us_ref[...], NT).astype(BF16)
+        for copy in kept_copies(b):
+            copy.start()
+        et_ref[rows, :] = dot(pt_ref[rows, :], ue_ref[...], NT).astype(BF16)
         return 0
 
     lax.fori_loop(0, n // step, order, 0)
     fe_ref[0:rank, :] = pair_ref[1 - core[0], 4 * rank :, :].astype(BF16)
-    fe_ref[rank : 2 * rank, :] = dot(v_ref[9][:, leaf:], ord_ref[leaf:, :]).astype(BF16)
-    fe_ref[2 * rank : 3 * rank, :] = dot(v_ref[9][:, :leaf], ord_ref[:leaf, :]).astype(BF16)
-
-    def apply(b, _):
-        rows = pl.ds(pl.multiple_of(b * step, step), step)
-        ue = dot(pt_ref[rows, :], ue_ref[...], NT).astype(BF16)
-        base_ref[rows, :] = dot(lp_ref[rows, :], ord_ref[...]) + dot(ue, fe_ref[...])
-        return 0
-
-    lax.fori_loop(0, n // step, apply, 0)
+    fe_ref[rank : 2 * rank, :] = dot(v_ref[:, leaf:], ord_ref[leaf:, :]).astype(BF16)
+    fe_ref[2 * rank : 3 * rank, :] = dot(v_ref[:, :leaf], ord_ref[:leaf, :]).astype(BF16)
+    token_ref[...] = jnp.zeros_like(token_ref)
+    for b in range(n // step):
+        for copy in kept_copies(b):
+            copy.wait()
+
+
+def base_kernel(ord_ref, lp_ref, et_ref, fe_ref, _, base_ref):
+    base_ref[...] = dot(lp_ref[...], ord_ref[...]) + dot(et_ref[...], fe_ref[...])
 
 
 def level_row(place, p):
@@ -116,7 +140,7 @@
     return jnp.where(py == y, same, jnp.where(py == (y ^ 1), 1, 0))
 
 
-def middle_kernel(place, got_ref, out_ref, fine_ref, tot_ref):
+def middle_kernel(place, got_ref, _, out_ref, fine_ref, tot_ref):
     row = lax.broadcasted_iota(jnp.int32, got_ref.shape[1:], 0)
     got = lambda zl, x: got_ref[zl * 4 + x]
     sums = [(got(zl, 0) + got(zl, 1)) + (got(zl, 2) + got(zl, 3)) for zl in range(4)]
@@ -130,7 +154,7 @@
         out_ref[p] = tot_ref[pl.ds(level_row(place, p), 1), :]
 
 
-def far_kernel(place, got_ref, fine_ref, _, out_ref, acc):
+def far_kernel(place, got_ref, fine_ref, out_ref, acc):
     acc[...] = jnp.zeros_like(acc)
     me = place[0] * 4 + place[1]
     for p in range(16):
@@ -153,10 +177,19 @@
 SMEM = pl.BlockSpec(memory_space=pltpu.SMEM)
 VMEM = pl.BlockSpec(memory_space=pltpu.VMEM)
 ANY = pl.BlockSpec(memory_space=pl.ANY)
+HBM = pl.BlockSpec(memory_space=pltpu.HBM)
 
 
 def grant(mib):
     return pltpu.CompilerParams(vmem_limit_bytes=mib << 20)
+
+
+def in_hbm(*arrays):
+    return [pltpu.with_memory_space_constraint(a, pltpu.HBM) for a in arrays]
+
+
+def in_vmem(*arrays):
+    return [pltpu.with_memory_space_constraint(a, pltpu.VMEM) for a in arrays]
 
 
 def shape(dims, dtype=F32):
@@ -173,60 +206,92 @@
     mine, send = pl.pallas_call(
         coef_kernel,
         name="coef",
-        in_specs=[SMEM, VMEM, ANY, ANY],
+        in_specs=[SMEM, HBM, HBM, HBM],
         out_specs=[VMEM, VMEM],
         out_shape=[shape((half, rhs)), shape((half + rank, rhs))],
         scratch_shapes=[
             pltpu.VMEM((rhs // 128, 2 * half, 128), F32),
+            pltpu.VMEM((1, n), jnp.int32),
             pltpu.VMEM((9, rank, n), BF16),
             pltpu.VMEM((n, rhs), BF16),
             pltpu.SemaphoreType.DMA,
+            pltpu.SemaphoreType.DMA,
             pltpu.SemaphoreType.DMA((n // 256,)),
         ],
         compiler_params=grant(14),
-    )(core, perm, v_factors, sources)
+    )(core, *in_hbm(perm, v_factors, sources))
     pair = lax.all_gather(send, "c")
     other = lax.dynamic_index_in_dim(pair, 1 - core[0], 0, keepdims=False)
     partial = (mine + other[:half]).reshape(16, 8, rhs)
+    ordered, leaves, ut, et, fe, token = pl.pallas_call(
+        local_kernel,
+        name="local",
+        in_specs=[SMEM, SMEM] + [HBM] * 5 + [VMEM, ANY],
+        out_specs=[HBM, HBM] + [VMEM] * 4,
+        out_shape=[
+            pltpu.HBM((n, rhs), BF16),
+            pltpu.HBM((n, n), BF16),
+            pltpu.VMEM((n, 2 * half), BF16),
+            pltpu.VMEM((n, 3 * rank), BF16),
+            pltpu.VMEM((3 * rank, rhs), BF16),
+            shape((8, 128)),
+        ],
+        scratch_shapes=[
+            pltpu.VMEM((1, n), jnp.int32),
+            pltpu.VMEM((n, rhs), BF16),
+            pltpu.VMEM(leaf_blocks.shape, BF16),
+            pltpu.VMEM(u_factors.shape, BF16),
+            pltpu.VMEM((rank, n), BF16),
+            pltpu.VMEM((n, n), BF16),
+            pltpu.VMEM((n, n), BF16),
+            pltpu.VMEM((n // 128, 2 * half, 128), F32),
+            pltpu.VMEM((2 * half, n), BF16),
+            pltpu.VMEM((3 * rank, n), BF16),
+            pltpu.VMEM((n, rhs), BF16),
+            pltpu.VMEM((n, n), BF16),
+            pltpu.SemaphoreType.DMA((5,)),
+            pltpu.SemaphoreType.DMA((n // 256,)),
+            pltpu.SemaphoreType.DMA((n // 256,)),
+        ],
+        compiler_params=grant(28),
+        cost_estimate=pl.CostEstimate(flops=3_500_000_000, bytes_accessed=8_000_000, transcendentals=0),
+    )(level_ranks, core, *in_hbm(perm, sources, leaf_blocks, u_factors, v_factors), *in_vmem(pair), partial)
     got = lax.all_to_all(partial, ("zl", "x"), 0, 0, tiled=True)
     rows, fine = pl.pallas_call(
         middle_kernel,
         name="middle",
-        in_specs=[SMEM, VMEM],
+        in_specs=[SMEM, VMEM, ANY],
         out_specs=[VMEM, VMEM],
         out_shape=[shape((16, 1, rhs)), shape((16, 8, rhs))],
         scratch_shapes=[pltpu.VMEM((8, rhs), F32)],
         compiler_params=grant(4),
-    )(place, got)
-    base, ut = pl.pallas_call(
-        local_kernel,
-        name="local",
-        in_specs=[SMEM, SMEM] + [VMEM] * 6 + [ANY],
-        out_specs=[VMEM, VMEM],
-        out_shape=[shape((n, rhs)), shape((n, 2 * half), BF16)],
-        scratch_shapes=[
-            pltpu.VMEM((n, n), BF16),
-            pltpu.VMEM((n, n), BF16),
-            pltpu.VMEM((n, rhs), BF16),
-            pltpu.VMEM((n, n), BF16),
-            pltpu.VMEM((n // 128, 2 * half, 128), F32),
-            pltpu.VMEM((2 * half, n), BF16),
-            pltpu.VMEM((3 * rank, n), BF16),
-            pltpu.VMEM((3 * rank, rhs), BF16),
-        ],
-        compiler_params=grant(32),
-        cost_estimate=pl.CostEstimate(flops=4_600_000_000, bytes_accessed=8_000_000, transcendentals=0),
-    )(level_ranks, core, perm, sources, leaf_blocks, u_factors, v_factors, pair, fine)
+    )(place, got, token)
     rows = lax.all_to_all(rows, ("y", "zh"), 0, 0, tiled=True)
     far = pl.pallas_call(
         far_kernel,
         name="far",
-        in_specs=[SMEM, VMEM, VMEM, ANY],
+        in_specs=[SMEM, VMEM, VMEM],
         out_specs=VMEM,
         out_shape=shape((16, 8, rhs)),
         scratch_shapes=[pltpu.VMEM((8, rhs), F32)],
         compiler_params=grant(4),
-    )(place, rows, fine, ut)
+    )(place, rows, fine)
+    base = pl.pallas_call(
+        base_kernel,
+        name="base",
+        grid=(n // 256,),
+        in_specs=[
+            pl.BlockSpec((n, rhs), lambda i: (0, 0)),
+            pl.BlockSpec((256, n), lambda i: (i, 0)),
+            pl.BlockSpec((256, 3 * rank), lambda i: (i, 0)),
+            pl.BlockSpec((3 * rank, rhs), lambda i: (0, 0)),
+            ANY,
+        ],
+        out_specs=pl.BlockSpec((256, rhs), lambda i: (i, 0)),
+        out_shape=pltpu.VMEM((n, rhs), F32),
+        compiler_params=grant(12),
+        cost_estimate=pl.CostEstimate(flops=2_000_000_000, bytes_accessed=8_000_000, transcendentals=0),
+    )(*in_hbm(ordered, leaves), et, fe, far)
     far = lax.all_to_all(far, ("zl", "x"), 0, 0, tiled=True)
     far = lax.all_gather(far.reshape(half, rhs), "c", axis=0, tiled=True)
     step = 256
@@ -243,7 +308,7 @@
         out_shape=shape((n, rhs), BF16),
         scratch_shapes=[pltpu.VMEM((2 * half, rhs), BF16)],
         compiler_params=grant(8),
-    )(far, ut, base)
+    )(far, *in_vmem(ut), base)
 
 
 def solution(mesh):

time: 85.4 us -> 80.5 us (0.943)
  blocking collectives: 27.9 us -> 42.3 us
  starting transfers between devices: 17.5 us -> 8.15 us
  local copies, waits for them, and re-layouts: 8.95 us -> 0.01 us
  waiting for transfers between devices: 11 us -> 7.91 us
  Pallas kernels: 18.4 us -> 20.8 us
    all_to_all x1, blocking collectives: 14.4 us -> 27.5 us  [per_device(): rows = lax.all_to_all(rows, ('y', 'zh'), 0, 0, tiled=True)]
    all_to_all x1, starting transfers between devices: 14 us -> 4.6 us  [per_device(): far = lax.all_to_all(far, ('zl', 'x'), 0, 0, tiled=True)]
    unnamed x22 -> x2, local copies, waits for them, and re-layouts: 8.95 us -> 0.01 us
    all_to_all x1, waiting for transfers between devices: 11 us -> 2.99 us  [per_device(): got = lax.all_to_all(partial, ('zl', 'x'), 0, 0, tiled=True)]
    all_to_all x1, waiting for transfers between devices: 0.01 us -> 4.92 us  [per_device(): far = lax.all_to_all(far, ('zl', 'x'), 0, 0, tiled=True)]
    pallas_call x4 -> x5, Pallas kernels: 16.1 us -> 18.5 us  [the longest x1 8.04 us: per_device(): pl.pallas_call(local_kernel, name='local', in_specs=[SMEM, SMEM] + [HBM]...]
    all_gather x1, blocking collectives: 4.65 us -> 5.98 us  [per_device(): far = lax.all_gather(far.reshape(half, rhs), 'c', axis=0, tiled=True)]
  transfers between devices with their start and end apart: 2 -> 2, of which waited for: 1 -> 2; matrix products, arithmetic and copies ran while one was open for 0% -> 0% of each run, Pallas kernels for 13% -> 16%
where the time goes in v3:
time: 80.5 us; the launch traced here: 80.1 us
  blocking collectives  42.3 us (53%)
  Pallas kernels  20.8 us (26%)
  starting transfers between devices  8.15 us (10%)
  waiting for transfers between devices  7.91 us (10%)
  other arithmetic  0.82 us (1%)
    all_to_all x1, blocking collectives, per_device(): rows = lax.all_to_all(rows, ('y', 'zh'), 0, 0, tiled=True)  27.5 us
    all_gather x1, blocking collectives, per_device(): pair = lax.all_gather(send, 'c')  8.85 us
    pallas_call x1, Pallas kernels, per_device(): pl.pallas_call(local_kernel, name='local', in_specs=[SMEM, SMEM] + [HBM]...  8.04 us
    all_gather x1, blocking collectives, per_device(): far = lax.all_gather(far.reshape(half, rhs), 'c', axis=0, tiled=True)  5.98 us
    all_to_all x1, waiting for transfers between devices, per_device(): far = lax.all_to_all(far, ('zl', 'x'), 0, 0, tiled=True)  4.92 us
    all_to_all x1, starting transfers between devices, per_device(): far = lax.all_to_all(far, ('zl', 'x'), 0, 0, tiled=True)  4.6 us
    pallas_call x1, Pallas kernels, per_device(): pl.pallas_call(base_kernel, name='base', grid=(n // 256,), in_specs=[pl.B...  4.54 us
    pallas_call x1, Pallas kernels, per_device(): pl.pallas_call(coef_kernel, name='coef', in_specs=[SMEM, HBM, HBM, HBM],...  3.85 us
  transfers between devices with their start and end apart: 2, of which 2 were waited for; matrix products, arithmetic and copies ran while one was open for 0% of the time, Pallas kernels for 16%

profile of v3, /device:TPU:1, one launch (start us, length us, event | category | flops | bytes accessed | tf_op | source)
XLA Modules:
  0.0 80.1 jit_solution(4614639889137202384)
XLA Ops:
  0.0 3.9 %coef.1 = (f32[128,640]{1,0:T(8,128)S(1)}, f32[160,640]{1,0:T(8,128)S(1)}) custom-call(s32[1]{0:T(128)} %bitcast.2.core, s32[1,1024]{1,0:T(1,128)} %bitcast.16, bf16[10,32,1024]{2,1,0:T(8,128)(2,1)} %v_hbm.3, bf16[1024,640]{1,0:T(8,128)(2,1)} %s_hbm.3), custom_call_target="tpu_custom_call" | custom-call | tf_op jit(solution)/shard_map/coef/pallas_call | solution.py:206
  3.9 0.0 copy-start
  3.9 8.9 %all-gather = f32[320,640]{1,0:T(8,128)S(1)} all-gather(f32[160,640]{1,0:T(8,128)S(1)} %get-tuple-element.16), channel_id=2, replica_groups=mesh['y'=4,'zh'=4,'zl'=4,'x'=4,'c'=2] {'c'}, dimensions={0}, use_global_device_ids=true | all-gather | bytes 1228800 | tf_op jit(solution)/shard_map/all_gather | solution.py:223
  12.7 0.7 fusion.1._
  13.5 3.5 %all-to-all-start = ((f32[16,8,640]{2,1,0:T(8,128)}), f32[16,8,640]{2,1,0:T(8,128)S(1)}, u32[]{:S(2)}, u32[]{:S(2)}) async-start(f32[16,8,640]{2,1,0:T(8,128)} %fusion.1._), calls=%async_computation | async-start | bytes 655360 | tf_op jit(solution)/shard_map/all_to_all | solution.py:259
  17.0 0.1 pad_add_fusion.place
  17.1 0.0 copy-done
  17.1 8.0 %local.1 = (bf16[1024,640]{1,0:T(8,128)(2,1)}, bf16[1024,1024]{1,0:T(8,128)(2,1)}, bf16[1024,256]{1,0:T(8,128)(2,1)S(1)}, bf16[1024,96]{1,0:T(8,128)(2,1)S(1)}, ...) custom-call(s32[10]{0:T(128)S(1)} %copy-done, s32[1]{0:T(128)} %bitcast.2.core, s32[1,1024]{1,0:T(1,128)} %bitcast.17, ...), custom_call_target="tpu_custom_call" | custom-call | flops 3500000000 | bytes 8000000 | tf_op jit(solution)/shard_map/local/pallas_call | solution.py:226
  25.2 3.0 %all-to-all-done.got_ref = f32[16,8,640]{2,1,0:T(8,128)S(1)} async-done(((f32[16,8,640]{2,1,0:T(8,128)}), f32[16,8,640]{2,1,0:T(8,128)S(1)}, u32[]{:S(2)}, u32[]{:S(2)}) %all-to-all-start) | async-done | bytes 327712 | tf_op jit(solution)/shard_map/all_to_all | solution.py:259
  28.1 0.6 middle.1
  28.8 27.5 %all_to_all.15.got_ref = f32[16,1,640]{2,1,0:T(1,128)S(1)} all-to-all(f32[16,1,640]{2,1,0:T(1,128)S(1)} %get-tuple-element.18), channel_id=1, replica_groups=mesh['y'=4,'zh'=4,'zl'=4,'x'=4,'c'=2] {'y','zh'}, dimensions={0} | all-to-all | bytes 81920 | tf_op jit(solution)/shard_map/all_to_all | solution.py:269
  56.2 1.4 %far.1._ = f32[16,8,640]{2,1,0:T(8,128)} custom-call(s32[2]{0:T(128)S(1)} %pad_add_fusion.place, f32[16,1,640]{2,1,0:T(1,128)S(1)} %all_to_all.15.got_ref, f32[16,8,640]{2,1,0:T(8,128)S(1)} %get-tuple-element.19.fine_ref), custom_call_target="tpu_custom_call" | custom-call | tf_op jit(solution)/shard_map/far/pallas_call | solution.py:270
  57.7 4.6 %all-to-all-start.2 = ((f32[16,8,640]{2,1,0:T(8,128)}), f32[16,8,640]{2,1,0:T(8,128)}, u32[]{:S(2)}, u32[]{:S(2)}) async-start(f32[16,8,640]{2,1,0:T(8,128)} %far.1._), calls=%async_computation.2 | async-start | bytes 655360 | tf_op jit(solution)/shard_map/all_to_all | solution.py:295
  62.3 4.5 %base.1.base_ref = f32[1024,640]{1,0:T(8,128)S(1)} custom-call(bf16[1024,640]{1,0:T(8,128)(2,1)} %get-tuple-element.21.ord_ref, bf16[1024,1024]{1,0:T(8,128)(2,1)} %get-tuple-element.22.lp_ref, bf16[1024,96]{1,0:T(8,128)(2,1)S(1)} %get-tuple-element.23.et_ref, bf16[96,640]{1,0:T(8,128)(2,1)S(1)} %get-tuple-element.24.fe_ref, f32[16,8,640]{2,1,0:T(8,128)} %far.1._), custom_call_target="tpu_custom_call" | custom-call | flops 2000000000 | bytes 8000000 | tf_op jit(solution)/shard_map/base/pallas_call | solution.py:279
  66.8 4.9 %all-to-all-done.2 = f32[16,8,640]{2,1,0:T(8,128)} async-done(((f32[16,8,640]{2,1,0:T(8,128)}), f32[16,8,640]{2,1,0:T(8,128)}, u32[]{:S(2)}, u32[]{:S(2)}) %all-to-all-start.2) | async-done | bytes 327712 | tf_op jit(solution)/shard_map/all_to_all | solution.py:295
  71.8 6.0 %all_gather.11.far_ref = f32[256,640]{1,0:T(8,128)S(1)} all-gather(f32[128,640]{1,0:T(8,128)} %bitcast.7), channel_id=1, replica_groups=mesh['y'=4,'zh'=4,'zl'=4,'x'=4,'c'=2] {'c'}, dimensions={0}, use_global_device_ids=true | all-gather | bytes 983040 | tf_op jit(solution)/shard_map/all_gather | solution.py:296
  77.7 2.3 %last.1 = bf16[1024,640]{1,0:T(8,128)(2,1)} custom-call(f32[256,640]{1,0:T(8,128)S(1)} %all_gather.11.far_ref, bf16[1024,256]{1,0:T(8,128)(2,1)S(1)} %get-tuple-element.20.ut_ref, f32[1024,640]{1,0:T(8,128)S(1)} %base.1.base_ref), custom_call_target="tpu_custom_call" | custom-call | tf_op jit(solution)/shard_map/last/pallas_call | solution.py:298
Async XLA Ops:
  3.9 13.2 %copy-start = (s32[10]{0:T(128)S(1)}, s32[10]{0:T(128)}, u32[]{:S(2)}) copy-start(s32[10]{0:T(128)} %ranks.1) | copy-start | bytes 124
  13.5 14.7 %all-to-all-start = ((f32[16,8,640]{2,1,0:T(8,128)}), f32[16,8,640]{2,1,0:T(8,128)S(1)}, u32[]{:S(2)}, u32[]{:S(2)}) async-start(f32[16,8,640]{2,1,0:T(8,128)} %fusion.1._), calls=%async_computation | async-start | bytes 655360 | tf_op jit(solution)/shard_map/all_to_all | solution.py:259
  57.7 14.1 %all-to-all-start.2 = ((f32[16,8,640]{2,1,0:T(8,128)}), f32[16,8,640]{2,1,0:T(8,128)}, u32[]{:S(2)}, u32[]{:S(2)}) async-start(f32[16,8,640]{2,1,0:T(8,128)} %far.1._), calls=%async_computation.2 | async-start | bytes 655360 | tf_op jit(solution)/shard_map/all_to_all | solution.py:295

commit v4 on v3

v4 whole, which is shorter than its diff:
```python
import jax
import jax.numpy as jnp
from jax import lax
from jax.experimental import pallas as pl
from jax.experimental.pallas import tpu as pltpu
from jax.sharding import Mesh
from jax.sharding import PartitionSpec as P

AXES = ("y", "zh", "z1", "z0", "x", "c")
OUTER = ("z0", "x")
MIDDLE = ("y", "zh", "z1")
F32 = jnp.float32
BF16 = jnp.bfloat16
NN = (((1,), (0,)), ((), ()))
NT = (((1,), (1,)), ((), ()))


def dot(a, b, dims=NN):
    return lax.dot_general(a, b, dims, preferred_element_type=F32)


def one_hot_t(perm, first, count):
    n = perm.shape[1]
    j = lax.broadcasted_iota(jnp.int32, (count, n), 0) + first
    return jnp.where(j == perm, 1.0, 0.0).astype(BF16)


def coef_kernel(core, perm_hbm, v_hbm, s_hbm, mine_ref, send_ref, acc, perm_ref, v_ref, s_ref, perm_sem, v_sem, s_sem):
    n = s_ref.shape[0]
    levels, rank, _ = v_ref.shape
    step = 256
    perm_copy = pltpu.make_async_copy(perm_hbm, perm_ref, perm_sem)
    perm_copy.start()
    v_copy = pltpu.make_async_copy(v_hbm.at[0:levels], v_ref, v_sem)
    v_copy.start()
    s_copy = [
        pltpu.make_async_copy(s_hbm.at[j : j + step], s_ref.at[j : j + step], s_sem.at[j // step])
        for j in range(0, n, step)
    ]
    for copy in s_copy:
        copy.start()
    perm_copy.wait()
    perm = perm_ref[...] & (n - 1)
    hot = one_hot_t(perm, 0, step)
    v_copy.wait()
    v = v_ref[...].reshape(levels * rank, n)
    total = None
    for j in range(0, n, step):
        vp = dot(v, hot, NT).astype(BF16)
        if j + step < n:
            hot = one_hot_t(perm, j + step, step)
        s_copy[j // step].wait()
        part = dot(vp, s_ref[j : j + step, :])
        total = part if total is None else total + part
    half = 4 * rank
    me = core[0]
    mine = pl.ds(pl.multiple_of(me * half, half), half)
    theirs = pl.ds(pl.multiple_of((1 - me) * half, half), half)
    for d in range(acc.shape[0]):
        lanes = slice(d * 128, (d + 1) * 128)
        for level in range(8):
            acc[d, pl.ds(level, rank, stride=8), :] = total[level * rank : (level + 1) * rank, lanes]
        mine_ref[:, lanes] = acc[d, mine, :]
        send_ref[0:half, lanes] = acc[d, theirs, :]
    send_ref[half : half + rank, :] = total[8 * rank : 9 * rank]


def order_kernel(
    core, perm_hbm, s_hbm, v_hbm, pair_ref, _,
    ord_hbm, fe_ref, token_ref,
    perm_ref, s_ref, v_ref, p_ref, ord_ref, sems, ord_sems,
):
    n, _ = s_ref.shape
    rank = v_ref.shape[0]
    leaf = n // 2
    step = 256
    pairs = ((perm_hbm, perm_ref), (s_hbm, s_ref), (v_hbm.at[9], v_ref))
    copies = [pltpu.make_async_copy(a, b, sems.at[k]) for k, (a, b) in enumerate(pairs)]
    for copy in copies:
        copy.start()
    copies[0].wait()
    perm = perm_ref[...] & (n - 1)
    lane = lax.broadcasted_iota(jnp.int32, (128, 128), 1)
    for i in range(0, n, 128):
        column = jnp.broadcast_to(perm[:, i : i + 128], (128, 128)).T
        for j in range(0, n, 128):
            p_ref[i : i + 128, j : j + 128] = jnp.where(column == lane + j, 1.0, 0.0).astype(BF16)
    for copy in copies[1:]:
        copy.wait()

    def kept_copy(b):
        rows = pl.ds(pl.multiple_of(b * step, step), step)
        return pltpu.make_async_copy(ord_ref.at[rows], ord_hbm.at[rows], ord_sems.at[b])

    def order(b, _):
        rows = pl.ds(pl.multiple_of(b * step, step), step)
        ord_ref[rows, :] = dot(p_ref[rows, :], s_ref[...]).astype(BF16)
        kept_copy(b).start()
        return 0

    lax.fori_loop(0, n // step, order, 0)
    fe_ref[0:rank, :] = pair_ref[1 - core[0], 4 * rank :, :].astype(BF16)
    fe_ref[rank : 2 * rank, :] = dot(v_ref[:, leaf:], ord_ref[leaf:, :]).astype(BF16)
    fe_ref[2 * rank : 3 * rank, :] = dot(v_ref[:, :leaf], ord_ref[:leaf, :]).astype(BF16)
    token_ref[...] = jnp.zeros_like(token_ref)
    for b in range(n // step):
        kept_copy(b).wait()


def bases_kernel(
    ranks, perm_hbm, leaf_hbm, u_hbm, _,
    lp_hbm, ut_ref, et_ref, token_ref,
    perm_ref, leaf_ref, u_ref, pt_ref, uf_ref, us_ref, ue_ref, lp_ref, sems, lp_sems,
):
    n, leaf = leaf_ref.shape
    rank = u_ref.shape[1]
    step = 256
    pairs = ((perm_hbm, perm_ref), (leaf_hbm, leaf_ref), (u_hbm, u_ref))
    copies = [pltpu.make_async_copy(a, b, sems.at[k]) for k, (a, b) in enumerate(pairs)]
    for copy in copies:
        copy.start()
    copies[0].wait()
    perm = perm_ref[...] & (n - 1)
    for j in range(0, n, step):
        pt_ref[j : j + step, :] = one_hot_t(perm, j, step)
    for copy in copies[1:]:
        copy.wait()

    row = lax.broadcasted_iota(jnp.int32, (rank, n), 0)
    lane_n = lax.broadcasted_iota(jnp.int32, (rank, n), 1)
    for level in range(8):
        kept = jnp.where(row < ranks[level], u_ref[level].astype(F32), 0.0)
        for d in range(n // 128):
            uf_ref[d, pl.ds(level, rank, stride=8), :] = kept[:, d * 128 : (d + 1) * 128]
    for d in range(n // 128):
        us_ref[:, d * 128 : (d + 1) * 128] = uf_ref[d].astype(BF16)
    ue_ref[0:rank, :] = jnp.where(row < ranks[8], u_ref[8].astype(F32), 0.0).astype(BF16)
    last = jnp.where(row < ranks[9], u_ref[9].astype(F32), 0.0)
    ue_ref[rank : 2 * rank, :] = jnp.where(lane_n < leaf, last, 0.0).astype(BF16)
    ue_ref[2 * rank : 3 * rank, :] = jnp.where(lane_n < leaf, 0.0, last).astype(BF16)

    def kept_copy(b):
        rows = pl.ds(pl.multiple_of(b * step, step), step)
        return pltpu.make_async_copy(lp_ref.at[rows], lp_hbm.at[rows], lp_sems.at[b])

    def permute(b, _):
        rows = pl.ds(pl.multiple_of(b * step, step), step)
        for g in range(0, n, leaf):
            lp_ref[rows, g : g + leaf] = dot(pt_ref[rows, g : g + leaf], leaf_ref[g : g + leaf, :]).astype(BF16)
        kept_copy(b).start()
        ut_ref[rows, :] = dot(pt_ref[rows, :], us_ref[...], NT).astype(BF16)
        et_ref[rows, :] = dot(pt_ref[rows, :], ue_ref[...], NT).astype(BF16)
        return 0

    lax.fori_loop(0, n // step, permute, 0)
    token_ref[...] = jnp.zeros_like(token_ref)
    for b in range(n // step):
        kept_copy(b).wait()


def base_kernel(ord_ref, lp_ref, et_ref, fe_ref, _, base_ref):
    base_ref[...] = dot(lp_ref[...], ord_ref[...]) + dot(et_ref[...], fe_ref[...])


def level_at(apart):
    for bit, row in ((16, 0), (8, 1), (4, 2), (2, 3)):
        if apart & bit:
            return row
    return 4


def middle_kernel(me, got_ref, _, out_ref, fine_ref):
    rows = got_ref.shape[1]
    level = lax.broadcasted_iota(jnp.int32, got_ref.shape[1:], 0) & 7
    got = lambda z, x: got_ref[z * 4 + x]
    sums = [(got(z, 0) + got(z, 1)) + (got(z, 2) + got(z, 3)) for z in range(2)]
    total = sums[0] + sums[1]
    for z in range(2):
        for x in range(4):
            high = jnp.where(level == 7, got(z, x ^ 1), got(z, x ^ 2) + got(z, x ^ 3))
            fine_ref[z * 4 + x] = jnp.where(level >= 6, high, sums[z ^ 1])
    for row in range(5):
        sent = jnp.concatenate([total[r + row : r + row + 1] for r in range(0, rows, 8)], axis=0)
        for apart in range(out_ref.shape[0]):
            if level_at(apart) == row:
                out_ref[me[0] ^ apart] = sent


def far_kernel(me, got_ref, fine_ref, _, out_ref, acc):
    rows = acc.shape[0]
    acc[...] = jnp.zeros_like(acc)
    for row in range(5):
        parts = [got_ref[me[0] ^ k] for k in range(1, got_ref.shape[0]) if level_at(k) == row]
        while len(parts) > 1:
            parts = [sum(parts[k : k + 2]) for k in range(0, len(parts), 2)]
        for j in range(rows // 8):
            acc[j * 8 + row : j * 8 + row + 1, :] = parts[0][j : j + 1]
    level = lax.broadcasted_iota(jnp.int32, acc.shape, 0) & 7
    far = acc[...]
    for p in range(out_ref.shape[0]):
        out_ref[p] = jnp.where(level < 5, far, fine_ref[p])


def last_kernel(far_ref, ut_ref, base_ref, out_ref, far16):
    @pl.when(pl.program_id(0) == 0)
    def _():
        far16[...] = far_ref[...].astype(BF16)

    out_ref[...] = (base_ref[...] + dot(ut_ref[...], far16[...])).astype(BF16)


SMEM = pl.BlockSpec(memory_space=pltpu.SMEM)
VMEM = pl.BlockSpec(memory_space=pltpu.VMEM)
ANY = pl.BlockSpec(memory_space=pl.ANY)
HBM = pl.BlockSpec(memory_space=pltpu.HBM)


def grant(mib):
    return pltpu.CompilerParams(vmem_limit_bytes=mib << 20)


def in_hbm(*arrays):
    return [pltpu.with_memory_space_constraint(a, pltpu.HBM) for a in arrays]


def in_vmem(*arrays):
    return [pltpu.with_memory_space_constraint(a, pltpu.VMEM) for a in arrays]


def shape(dims, dtype=F32):
    return jax.ShapeDtypeStruct(dims, dtype)


def per_device(sources, tree_perm, leaf_blocks, u_factors, v_factors, level_ranks):
    n, rhs = sources.shape
    rank = u_factors.shape[1]
    half = 4 * rank
    core = lax.axis_index("c").reshape(1)
    me = lax.axis_index(MIDDLE).reshape(1)
    perm = tree_perm.reshape(1, n)
    mine, send = pl.pallas_call(
        coef_kernel,
        name="coef",
        in_specs=[SMEM, HBM, HBM, HBM],
        out_specs=[VMEM, VMEM],
        out_shape=[shape((half, rhs)), shape((half + rank, rhs))],
        scratch_shapes=[
            pltpu.VMEM((rhs // 128, 2 * half, 128), F32),
            pltpu.VMEM((1, n), jnp.int32),
            pltpu.VMEM((9, rank, n), BF16),
            pltpu.VMEM((n, rhs), BF16),
            pltpu.SemaphoreType.DMA,
            pltpu.SemaphoreType.DMA,
            pltpu.SemaphoreType.DMA((n // 256,)),
        ],
        compiler_params=grant(14),
    )(core, *in_hbm(perm, v_factors, sources))
    pair = lax.all_gather(send, "c")
    other = lax.dynamic_index_in_dim(pair, 1 - core[0], 0, keepdims=False)
    partial = (mine + other[:half]).reshape(8, 16, rhs)
    ordered, fe, token = pl.pallas_call(
        order_kernel,
        name="order",
        in_specs=[SMEM, HBM, HBM, HBM, VMEM, ANY],
        out_specs=[HBM, VMEM, VMEM],
        out_shape=[pltpu.HBM((n, rhs), BF16), pltpu.VMEM((3 * rank, rhs), BF16), shape((8, 128))],
        scratch_shapes=[
            pltpu.VMEM((1, n), jnp.int32),
            pltpu.VMEM((n, rhs), BF16),
            pltpu.VMEM((rank, n), BF16),
            pltpu.VMEM((n, n), BF16),
            pltpu.VMEM((n, rhs), BF16),
            pltpu.SemaphoreType.DMA((3,)),
            pltpu.SemaphoreType.DMA((n // 256,)),
        ],
        compiler_params=grant(16),
        cost_estimate=pl.CostEstimate(flops=2_000_000_000, bytes_accessed=4_000_000, transcendentals=0),
    )(core, *in_hbm(perm, sources, v_factors), *in_vmem(pair), partial)
    got = lax.all_to_all(partial, OUTER, 0, 0, tiled=True)
    rows, fine = pl.pallas_call(
        middle_kernel,
        name="middle",
        in_specs=[SMEM, VMEM, ANY],
        out_specs=[VMEM, VMEM],
        out_shape=[shape((32, 2, rhs)), shape((8, 16, rhs))],
        compiler_params=grant(4),
    )(me, got, token)
    leaves, ut, et, token = pl.pallas_call(
        bases_kernel,
        name="bases",
        in_specs=[SMEM, HBM, HBM, HBM, ANY],
        out_specs=[HBM, VMEM, VMEM, VMEM],
        out_shape=[
            pltpu.HBM((n, n), BF16),
            pltpu.VMEM((n, 2 * half), BF16),
            pltpu.VMEM((n, 3 * rank), BF16),
            shape((8, 128)),
        ],
        scratch_shapes=[
            pltpu.VMEM((1, n), jnp.int32),
            pltpu.VMEM(leaf_blocks.shape, BF16),
            pltpu.VMEM(u_factors.shape, BF16),
            pltpu.VMEM((n, n), BF16),
            pltpu.VMEM((n // 128, 2 * half, 128), F32),
            pltpu.VMEM((2 * half, n), BF16),
            pltpu.VMEM((3 * rank, n), BF16),
            pltpu.VMEM((n, n), BF16),
            pltpu.SemaphoreType.DMA((3,)),
            pltpu.SemaphoreType.DMA((n // 256,)),
        ],
        compiler_params=grant(20),
        cost_estimate=pl.CostEstimate(flops=2_000_000_000, bytes_accessed=4_000_000, transcendentals=0),
    )(level_ranks, *in_hbm(perm, leaf_blocks, u_factors), fine)
    rows = lax.all_to_all(rows, MIDDLE, 0, 0, tiled=True)
    far = pl.pallas_call(
        far_kernel,
        name="far",
        in_specs=[SMEM, VMEM, VMEM, ANY],
        out_specs=VMEM,
        out_shape=shape((8, 16, rhs)),
        scratch_shapes=[pltpu.VMEM((16, rhs), F32)],
        compiler_params=grant(4),
    )(me, rows, fine, token)
    base = pl.pallas_call(
        base_kernel,
        name="base",
        grid=(n // 256,),
        in_specs=[
            pl.BlockSpec((n, rhs), lambda i: (0, 0)),
            pl.BlockSpec((256, n), lambda i: (i, 0)),
            pl.BlockSpec((256, 3 * rank), lambda i: (i, 0)),
            pl.BlockSpec((3 * rank, rhs), lambda i: (0, 0)),
            ANY,
        ],
        out_specs=pl.BlockSpec((256, rhs), lambda i: (i, 0)),
        out_shape=pltpu.VMEM((n, rhs), F32),
        compiler_params=grant(12),
        cost_estimate=pl.CostEstimate(flops=2_000_000_000, bytes_accessed=8_000_000, transcendentals=0),
    )(*in_hbm(ordered, leaves), et, fe, far)
    far = lax.all_to_all(far, OUTER, 0, 0, tiled=True)
    far = lax.all_gather(far.reshape(half, rhs), "c", axis=0, tiled=True)
    step = 256
    return pl.pallas_call(
        last_kernel,
        name="last",
        grid=(n // step,),
        in_specs=[
            pl.BlockSpec((2 * half, rhs), lambda i: (0, 0)),
            pl.BlockSpec((step, 2 * half), lambda i: (i, 0)),
            pl.BlockSpec((step, rhs), lambda i: (i, 0)),
        ],
        out_specs=pl.BlockSpec((step, rhs), lambda i: (i, 0)),
        out_shape=shape((n, rhs), BF16),
        scratch_shapes=[pltpu.VMEM((2 * half, rhs), BF16)],
        compiler_params=grant(8),
    )(far, *in_vmem(ut), base)


def solution(mesh):
    torus = Mesh(mesh.devices.reshape(4, 4, 2, 2, 4, 2), AXES)
    placed = (P(AXES, None), P(AXES), P(AXES, None), P(None, None, AXES), P(None, None, AXES), P())
    return jax.shard_map(
        per_device, mesh=torus, in_specs=placed, out_specs=P(AXES, None), check_vma=False
    )
```

time: 80.5 us -> 73.8 us (0.917)
  blocking collectives: 42.3 us -> 16.1 us
  starting transfers between devices: 8.15 us -> 21.7 us
  waiting for transfers between devices: 7.91 us -> 12.1 us
  Pallas kernels: 20.8 us -> 22.6 us
    all_to_all x1 -> x0, blocking collectives: 27.5 us -> none  [per_device(): rows = lax.all_to_all(rows, ('y', 'zh'), 0, 0, tiled=True)]
    all_to_all x2 -> x3, starting transfers between devices: 8.15 us -> 21.7 us  [the longest x1 13.6 us: per_device(): rows = lax.all_to_all(rows, MIDDLE, 0, 0, tiled=True)]
    all_to_all x2 -> x3, waiting for transfers between devices: 7.91 us -> 12.1 us  [the longest x1 8.28 us: per_device(): rows = lax.all_to_all(rows, MIDDLE, 0, 0, tiled=True)]
    pallas_call x2 -> x3, Pallas kernels: 9.46 us -> 11.1 us  [the longest x1 5.86 us: per_device(): pl.pallas_call(bases_kernel, name='bases', in_specs=[SMEM, HBM, HBM, HBM,...]
    all_gather x1, blocking collectives: 5.98 us -> 7.2 us  [per_device(): far = lax.all_gather(far.reshape(half, rhs), 'c', axis=0, tiled=True)]
  transfers between devices with their start and end apart: 2 -> 3, of which waited for: 2 -> 3; matrix products, arithmetic and copies ran while one was open for 0% -> 0% of each run, Pallas kernels for 16% -> 20%
where the time goes in v4:
time: 73.8 us; the launch traced here: 73.3 us
  Pallas kernels  22.6 us (31%)
  starting transfers between devices  21.7 us (29%)
  blocking collectives  16.1 us (22%)
  waiting for transfers between devices  12.1 us (16%)
  other arithmetic  0.76 us (1%)
    all_to_all x1, starting transfers between devices, per_device(): rows = lax.all_to_all(rows, MIDDLE, 0, 0, tiled=True)  13.6 us
    all_gather x1, blocking collectives, per_device(): pair = lax.all_gather(send, 'c')  8.85 us
    all_to_all x1, waiting for transfers between devices, per_device(): rows = lax.all_to_all(rows, MIDDLE, 0, 0, tiled=True)  8.28 us
    all_gather x1, blocking collectives, per_device(): far = lax.all_gather(far.reshape(half, rhs), 'c', axis=0, tiled=True)  7.2 us
    pallas_call x1, Pallas kernels, per_device(): pl.pallas_call(bases_kernel, name='bases', in_specs=[SMEM, HBM, HBM, HBM,...  5.86 us
    all_to_all x1, starting transfers between devices, per_device(): far = lax.all_to_all(far, OUTER, 0, 0, tiled=True)  4.69 us
    pallas_call x1, Pallas kernels, per_device(): pl.pallas_call(base_kernel, name='base', grid=(n // 256,), in_specs=[pl.B...  4.55 us
    pallas_call x1, Pallas kernels, per_device(): pl.pallas_call(order_kernel, name='order', in_specs=[SMEM, HBM, HBM, HBM,...  4.48 us
  transfers between devices with their start and end apart: 3, of which 3 were waited for; matrix products, arithmetic and copies ran while one was open for 0% of the time, Pallas kernels for 20%

profile of v4, /device:TPU:1, one launch (start us, length us, event | category | flops | bytes accessed | tf_op | source)
XLA Modules:
  0.0 73.3 jit_solution(1314295904827767235)
XLA Ops:
  0.0 3.9 %coef.1 = (f32[128,640]{1,0:T(8,128)S(1)}, f32[160,640]{1,0:T(8,128)S(1)}) custom-call(s32[1]{0:T(128)} %bitcast.1.core, s32[1,1024]{1,0:T(1,128)} %bitcast.12, bf16[10,32,1024]{2,1,0:T(8,128)(2,1)} %v_hbm.3, bf16[1024,640]{1,0:T(8,128)(2,1)} %s_hbm.3), custom_call_target="tpu_custom_call" | custom-call | tf_op jit(solution)/shard_map/coef/pallas_call | solution.py:241
  3.9 8.9 %all-gather = f32[320,640]{1,0:T(8,128)S(1)} all-gather(f32[160,640]{1,0:T(8,128)S(1)} %get-tuple-element.17), channel_id=2, replica_groups=mesh['y'=4,'zh'=4,'z1'=2,'z0'=2,'x'=4,'c'=2] {'c'}, dimensions={0}, use_global_device_ids=true | all-gather | bytes 1228800 | tf_op jit(solution)/shard_map/all_gather | solution.py:258
  12.7 0.8 %fusion = f32[128,640]{1,0:T(8,128)} fusion(f32[128,640]{1,0:T(8,128)S(1)} %get-tuple-element.16, f32[2,160,640]{2,1,0:T(8,128)S(1)} %bitcast.10, s32[]{:T(128)S(6)} %select_n.4), kind=kLoop, calls=%fused_computation.1 | loop fusion | flops 81920 | bytes 983044 | tf_op jit(solution)/shard_map/add | solution.py:260
  13.5 3.4 %all-to-all-start = ((f32[8,16,640]{2,1,0:T(8,128)}), f32[8,16,640]{2,1,0:T(8,128)S(1)}, u32[]{:S(2)}, u32[]{:S(2)}) async-start(f32[8,16,640]{2,1,0:T(8,128)} %bitcast.5._), calls=%async_computation | async-start | bytes 655360 | tf_op jit(solution)/shard_map/all_to_all | solution.py:279
  16.9 0.0 copy-start
  16.9 4.5 %order.1 = (bf16[1024,640]{1,0:T(8,128)(2,1)}, bf16[96,640]{1,0:T(8,128)(2,1)S(1)}, f32[8,128]{1,0:T(8,128)S(1)}) custom-call(s32[1]{0:T(128)} %bitcast.1.core, s32[1,1024]{1,0:T(1,128)} %bitcast.13, bf16[1024,640]{1,0:T(8,128)(2,1)} %s_hbm.3, bf16[10,32,1024]{2,1,0:T(8,128)(2,1)} %v_hbm.3, f32[2,160,640]{2,1,0:T(8,128)S(1)} %bitcast.11, f32[8,16,640]{2,1,0:T(8,128)} %bitcast.5._), custom_call_target="tpu_custom_call" | custom-call | flops 2000000000 | bytes 4000000 | tf_op jit(solution)/shard_map/order/pallas_call | solution.py:261
  21.4 2.0 %all-to-all-done.got_ref = f32[8,16,640]{2,1,0:T(8,128)S(1)} async-done(((f32[8,16,640]{2,1,0:T(8,128)}), f32[8,16,640]{2,1,0:T(8,128)S(1)}, u32[]{:S(2)}, u32[]{:S(2)}) %all-to-all-start) | async-done | bytes 327712 | tf_op jit(solution)/shard_map/all_to_all | solution.py:279
  23.4 0.7 middle.1
  24.1 13.6 %all-to-all-start.1 = ((f32[32,2,640]{2,1,0:T(2,128)}), f32[32,2,640]{2,1,0:T(2,128)S(1)}, u32[]{:S(2)}, u32[]{:S(2)}) async-start(f32[32,2,640]{2,1,0:T(2,128)} %get-tuple-element.19), calls=%async_computation.1 | async-start | bytes 327680 | tf_op jit(solution)/shard_map/all_to_all | solution.py:314
  37.7 0.0 copy-done
  37.7 5.9 %bases.1 = (bf16[1024,1024]{1,0:T(8,128)(2,1)}, bf16[1024,256]{1,0:T(8,128)(2,1)S(1)}, bf16[1024,96]{1,0:T(8,128)(2,1)S(1)}, f32[8,128]{1,0:T(8,128)S(1)}) custom-call(s32[10]{0:T(128)S(1)} %copy-done, s32[1,1024]{1,0:T(1,128)} %bitcast.14, bf16[1024,512]{1,0:T(8,128)(2,1)} %leaf_hbm.1, bf16[10,32,1024]{2,1,0:T(8,128)(2,1)} %u_hbm.1, ...), custom_call_target="tpu_custom_call" | custom-call | flops 2000000000 | bytes 4000000 | tf_op jit(solution)/shard_map/bases/pallas_call | solution.py:288
  43.6 8.3 %all-to-all-done.1.got_ref = f32[32,2,640]{2,1,0:T(2,128)S(1)} async-done(((f32[32,2,640]{2,1,0:T(2,128)}), f32[32,2,640]{2,1,0:T(2,128)S(1)}, u32[]{:S(2)}, u32[]{:S(2)}) %all-to-all-start.1) | async-done | bytes 163872 | tf_op jit(solution)/shard_map/all_to_all | solution.py:314
  51.9 0.8 %far.1._ = f32[8,16,640]{2,1,0:T(8,128)} custom-call(s32[1]{0:T(128)} %bitcast.me, f32[32,2,640]{2,1,0:T(2,128)S(1)} %all-to-all-done.1.got_ref, f32[8,16,640]{2,1,0:T(8,128)S(1)} %get-tuple-element.20._.fine_ref, f32[8,128]{1,0:T(8,128)S(1)} %get-tuple-element.21._), custom_call_target="tpu_custom_call" | custom-call | tf_op jit(solution)/shard_map/far/pallas_call | solution.py:315
  52.7 4.7 %all-to-all-start.2 = ((f32[8,16,640]{2,1,0:T(8,128)}), f32[8,16,640]{2,1,0:T(8,128)}, u32[]{:S(2)}, u32[]{:S(2)}) async-start(f32[8,16,640]{2,1,0:T(8,128)} %far.1._), calls=%async_computation.2 | async-start | bytes 655360 | tf_op jit(solution)/shard_map/all_to_all | solution.py:340
  57.4 4.5 %base.1.base_ref = f32[1024,640]{1,0:T(8,128)S(1)} custom-call(bf16[1024,640]{1,0:T(8,128)(2,1)} %get-tuple-element.23.ord_ref, bf16[1024,1024]{1,0:T(8,128)(2,1)} %get-tuple-element.24.lp_ref, bf16[1024,96]{1,0:T(8,128)(2,1)S(1)} %get-tuple-element.25.et_ref, bf16[96,640]{1,0:T(8,128)(2,1)S(1)} %get-tuple-element.26.fe_ref, f32[8,16,640]{2,1,0:T(8,128)} %far.1._), custom_call_target="tpu_custom_call" | custom-call | flops 2000000000 | bytes 8000000 | tf_op jit(solution)/shard_map/base/pallas_call | solution.py:324
  61.9 1.9 %all-to-all-done.2 = f32[8,16,640]{2,1,0:T(8,128)} async-done(((f32[8,16,640]{2,1,0:T(8,128)}), f32[8,16,640]{2,1,0:T(8,128)}, u32[]{:S(2)}, u32[]{:S(2)}) %all-to-all-start.2) | async-done | bytes 327712 | tf_op jit(solution)/shard_map/all_to_all | solution.py:340
  63.8 7.2 %all_gather.11.far_ref = f32[256,640]{1,0:T(8,128)S(1)} all-gather(f32[128,640]{1,0:T(8,128)} %bitcast.6), channel_id=1, replica_groups=mesh['y'=4,'zh'=4,'z1'=2,'z0'=2,'x'=4,'c'=2] {'c'}, dimensions={0}, use_global_device_ids=true | all-gather | bytes 983040 | tf_op jit(solution)/shard_map/all_gather | solution.py:341
  71.0 2.3 %last.1 = bf16[1024,640]{1,0:T(8,128)(2,1)} custom-call(f32[256,640]{1,0:T(8,128)S(1)} %all_gather.11.far_ref, bf16[1024,256]{1,0:T(8,128)(2,1)S(1)} %get-tuple-element.22.ut_ref, f32[1024,640]{1,0:T(8,128)S(1)} %base.1.base_ref), custom_call_target="tpu_custom_call" | custom-call | tf_op jit(solution)/shard_map/last/pallas_call | solution.py:343
Async XLA Ops:
  13.5 9.9 %all-to-all-start = ((f32[8,16,640]{2,1,0:T(8,128)}), f32[8,16,640]{2,1,0:T(8,128)S(1)}, u32[]{:S(2)}, u32[]{:S(2)}) async-start(f32[8,16,640]{2,1,0:T(8,128)} %bitcast.5._), calls=%async_computation | async-start | bytes 655360 | tf_op jit(solution)/shard_map/all_to_all | solution.py:279
  16.9 20.8 %copy-start = (s32[10]{0:T(128)S(1)}, s32[10]{0:T(128)}, u32[]{:S(2)}) copy-start(s32[10]{0:T(128)} %ranks.1) | copy-start | bytes 124
  24.1 27.8 %all-to-all-start.1 = ((f32[32,2,640]{2,1,0:T(2,128)}), f32[32,2,640]{2,1,0:T(2,128)S(1)}, u32[]{:S(2)}, u32[]{:S(2)}) async-start(f32[32,2,640]{2,1,0:T(2,128)} %get-tuple-element.19), calls=%async_computation.1 | async-start | bytes 327680 | tf_op jit(solution)/shard_map/all_to_all | solution.py:314
  52.7 11.1 %all-to-all-start.2 = ((f32[8,16,640]{2,1,0:T(8,128)}), f32[8,16,640]{2,1,0:T(8,128)}, u32[]{:S(2)}, u32[]{:S(2)}) async-start(f32[8,16,640]{2,1,0:T(8,128)} %far.1._), calls=%async_computation.2 | async-start | bytes 655360 | tf_op jit(solution)/shard_map/all_to_all | solution.py:340

commit v5 on v4

--- a/solution.py
+++ b/solution.py
@@ -33,12 +33,16 @@
     perm_copy.start()
     v_copy = pltpu.make_async_copy(v_hbm.at[0:levels], v_ref, v_sem)
     v_copy.start()
-    s_copy = [
-        pltpu.make_async_copy(s_hbm.at[j : j + step], s_ref.at[j : j + step], s_sem.at[j // step])
-        for j in range(0, n, step)
-    ]
-    for copy in s_copy:
-        copy.start()
+
+    def s_copy(k):
+        rows = pl.ds(pl.multiple_of(k * step, step), step)
+        return pltpu.make_async_copy(s_hbm.at[rows], s_ref.at[rows], s_sem.at[k])
+
+    def start(k, _):
+        s_copy(k).start()
+        return 0
+
+    lax.fori_loop(0, n // step, start, 0)
     perm_copy.wait()
     perm = perm_ref[...] & (n - 1)
     hot = one_hot_t(perm, 0, step)
@@ -49,7 +53,7 @@
         vp = dot(v, hot, NT).astype(BF16)
         if j + step < n:
             hot = one_hot_t(perm, j + step, step)
-        s_copy[j // step].wait()
+        s_copy(j // step).wait()
         part = dot(vp, s_ref[j : j + step, :])
         total = part if total is None else total + part
     half = 4 * rank
@@ -81,24 +85,22 @@
     copies[0].wait()
     perm = perm_ref[...] & (n - 1)
     lane = lax.broadcasted_iota(jnp.int32, (128, 128), 1)
-    for i in range(0, n, 128):
-        column = jnp.broadcast_to(perm[:, i : i + 128], (128, 128)).T
-        for j in range(0, n, 128):
-            p_ref[i : i + 128, j : j + 128] = jnp.where(column == lane + j, 1.0, 0.0).astype(BF16)
-    for copy in copies[1:]:
-        copy.wait()
 
     def kept_copy(b):
-        rows = pl.ds(pl.multiple_of(b * step, step), step)
+        rows = slice(b * step, (b + 1) * step)
         return pltpu.make_async_copy(ord_ref.at[rows], ord_hbm.at[rows], ord_sems.at[b])
 
-    def order(b, _):
-        rows = pl.ds(pl.multiple_of(b * step, step), step)
+    for b in range(n // step):
+        rows = slice(b * step, (b + 1) * step)
+        for i in range(b * step, (b + 1) * step, 128):
+            column = jnp.broadcast_to(perm[:, i : i + 128], (128, 128)).T
+            for j in range(0, n, 128):
+                p_ref[i : i + 128, j : j + 128] = jnp.where(column == lane + j, 1.0, 0.0).astype(BF16)
+        if b == 0:
+            copies[1].wait()
         ord_ref[rows, :] = dot(p_ref[rows, :], s_ref[...]).astype(BF16)
         kept_copy(b).start()
-        return 0
-
-    lax.fori_loop(0, n // step, order, 0)
+    copies[2].wait()
     fe_ref[0:rank, :] = pair_ref[1 - core[0], 4 * rank :, :].astype(BF16)
     fe_ref[rank : 2 * rank, :] = dot(v_ref[:, leaf:], ord_ref[leaf:, :]).astype(BF16)
     fe_ref[2 * rank : 3 * rank, :] = dot(v_ref[:, :leaf], ord_ref[:leaf, :]).astype(BF16)
@@ -158,8 +160,31 @@
         kept_copy(b).wait()
 
 
-def base_kernel(ord_ref, lp_ref, et_ref, fe_ref, _, base_ref):
-    base_ref[...] = dot(lp_ref[...], ord_ref[...]) + dot(et_ref[...], fe_ref[...])
+def base_kernel(ord_hbm, lp_hbm, et_ref, fe_ref, _, base_ref, ord_ref, lp_ref, ord_sem, lp_sems):
+    n, step = lp_ref.shape[0], 256
+    ord_copy = pltpu.make_async_copy(ord_hbm, ord_ref, ord_sem)
+    ord_copy.start()
+
+    def block(b):
+        return pl.ds(pl.multiple_of(b * step, step), step)
+
+    def lp_copy(b):
+        return pltpu.make_async_copy(lp_hbm.at[block(b)], lp_ref.at[block(b)], lp_sems.at[b])
+
+    def first(b, _):
+        lp_copy(b).start()
+        base_ref[block(b), :] = dot(et_ref[block(b), :], fe_ref[...])
+        return 0
+
+    lax.fori_loop(0, n // step, first, 0)
+    ord_copy.wait()
+
+    def second(b, _):
+        lp_copy(b).wait()
+        base_ref[block(b), :] += dot(lp_ref[block(b), :], ord_ref[...])
+        return 0
+
+    lax.fori_loop(0, n // step, second, 0)
 
 
 def level_at(apart):
@@ -201,12 +226,23 @@
         out_ref[p] = jnp.where(level < 5, far, fine_ref[p])
 
 
-def last_kernel(far_ref, ut_ref, base_ref, out_ref, far16):
-    @pl.when(pl.program_id(0) == 0)
-    def _():
-        far16[...] = far_ref[...].astype(BF16)
-
-    out_ref[...] = (base_ref[...] + dot(ut_ref[...], far16[...])).astype(BF16)
+def last_kernel(far_ref, ut_ref, base_ref, out_hbm, far16, out_ref, sems):
+    n, step = base_ref.shape[0], 256
+    far16[...] = far_ref[...].astype(BF16)
+
+    def out_copy(b):
+        rows = pl.ds(pl.multiple_of(b * step, step), step)
+        return pltpu.make_async_copy(out_ref.at[rows], out_hbm.at[rows], sems.at[b])
+
+    def apply(b, _):
+        rows = pl.ds(pl.multiple_of(b * step, step), step)
+        out_ref[rows, :] = (base_ref[rows, :] + dot(ut_ref[rows, :], far16[...])).astype(BF16)
+        out_copy(b).start()
+        return 0
+
+    lax.fori_loop(0, n // step, apply, 0)
+    for b in range(n // step):
+        out_copy(b).wait()
 
 
 SMEM = pl.BlockSpec(memory_space=pltpu.SMEM)
@@ -324,36 +360,33 @@
     base = pl.pallas_call(
         base_kernel,
         name="base",
-        grid=(n // 256,),
-        in_specs=[
-            pl.BlockSpec((n, rhs), lambda i: (0, 0)),
-            pl.BlockSpec((256, n), lambda i: (i, 0)),
-            pl.BlockSpec((256, 3 * rank), lambda i: (i, 0)),
-            pl.BlockSpec((3 * rank, rhs), lambda i: (0, 0)),
-            ANY,
-        ],
-        out_specs=pl.BlockSpec((256, rhs), lambda i: (i, 0)),
+        in_specs=[HBM, HBM, VMEM, VMEM, ANY],
+        out_specs=VMEM,
         out_shape=pltpu.VMEM((n, rhs), F32),
+        scratch_shapes=[
+            pltpu.VMEM((n, rhs), BF16),
+            pltpu.VMEM((n, n), BF16),
+            pltpu.SemaphoreType.DMA,
+            pltpu.SemaphoreType.DMA((n // 256,)),
+        ],
         compiler_params=grant(12),
         cost_estimate=pl.CostEstimate(flops=2_000_000_000, bytes_accessed=8_000_000, transcendentals=0),
-    )(*in_hbm(ordered, leaves), et, fe, far)
+    )(*in_hbm(ordered, leaves), *in_vmem(et, fe), far)
     far = lax.all_to_all(far, OUTER, 0, 0, tiled=True)
     far = lax.all_gather(far.reshape(half, rhs), "c", axis=0, tiled=True)
-    step = 256
     return pl.pallas_call(
         last_kernel,
         name="last",
-        grid=(n // step,),
-        in_specs=[
-            pl.BlockSpec((2 * half, rhs), lambda i: (0, 0)),
-            pl.BlockSpec((step, 2 * half), lambda i: (i, 0)),
-            pl.BlockSpec((step, rhs), lambda i: (i, 0)),
-        ],
-        out_specs=pl.BlockSpec((step, rhs), lambda i: (i, 0)),
-        out_shape=shape((n, rhs), BF16),
-        scratch_shapes=[pltpu.VMEM((2 * half, rhs), BF16)],
+        in_specs=[VMEM] * 3,
+        out_specs=HBM,
+        out_shape=pltpu.HBM((n, rhs), BF16),
+        scratch_shapes=[
+            pltpu.VMEM((2 * half, rhs), BF16),
+            pltpu.VMEM((n, rhs), BF16),
+            pltpu.SemaphoreType.DMA((n // 256,)),
+        ],
         compiler_params=grant(8),
-    )(far, *in_vmem(ut), base)
+    )(*in_vmem(far, ut, base))
 
 
 def solution(mesh):

time: 73.8 us -> 73 us (0.989)
  Pallas kernels: 22.6 us -> 20.7 us
  waiting for transfers between devices: 12.1 us -> 13.3 us
    pallas_call x2, Pallas kernels: 6.86 us -> 5.67 us  [the longest x1 3.79 us: per_device(): pl.pallas_call(base_kernel, name='base', in_specs=[HBM, HBM, VMEM, VMEM,...]
    all_to_all x1, waiting for transfers between devices: 1.89 us -> 2.65 us  [per_device(): far = lax.all_to_all(far, OUTER, 0, 0, tiled=True)]
  transfers between devices with their start and end apart: 3 -> 3, of which waited for: 3 -> 3; matrix products, arithmetic and copies ran while one was open for 0% -> 0% of each run, Pallas kernels for 20% -> 19%
where the time goes in v5:
time: 73 us; the launch traced here: 72.6 us
  starting transfers between devices  21.7 us (30%)
  Pallas kernels  20.7 us (28%)
  blocking collectives  16.1 us (22%)
  waiting for transfers between devices  13.3 us (18%)
  other arithmetic  0.76 us (1%)
    all_to_all x1, starting transfers between devices, per_device(): rows = lax.all_to_all(rows, MIDDLE, 0, 0, tiled=True)  13.6 us
    all_gather x1, blocking collectives, per_device(): pair = lax.all_gather(send, 'c')  8.85 us
    all_to_all x1, waiting for transfers between devices, per_device(): rows = lax.all_to_all(rows, MIDDLE, 0, 0, tiled=True)  8.28 us
    all_gather x1, blocking collectives, per_device(): far = lax.all_gather(far.reshape(half, rhs), 'c', axis=0, tiled=True)  7.2 us
    pallas_call x1, Pallas kernels, per_device(): pl.pallas_call(bases_kernel, name='bases', in_specs=[SMEM, HBM, HBM, HBM,...  5.86 us
    all_to_all x1, starting transfers between devices, per_device(): far = lax.all_to_all(far, OUTER, 0, 0, tiled=True)  4.69 us
    pallas_call x1, Pallas kernels, per_device(): pl.pallas_call(order_kernel, name='order', in_specs=[SMEM, HBM, HBM, HBM,...  4.06 us
    pallas_call x1, Pallas kernels, per_device(): pl.pallas_call(base_kernel, name='base', in_specs=[HBM, HBM, VMEM, VMEM,...  3.79 us
  transfers between devices with their start and end apart: 3, of which 3 were waited for; matrix products, arithmetic and copies ran while one was open for 0% of the time, Pallas kernels for 19%

profile of v5, /device:TPU:1, one launch (start us, length us, event | category | flops | bytes accessed | tf_op | source)
XLA Modules:
  0.0 72.6 jit_solution(17924193794794119657)
XLA Ops:
  0.0 3.6 %coef.1 = (f32[128,640]{1,0:T(8,128)S(1)}, f32[160,640]{1,0:T(8,128)S(1)}) custom-call(s32[1]{0:T(128)} %bitcast.1.core, s32[1,1024]{1,0:T(1,128)} %bitcast.12, bf16[10,32,1024]{2,1,0:T(8,128)(2,1)} %v_hbm.3, bf16[1024,640]{1,0:T(8,128)(2,1)} %s_hbm.3), custom_call_target="tpu_custom_call" | custom-call | tf_op jit(solution)/shard_map/coef/pallas_call | solution.py:277
  3.6 8.9 %all-gather = f32[320,640]{1,0:T(8,128)S(1)} all-gather(f32[160,640]{1,0:T(8,128)S(1)} %get-tuple-element.17), channel_id=2, replica_groups=mesh['y'=4,'zh'=4,'z1'=2,'z0'=2,'x'=4,'c'=2] {'c'}, dimensions={0}, use_global_device_ids=true | all-gather | bytes 1228800 | tf_op jit(solution)/shard_map/all_gather | solution.py:294
  12.4 0.8 %fusion = f32[128,640]{1,0:T(8,128)} fusion(f32[128,640]{1,0:T(8,128)S(1)} %get-tuple-element.16, f32[2,160,640]{2,1,0:T(8,128)S(1)} %bitcast.10, s32[]{:T(128)S(6)} %select_n.4), kind=kLoop, calls=%fused_computation.1 | loop fusion | flops 81920 | bytes 983044 | tf_op jit(solution)/shard_map/add | solution.py:296
  13.2 3.4 %all-to-all-start = ((f32[8,16,640]{2,1,0:T(8,128)}), f32[8,16,640]{2,1,0:T(8,128)S(1)}, u32[]{:S(2)}, u32[]{:S(2)}) async-start(f32[8,16,640]{2,1,0:T(8,128)} %bitcast.5._), calls=%async_computation | async-start | bytes 655360 | tf_op jit(solution)/shard_map/all_to_all | solution.py:315
  16.6 0.0 copy-start
  16.6 4.1 %order.1 = (bf16[1024,640]{1,0:T(8,128)(2,1)}, bf16[96,640]{1,0:T(8,128)(2,1)S(1)}, f32[8,128]{1,0:T(8,128)S(1)}) custom-call(s32[1]{0:T(128)} %bitcast.1.core, s32[1,1024]{1,0:T(1,128)} %bitcast.13, bf16[1024,640]{1,0:T(8,128)(2,1)} %s_hbm.3, bf16[10,32,1024]{2,1,0:T(8,128)(2,1)} %v_hbm.3, f32[2,160,640]{2,1,0:T(8,128)S(1)} %bitcast.11, f32[8,16,640]{2,1,0:T(8,128)} %bitcast.5._), custom_call_target="tpu_custom_call" | custom-call | flops 2000000000 | bytes 4000000 | tf_op jit(solution)/shard_map/order/pallas_call | solution.py:297
  20.7 2.4 %all-to-all-done.got_ref = f32[8,16,640]{2,1,0:T(8,128)S(1)} async-done(((f32[8,16,640]{2,1,0:T(8,128)}), f32[8,16,640]{2,1,0:T(8,128)S(1)}, u32[]{:S(2)}, u32[]{:S(2)}) %all-to-all-start) | async-done | bytes 327712 | tf_op jit(solution)/shard_map/all_to_all | solution.py:315
  23.1 0.7 middle.1
  23.8 13.6 %all-to-all-start.1 = ((f32[32,2,640]{2,1,0:T(2,128)}), f32[32,2,640]{2,1,0:T(2,128)S(1)}, u32[]{:S(2)}, u32[]{:S(2)}) async-start(f32[32,2,640]{2,1,0:T(2,128)} %get-tuple-element.19), calls=%async_computation.1 | async-start | bytes 327680 | tf_op jit(solution)/shard_map/all_to_all | solution.py:350
  37.4 0.0 copy-done
  37.4 5.9 %bases.1 = (bf16[1024,1024]{1,0:T(8,128)(2,1)}, bf16[1024,256]{1,0:T(8,128)(2,1)S(1)}, bf16[1024,96]{1,0:T(8,128)(2,1)S(1)}, f32[8,128]{1,0:T(8,128)S(1)}) custom-call(s32[10]{0:T(128)S(1)} %copy-done, s32[1,1024]{1,0:T(1,128)} %bitcast.14, bf16[1024,512]{1,0:T(8,128)(2,1)} %leaf_hbm.1, bf16[10,32,1024]{2,1,0:T(8,128)(2,1)} %u_hbm.1, ...), custom_call_target="tpu_custom_call" | custom-call | flops 2000000000 | bytes 4000000 | tf_op jit(solution)/shard_map/bases/pallas_call | solution.py:324
  43.3 8.3 %all-to-all-done.1.got_ref = f32[32,2,640]{2,1,0:T(2,128)S(1)} async-done(((f32[32,2,640]{2,1,0:T(2,128)}), f32[32,2,640]{2,1,0:T(2,128)S(1)}, u32[]{:S(2)}, u32[]{:S(2)}) %all-to-all-start.1) | async-done | bytes 163872 | tf_op jit(solution)/shard_map/all_to_all | solution.py:350
  51.6 0.8 %far.1._ = f32[8,16,640]{2,1,0:T(8,128)} custom-call(s32[1]{0:T(128)} %bitcast.me, f32[32,2,640]{2,1,0:T(2,128)S(1)} %all-to-all-done.1.got_ref, f32[8,16,640]{2,1,0:T(8,128)S(1)} %get-tuple-element.20._.fine_ref, f32[8,128]{1,0:T(8,128)S(1)} %get-tuple-element.21._), custom_call_target="tpu_custom_call" | custom-call | tf_op jit(solution)/shard_map/far/pallas_call | solution.py:351
  52.4 4.7 %all-to-all-start.2 = ((f32[8,16,640]{2,1,0:T(8,128)}), f32[8,16,640]{2,1,0:T(8,128)}, u32[]{:S(2)}, u32[]{:S(2)}) async-start(f32[8,16,640]{2,1,0:T(8,128)} %far.1._), calls=%async_computation.2 | async-start | bytes 655360 | tf_op jit(solution)/shard_map/all_to_all | solution.py:375
  57.0 3.8 %base.1.base_ref = f32[1024,640]{1,0:T(8,128)S(1)} custom-call(bf16[1024,640]{1,0:T(8,128)(2,1)} %get-tuple-element.23.ord_hbm, bf16[1024,1024]{1,0:T(8,128)(2,1)} %get-tuple-element.24.lp_hbm, bf16[1024,96]{1,0:T(8,128)(2,1)S(1)} %get-tuple-element.25.et_ref, bf16[96,640]{1,0:T(8,128)(2,1)S(1)} %get-tuple-element.26.fe_ref, f32[8,16,640]{2,1,0:T(8,128)} %far.1._), custom_call_target="tpu_custom_call" | custom-call | flops 2000000000 | bytes 8000000 | tf_op jit(solution)/shard_map/base/pallas_call | solution.py:360
  60.8 2.6 %all-to-all-done.2 = f32[8,16,640]{2,1,0:T(8,128)} async-done(((f32[8,16,640]{2,1,0:T(8,128)}), f32[8,16,640]{2,1,0:T(8,128)}, u32[]{:S(2)}, u32[]{:S(2)}) %all-to-all-start.2) | async-done | bytes 327712 | tf_op jit(solution)/shard_map/all_to_all | solution.py:375
  63.5 7.2 %all_gather.11.far_ref = f32[256,640]{1,0:T(8,128)S(1)} all-gather(f32[128,640]{1,0:T(8,128)} %bitcast.6), channel_id=1, replica_groups=mesh['y'=4,'zh'=4,'z1'=2,'z0'=2,'x'=4,'c'=2] {'c'}, dimensions={0}, use_global_device_ids=true | all-gather | bytes 983040 | tf_op jit(solution)/shard_map/all_gather | solution.py:376
  70.7 1.9 %last.1 = bf16[1024,640]{1,0:T(8,128)(2,1)} custom-call(f32[256,640]{1,0:T(8,128)S(1)} %all_gather.11.far_ref, bf16[1024,256]{1,0:T(8,128)(2,1)S(1)} %get-tuple-element.22.ut_ref, f32[1024,640]{1,0:T(8,128)S(1)} %base.1.base_ref), custom_call_target="tpu_custom_call" | custom-call | tf_op jit(solution)/shard_map/last/pallas_call | solution.py:377
Async XLA Ops:
  13.2 9.9 %all-to-all-start = ((f32[8,16,640]{2,1,0:T(8,128)}), f32[8,16,640]{2,1,0:T(8,128)S(1)}, u32[]{:S(2)}, u32[]{:S(2)}) async-start(f32[8,16,640]{2,1,0:T(8,128)} %bitcast.5._), calls=%async_computation | async-start | bytes 655360 | tf_op jit(solution)/shard_map/all_to_all | solution.py:315
  16.6 20.8 %copy-start = (s32[10]{0:T(128)S(1)}, s32[10]{0:T(128)}, u32[]{:S(2)}) copy-start(s32[10]{0:T(128)} %ranks.1) | copy-start | bytes 124
  23.8 27.8 %all-to-all-start.1 = ((f32[32,2,640]{2,1,0:T(2,128)}), f32[32,2,640]{2,1,0:T(2,128)S(1)}, u32[]{:S(2)}, u32[]{:S(2)}) async-start(f32[32,2,640]{2,1,0:T(2,128)} %get-tuple-element.19), calls=%async_computation.1 | async-start | bytes 327680 | tf_op jit(solution)/shard_map/all_to_all | solution.py:350
  52.4 11.1 %all-to-all-start.2 = ((f32[8,16,640]{2,1,0:T(8,128)}), f32[8,16,640]{2,1,0:T(8,128)}, u32[]{:S(2)}, u32[]{:S(2)}) async-start(f32[8,16,640]{2,1,0:T(8,128)} %far.1._), calls=%async_computation.2 | async-start | bytes 655360 | tf_op jit(solution)/shard_map/all_to_all | solution.py:375

commit v6 on v5

v6 whole, which is shorter than its diff:
```python
import jax
import jax.numpy as jnp
from jax import lax
from jax.experimental import pallas as pl
from jax.experimental.pallas import tpu as pltpu
from jax.sharding import Mesh
from jax.sharding import PartitionSpec as P

AXES = ("y", "zh", "z1", "z0", "x", "c")
OUTER = ("z0", "x")
MIDDLE = ("y", "zh", "z1")
F32 = jnp.float32
BF16 = jnp.bfloat16
NN = (((1,), (0,)), ((), ()))
NT = (((1,), (1,)), ((), ()))


def dot(a, b, dims=NN):
    return lax.dot_general(a, b, dims, preferred_element_type=F32)


def one_hot_t(perm, first, count):
    n = perm.shape[1]
    j = lax.broadcasted_iota(jnp.int32, (count, n), 0) + first
    return jnp.where(j == perm, 1.0, 0.0).astype(BF16)


def coef_kernel(core, perm_hbm, v_hbm, s_hbm, mine_ref, send_ref, acc, perm_ref, v_ref, s_ref, perm_sem, v_sem, s_sem):
    n = s_ref.shape[0]
    levels, rank, _ = v_ref.shape
    step = 256
    perm_copy = pltpu.make_async_copy(perm_hbm, perm_ref, perm_sem)
    perm_copy.start()
    v_copy = pltpu.make_async_copy(v_hbm.at[0:levels], v_ref, v_sem)
    v_copy.start()

    def s_copy(k):
        rows = pl.ds(pl.multiple_of(k * step, step), step)
        return pltpu.make_async_copy(s_hbm.at[rows], s_ref.at[rows], s_sem.at[k])

    def start(k, _):
        s_copy(k).start()
        return 0

    lax.fori_loop(0, n // step, start, 0)
    perm_copy.wait()
    perm = perm_ref[...] & (n - 1)
    v_copy.wait()
    v = v_ref[...].reshape(levels * rank, n)
    vp = [dot(v, one_hot_t(perm, j, step), NT).astype(BF16) for j in range(0, n, step)]
    for k in range(n // step):
        s_copy(k).wait()
    total = dot(jnp.concatenate(vp, axis=1), s_ref[...])
    half = 4 * rank
    me = core[0]
    mine = pl.ds(pl.multiple_of(me * half, half), half)
    theirs = pl.ds(pl.multiple_of((1 - me) * half, half), half)
    for d in range(acc.shape[0]):
        lanes = slice(d * 128, (d + 1) * 128)
        for level in range(8):
            acc[d, pl.ds(level, rank, stride=8), :] = total[level * rank : (level + 1) * rank, lanes]
        mine_ref[:, lanes] = acc[d, mine, :]
        send_ref[0:half, lanes] = acc[d, theirs, :]
    send_ref[half : half + rank, :] = total[8 * rank : 9 * rank]


def add_kernel(core, _, mine_ref, pair_ref, out_ref):
    half = mine_ref.shape[0]
    out_ref[...] = mine_ref[...] + pair_ref[1 - core[0], 0:half, :]


def local_kernel(
    ranks, core, perm_hbm, s_hbm, leaf_hbm, u_hbm, v_hbm, pair_ref, _,
    top_ref, low_hbm, ut_ref, token_ref,
    perm_ref, s_ref, leaf_ref, u_ref, v_ref, ord_ref, uf_ref, us_ref, ue_ref, fe_ref, low_ref, sems, s_sem, leaf_sem, low_sem,
):
    n, leaf = leaf_ref.shape
    rank = v_ref.shape[0]
    step = 256
    pairs = ((perm_hbm, perm_ref), (u_hbm, u_ref), (v_hbm.at[9], v_ref))
    copies = [pltpu.make_async_copy(a, b, sems.at[k]) for k, (a, b) in enumerate(pairs)]
    for copy in copies:
        copy.start()

    def tall_copies(k):
        rows = pl.ds(pl.multiple_of(k * step, step), step)
        return (
            pltpu.make_async_copy(s_hbm.at[rows], s_ref.at[rows], s_sem.at[k]),
            pltpu.make_async_copy(leaf_hbm.at[rows], leaf_ref.at[rows], leaf_sem.at[k]),
        )

    def start(k, _):
        for copy in tall_copies(k):
            copy.start()
        return 0

    lax.fori_loop(0, n // step, start, 0)
    copies[0].wait()
    perm = perm_ref[...] & (n - 1)
    copies[1].wait()
    row = lax.broadcasted_iota(jnp.int32, (rank, n), 0)
    lane_n = lax.broadcasted_iota(jnp.int32, (rank, n), 1)
    for level in range(8):
        kept = jnp.where(row < ranks[level], u_ref[level].astype(F32), 0.0)
        for d in range(n // 128):
            uf_ref[d, pl.ds(level, rank, stride=8), :] = kept[:, d * 128 : (d + 1) * 128]
    for d in range(n // 128):
        us_ref[:, d * 128 : (d + 1) * 128] = uf_ref[d].astype(BF16)
    ue_ref[0:rank, :] = jnp.where(row < ranks[8], u_ref[8].astype(F32), 0.0).astype(BF16)
    last = jnp.where(row < ranks[9], u_ref[9].astype(F32), 0.0)
    ue_ref[rank : 2 * rank, :] = jnp.where(lane_n < leaf, last, 0.0).astype(BF16)
    ue_ref[2 * rank : 3 * rank, :] = jnp.where(lane_n < leaf, 0.0, last).astype(BF16)

    copies[2].wait()
    for k in range(n // step):
        for copy in tall_copies(k):
            copy.wait()
    lane = lax.broadcasted_iota(jnp.int32, (128, 128), 1)
    for i in range(0, n, step):
        hot = []
        for h in range(i, i + step, 128):
            column = jnp.broadcast_to(perm[:, h : h + 128], (128, 128)).T
            hot.append(
                jnp.concatenate(
                    [jnp.where(column == lane + j, 1.0, 0.0).astype(BF16) for j in range(0, n, 128)], axis=1
                )
            )
        ord_ref[i : i + step, :] = dot(jnp.concatenate(hot, axis=0), s_ref[...]).astype(BF16)
    fe_ref[0:rank, :] = pair_ref[1 - core[0], 4 * rank :, :].astype(BF16)
    fe_ref[rank : 2 * rank, :] = dot(v_ref[:, leaf:], ord_ref[leaf:, :]).astype(BF16)
    fe_ref[2 * rank : 3 * rank, :] = dot(v_ref[:, :leaf], ord_ref[:leaf, :]).astype(BF16)
    top = top_ref.shape[0]
    kept = []
    for j in [*range(top, n, step), *range(0, top, step)]:
        rows = slice(j, j + step)
        hot = one_hot_t(perm, j, step)
        leaves = [dot(hot[:, g : g + leaf], leaf_ref[g : g + leaf, :]).astype(BF16) for g in range(0, n, leaf)]
        ut_ref[rows, :] = dot(hot, us_ref[...], NT).astype(BF16)
        et = dot(hot, ue_ref[...], NT).astype(BF16)
        base = dot(jnp.concatenate(leaves, axis=1), ord_ref[...]) + dot(et, fe_ref[...])
        if j < top:
            top_ref[rows, :] = base
        else:
            part = slice(j - top, j - top + step)
            low_ref[part, :] = base
            kept.append(pltpu.make_async_copy(low_ref.at[part], low_hbm.at[part], low_sem.at[len(kept)]))
            kept[-1].start()
    token_ref[...] = jnp.zeros_like(token_ref)
    for copy in kept:
        copy.wait()


def level_at(apart):
    for bit, row in ((16, 0), (8, 1), (4, 2), (2, 3)):
        if apart & bit:
            return row
    return 4


def middle_kernel(me, got_ref, out_ref, fine_ref, token_ref):
    token_ref[...] = jnp.zeros_like(token_ref)
    rows = got_ref.shape[1]
    got = lambda z, x: got_ref[z * 4 + x]
    sums = [(got(z, 0) + got(z, 1)) + (got(z, 2) + got(z, 3)) for z in range(2)]
    total = sums[0] + sums[1]
    for z in range(2):
        for x in range(4):
            for j in range(rows // 8):
                at = lambda a, row: a[j * 8 + row : j * 8 + row + 1]
                fine_ref[z * 4 + x, j * 4 : j * 4 + 1, :] = at(sums[z ^ 1], 5)
                fine_ref[z * 4 + x, j * 4 + 1 : j * 4 + 2, :] = at(got(z, x ^ 2), 6) + at(got(z, x ^ 3), 6)
                fine_ref[z * 4 + x, j * 4 + 2 : j * 4 + 3, :] = at(got(z, x ^ 1), 7)
    for row in range(5):
        sent = jnp.concatenate([total[r + row : r + row + 1] for r in range(0, rows, 8)], axis=0)
        for apart in range(out_ref.shape[0]):
            if level_at(apart) == row:
                out_ref[me[0] ^ apart] = sent


def far_kernel(me, got_ref, fine_ref, _, out_ref, acc):
    rows = acc.shape[0]
    acc[...] = jnp.zeros_like(acc)
    for row in range(5):
        parts = [got_ref[me[0] ^ k] for k in range(1, got_ref.shape[0]) if level_at(k) == row]
        while len(parts) > 1:
            parts = [sum(parts[k : k + 2]) for k in range(0, len(parts), 2)]
        for j in range(rows // 8):
            acc[j * 8 + row : j * 8 + row + 1, :] = parts[0][j : j + 1]
    far = acc[...]
    for p in range(out_ref.shape[0]):
        out_ref[p] = far
        for j in range(rows // 8):
            out_ref[p, j * 8 + 5 : j * 8 + 8, :] = fine_ref[p, j * 4 : j * 4 + 3, :]


def last_kernel(far_ref, ut_ref, top_ref, low_hbm, out_hbm, low_ref, out_ref, low_sem, sems):
    n, step = out_ref.shape[0], 128
    top = top_ref.shape[0]
    low_copies = []
    for k in range((n - top) // step):
        part = slice(k * step, (k + 1) * step)
        low_copies.append(pltpu.make_async_copy(low_hbm.at[part], low_ref.at[part], low_sem.at[k]))
        low_copies[k].start()
    far = far_ref[...].astype(BF16)
    copies = []
    for b in range(n // step):
        rows = slice(b * step, (b + 1) * step)
        if b * step >= top:
            low_copies[b - top // step].wait()
        base = top_ref[rows, :] if b * step < top else low_ref[b * step - top : (b + 1) * step - top, :]
        out_ref[rows, :] = (base + dot(ut_ref[rows, :], far)).astype(BF16)
        copies.append(pltpu.make_async_copy(out_ref.at[rows], out_hbm.at[rows], sems.at[b]))
        copies[-1].start()
    for copy in copies:
        copy.wait()


SMEM = pl.BlockSpec(memory_space=pltpu.SMEM)
VMEM = pl.BlockSpec(memory_space=pltpu.VMEM)
ANY = pl.BlockSpec(memory_space=pl.ANY)
HBM = pl.BlockSpec(memory_space=pltpu.HBM)


def grant(mib):
    return pltpu.CompilerParams(vmem_limit_bytes=mib << 20)


def in_hbm(*arrays):
    return [pltpu.with_memory_space_constraint(a, pltpu.HBM) for a in arrays]


def in_vmem(*arrays):
    return [pltpu.with_memory_space_constraint(a, pltpu.VMEM) for a in arrays]


def shape(dims, dtype=F32):
    return jax.ShapeDtypeStruct(dims, dtype)


def per_device(sources, tree_perm, leaf_blocks, u_factors, v_factors, level_ranks):
    n, rhs = sources.shape
    rank = u_factors.shape[1]
    half = 4 * rank
    low_rows = 512
    core = lax.axis_index("c").reshape(1)
    me = lax.axis_index(MIDDLE).reshape(1)
    perm = tree_perm.reshape(1, n)
    mine, send = pl.pallas_call(
        coef_kernel,
        name="coef",
        in_specs=[SMEM, HBM, HBM, HBM],
        out_specs=[VMEM, VMEM],
        out_shape=[shape((half, rhs)), shape((half + rank, rhs))],
        scratch_shapes=[
            pltpu.VMEM((rhs // 128, 2 * half, 128), F32),
            pltpu.VMEM((1, n), jnp.int32),
            pltpu.VMEM((9, rank, n), BF16),
            pltpu.VMEM((n, rhs), BF16),
            pltpu.SemaphoreType.DMA,
            pltpu.SemaphoreType.DMA,
            pltpu.SemaphoreType.DMA((n // 256,)),
        ],
        compiler_params=grant(14),
    )(core, *in_hbm(perm, v_factors, sources))
    pair = lax.all_gather(send, "c")
    partial = pl.pallas_call(
        add_kernel,
        name="add",
        in_specs=[SMEM, SMEM, VMEM, VMEM],
        out_specs=VMEM,
        out_shape=pltpu.VMEM((half, rhs), F32),
        compiler_params=grant(4),
    )(core, me, *in_vmem(mine, pair)).reshape(8, 16, rhs)
    got = lax.all_to_all(partial, OUTER, 0, 0, tiled=True)
    rows, fine, token = pl.pallas_call(
        middle_kernel,
        name="middle",
        in_specs=[SMEM, VMEM],
        out_specs=[VMEM] * 3,
        out_shape=[shape((32, 2, rhs)), pltpu.VMEM((8, 8, rhs), F32), shape((8, 128))],
        compiler_params=grant(4),
    )(me, got)
    top, low, ut, token = pl.pallas_call(
        local_kernel,
        name="local",
        in_specs=[SMEM, SMEM] + [HBM] * 5 + [VMEM, ANY],
        out_specs=[VMEM, HBM, VMEM, VMEM],
        out_shape=[
            pltpu.VMEM((n - low_rows, rhs), F32),
            pltpu.HBM((low_rows, rhs), F32),
            pltpu.VMEM((n, 2 * half), BF16),
            shape((8, 128)),
        ],
        scratch_shapes=[
            pltpu.VMEM((1, n), jnp.int32),
            pltpu.VMEM((n, rhs), BF16),
            pltpu.VMEM(leaf_blocks.shape, BF16),
            pltpu.VMEM(u_factors.shape, BF16),
            pltpu.VMEM((rank, n), BF16),
            pltpu.VMEM((n, rhs), BF16),
            pltpu.VMEM((n // 128, 2 * half, 128), F32),
            pltpu.VMEM((2 * half, n), BF16),
            pltpu.VMEM((3 * rank, n), BF16),
            pltpu.VMEM((3 * rank, rhs), BF16),
            pltpu.VMEM((low_rows, rhs), F32),
            pltpu.SemaphoreType.DMA((3,)),
            pltpu.SemaphoreType.DMA((n // 256,)),
            pltpu.SemaphoreType.DMA((n // 256,)),
            pltpu.SemaphoreType.DMA((low_rows // 256,)),
        ],
        compiler_params=grant(12),
        cost_estimate=pl.CostEstimate(flops=4_700_000_000, bytes_accessed=8_000_000, transcendentals=0),
    )(level_ranks, core, *in_hbm(perm, sources, leaf_blocks, u_factors, v_factors), *in_vmem(pair), token)
    rows = lax.all_to_all(rows, MIDDLE, 0, 0, tiled=True)
    far = pl.pallas_call(
        far_kernel,
        name="far",
        in_specs=[SMEM, VMEM, VMEM, ANY],
        out_specs=VMEM,
        out_shape=shape((8, 16, rhs)),
        scratch_shapes=[pltpu.VMEM((16, rhs), F32)],
        compiler_params=grant(4),
    )(me, rows, *in_vmem(fine), token)
    far = lax.all_to_all(far, OUTER, 0, 0, tiled=True)
    far = lax.all_gather(far.reshape(half, rhs), "c", axis=0, tiled=True)
    return pl.pallas_call(
        last_kernel,
        name="last",
        in_specs=[VMEM, VMEM, VMEM, HBM],
        out_specs=HBM,
        out_shape=pltpu.HBM((n, rhs), BF16),
        scratch_shapes=[
            pltpu.VMEM((low_rows, rhs), F32),
            pltpu.VMEM((n, rhs), BF16),
            pltpu.SemaphoreType.DMA((low_rows // 128,)),
            pltpu.SemaphoreType.DMA((n // 128,)),
        ],
        compiler_params=grant(8),
    )(*in_vmem(far, ut, top), *in_hbm(low))


def solution(mesh):
    torus = Mesh(mesh.devices.reshape(4, 4, 2, 2, 4, 2), AXES)
    placed = (P(AXES, None), P(AXES), P(AXES, None), P(None, None, AXES), P(None, None, AXES), P())
    return jax.shard_map(
        per_device, mesh=torus, in_specs=placed, out_specs=P(AXES, None), check_vma=False
    )
```

time: 73 us -> 70.7 us (0.968)
  blocking collectives: 16.1 us -> 35.4 us
  waiting for transfers between devices: 13.3 us -> 5.04 us
  starting transfers between devices: 21.7 us -> 14.2 us
  Pallas kernels: 20.7 us -> 15.7 us
  other arithmetic: 0.76 us -> 0 us
    all_to_all x0 -> x2, blocking collectives: none -> 19.2 us  [the longest x1 9.93 us: per_device(): got = lax.all_to_all(partial, OUTER, 0, 0, tiled=True)]
    all_to_all x2 -> x0, starting transfers between devices: 8.12 us -> none  [the longest x1 4.69 us: per_device(): far = lax.all_to_all(far, OUTER, 0, 0, tiled=True)]
    all_to_all x2 -> x0, waiting for transfers between devices: 5.02 us -> none  [the longest x1 2.65 us: per_device(): far = lax.all_to_all(far, OUTER, 0, 0, tiled=True)]
    pallas_call x5 -> x4, Pallas kernels: 16.3 us -> 12.7 us  [the longest x1 9.15 us: per_device(): pl.pallas_call(local_kernel, name='local', in_specs=[SMEM, SMEM] + [HBM]...]
    all_to_all x1, waiting for transfers between devices: 8.28 us -> 5.04 us  [per_device(): rows = lax.all_to_all(rows, MIDDLE, 0, 0, tiled=True)]
    add x1 -> x0, other arithmetic: 0.76 us -> none  [per_device(): partial = (mine + other[:half]).reshape(8, 16, rhs)]
  transfers between devices with their start and end apart: 3 -> 1, of which waited for: 3 -> 1; matrix products, arithmetic and copies ran while one was open for 0% -> 0% of each run, Pallas kernels for 19% -> 13%
where the time goes in v6:
time: 70.7 us; the launch traced here: 70.4 us
  blocking collectives  35.4 us (50%)
  Pallas kernels  15.7 us (22%)
  starting transfers between devices  14.2 us (20%)
  waiting for transfers between devices  5.04 us (7%)
    all_to_all x1, starting transfers between devices, per_device(): rows = lax.all_to_all(rows, MIDDLE, 0, 0, tiled=True)  14.2 us
    all_to_all x1, blocking collectives, per_device(): got = lax.all_to_all(partial, OUTER, 0, 0, tiled=True)  9.93 us
    all_to_all x1, blocking collectives, per_device(): far = lax.all_to_all(far, OUTER, 0, 0, tiled=True)  9.26 us
    pallas_call x1, Pallas kernels, per_device(): pl.pallas_call(local_kernel, name='local', in_specs=[SMEM, SMEM] + [HBM]...  9.15 us
    all_gather x1, blocking collectives, per_device(): pair = lax.all_gather(send, 'c')  8.86 us
    all_gather x1, blocking collectives, per_device(): far = lax.all_gather(far.reshape(half, rhs), 'c', axis=0, tiled=True)  7.38 us
    all_to_all x1, waiting for transfers between devices, per_device(): rows = lax.all_to_all(rows, MIDDLE, 0, 0, tiled=True)  5.04 us
    pallas_call x1, Pallas kernels, per_device(): pl.pallas_call(coef_kernel, name='coef', in_specs=[SMEM, HBM, HBM, HBM],...  2.97 us
  transfers between devices with their start and end apart: 1, of which 1 were waited for; matrix products, arithmetic and copies ran while one was open for 0% of the time, Pallas kernels for 13%

profile of v6, /device:TPU:1, one launch (start us, length us, event | category | flops | bytes accessed | tf_op | source)
XLA Modules:
  0.0 70.4 jit_solution(13494532419876039282)
XLA Ops:
  0.0 3.0 %coef.1 = (f32[128,640]{1,0:T(8,128)S(1)}, f32[160,640]{1,0:T(8,128)S(1)}) custom-call(s32[1]{0:T(128)} %bitcast.1.core, s32[1,1024]{1,0:T(1,128)} %bitcast.10, bf16[10,32,1024]{2,1,0:T(8,128)(2,1)} %v_hbm.3, bf16[1024,640]{1,0:T(8,128)(2,1)} %s_hbm.3), custom_call_target="tpu_custom_call" | custom-call | tf_op jit(solution)/shard_map/coef/pallas_call | solution.py:248
  3.0 8.9 %all-gather = f32[320,640]{1,0:T(8,128)S(1)} all-gather(f32[160,640]{1,0:T(8,128)S(1)} %get-tuple-element.15), channel_id=2, replica_groups=mesh['y'=4,'zh'=4,'z1'=2,'z0'=2,'x'=4,'c'=2] {'c'}, dimensions={0}, use_global_device_ids=true | all-gather | bytes 1228800 | tf_op jit(solution)/shard_map/all_gather | solution.py:265
  11.8 0.0 copy-start
  11.9 9.9 %all_to_all.15.got_ref = f32[8,16,640]{2,1,0:T(8,128)S(1)} all-to-all(f32[8,16,640]{2,1,0:T(8,128)S(1)} %bitcast.8), channel_id=1, replica_groups=mesh['y'=4,'zh'=4,'z1'=2,'z0'=2,'x'=4,'c'=2] {'z0','x'}, dimensions={0} | all-to-all | bytes 655360 | tf_op jit(solution)/shard_map/all_to_all | solution.py:274
  21.8 0.7 %middle.1 = (f32[32,2,640]{2,1,0:T(2,128)}, f32[8,8,640]{2,1,0:T(8,128)S(1)}, f32[8,128]{1,0:T(8,128)S(1)}) custom-call(s32[1]{0:T(128)} %bitcast._.me, f32[8,16,640]{2,1,0:T(8,128)S(1)} %all_to_all.15.got_ref), custom_call_target="tpu_custom_call" | custom-call | tf_op jit(solution)/shard_map/middle/pallas_call | solution.py:275
  22.5 14.2 %all-to-all-start.1 = ((f32[32,2,640]{2,1,0:T(2,128)}), f32[32,2,640]{2,1,0:T(2,128)S(1)}, u32[]{:S(2)}, u32[]{:S(2)}) async-start(f32[32,2,640]{2,1,0:T(2,128)} %get-tuple-element.16), calls=%async_computation.1 | async-start | bytes 327680 | tf_op jit(solution)/shard_map/all_to_all | solution.py:314
  36.7 0.0 copy-done
  36.7 9.2 %local.1 = (f32[512,640]{1,0:T(8,128)S(1)}, f32[512,640]{1,0:T(8,128)}, bf16[1024,256]{1,0:T(8,128)(2,1)S(1)}, f32[8,128]{1,0:T(8,128)S(1)}) custom-call(s32[10]{0:T(128)S(1)} %copy-done, s32[1]{0:T(128)} %bitcast.1.core, s32[1,1024]{1,0:T(1,128)} %bitcast.11, bf16[1024,640]{1,0:T(8,128)(2,1)} %s_hbm.3, bf16[1024,512]{1,0:T(8,128)(2,1)} %leaf_hbm.1, ...), custom_call_target="tpu_custom_call" | custom-call | flops 4700000256 | bytes 8000000 | tf_op jit(solution)/shard_map/local/pallas_call | solution.py:283
  45.9 5.0 %all-to-all-done.1.got_ref = f32[32,2,640]{2,1,0:T(2,128)S(1)} async-done(((f32[32,2,640]{2,1,0:T(2,128)}), f32[32,2,640]{2,1,0:T(2,128)S(1)}, u32[]{:S(2)}, u32[]{:S(2)}) %all-to-all-start.1) | async-done | bytes 163872 | tf_op jit(solution)/shard_map/all_to_all | solution.py:314
  50.9 0.1 far.1
  51.0 9.3 %all_to_all.16 = f32[8,16,640]{2,1,0:T(8,128)S(1)} all-to-all(f32[8,16,640]{2,1,0:T(8,128)S(1)} %far.1), channel_id=1, replica_groups=mesh['y'=4,'zh'=4,'z1'=2,'z0'=2,'x'=4,'c'=2] {'z0','x'}, dimensions={0} | all-to-all | bytes 655360 | tf_op jit(solution)/shard_map/all_to_all | solution.py:324
  60.3 7.4 %all_gather.11.far_ref = f32[256,640]{1,0:T(8,128)S(1)} all-gather(f32[128,640]{1,0:T(8,128)S(1)} %bitcast.9), channel_id=1, replica_groups=mesh['y'=4,'zh'=4,'z1'=2,'z0'=2,'x'=4,'c'=2] {'c'}, dimensions={0}, use_global_device_ids=true | all-gather | bytes 983040 | tf_op jit(solution)/shard_map/all_gather | solution.py:325
  67.7 2.7 %last.1 = bf16[1024,640]{1,0:T(8,128)(2,1)} custom-call(f32[256,640]{1,0:T(8,128)S(1)} %all_gather.11.far_ref, bf16[1024,256]{1,0:T(8,128)(2,1)S(1)} %get-tuple-element.20.ut_ref, f32[512,640]{1,0:T(8,128)S(1)} %get-tuple-element.21.top_ref, f32[512,640]{1,0:T(8,128)} %get-tuple-element.22.low_hbm), custom_call_target="tpu_custom_call" | custom-call | tf_op jit(solution)/shard_map/last/pallas_call | solution.py:326
  (1 shorter events, 0.0 us)
Async XLA Ops:
  11.8 24.9 %copy-start = (s32[10]{0:T(128)S(1)}, s32[10]{0:T(128)}, u32[]{:S(2)}) copy-start(s32[10]{0:T(128)} %ranks.1) | copy-start | bytes 124
  22.5 28.4 %all-to-all-start.1 = ((f32[32,2,640]{2,1,0:T(2,128)}), f32[32,2,640]{2,1,0:T(2,128)S(1)}, u32[]{:S(2)}, u32[]{:S(2)}) async-start(f32[32,2,640]{2,1,0:T(2,128)} %get-tuple-element.16), calls=%async_computation.1 | async-start | bytes 327680 | tf_op jit(solution)/shard_map/all_to_all | solution.py:314

commit v7 on v6

--- a/solution.py
+++ b/solution.py
@@ -193,20 +193,13 @@
             out_ref[p, j * 8 + 5 : j * 8 + 8, :] = fine_ref[p, j * 4 : j * 4 + 3, :]
 
 
-def last_kernel(far_ref, ut_ref, top_ref, low_hbm, out_hbm, low_ref, out_ref, low_sem, sems):
+def last_kernel(far_ref, ut_ref, top_ref, low_ref, out_hbm, out_ref, sems):
     n, step = out_ref.shape[0], 128
     top = top_ref.shape[0]
-    low_copies = []
-    for k in range((n - top) // step):
-        part = slice(k * step, (k + 1) * step)
-        low_copies.append(pltpu.make_async_copy(low_hbm.at[part], low_ref.at[part], low_sem.at[k]))
-        low_copies[k].start()
     far = far_ref[...].astype(BF16)
     copies = []
     for b in range(n // step):
         rows = slice(b * step, (b + 1) * step)
-        if b * step >= top:
-            low_copies[b - top // step].wait()
         base = top_ref[rows, :] if b * step < top else low_ref[b * step - top : (b + 1) * step - top, :]
         out_ref[rows, :] = (base + dot(ut_ref[rows, :], far)).astype(BF16)
         copies.append(pltpu.make_async_copy(out_ref.at[rows], out_hbm.at[rows], sems.at[b]))
@@ -241,7 +234,7 @@
     n, rhs = sources.shape
     rank = u_factors.shape[1]
     half = 4 * rank
-    low_rows = 512
+    low_rows = 768
     core = lax.axis_index("c").reshape(1)
     me = lax.axis_index(MIDDLE).reshape(1)
     perm = tree_perm.reshape(1, n)
@@ -326,17 +319,15 @@
     return pl.pallas_call(
         last_kernel,
         name="last",
-        in_specs=[VMEM, VMEM, VMEM, HBM],
+        in_specs=[VMEM] * 4,
         out_specs=HBM,
         out_shape=pltpu.HBM((n, rhs), BF16),
         scratch_shapes=[
-            pltpu.VMEM((low_rows, rhs), F32),
             pltpu.VMEM((n, rhs), BF16),
-            pltpu.SemaphoreType.DMA((low_rows // 128,)),
             pltpu.SemaphoreType.DMA((n // 128,)),
         ],
         compiler_params=grant(8),
-    )(*in_vmem(far, ut, top), *in_hbm(low))
+    )(*in_vmem(far, ut, top, low))
 
 
 def solution(mesh):

time: 70.7 us -> 69.3 us (0.980)
  Pallas kernels: 15.7 us -> 14.3 us
    pallas_call x1, Pallas kernels: 2.74 us -> 1.35 us  [per_device(): pl.pallas_call(last_kernel, name='last', in_specs=[VMEM] * 4, out_specs=H...]
where the time goes in v7:
time: 69.3 us; the launch traced here: 69 us
  blocking collectives  35.4 us (51%)
  Pallas kernels  14.3 us (21%)
  starting transfers between devices  14.2 us (20%)
  waiting for transfers between devices  5.02 us (7%)
    all_to_all x1, starting transfers between devices, per_device(): rows = lax.all_to_all(rows, MIDDLE, 0, 0, tiled=True)  14.2 us
    all_to_all x1, blocking collectives, per_device(): got = lax.all_to_all(partial, OUTER, 0, 0, tiled=True)  9.93 us
    all_to_all x1, blocking collectives, per_device(): far = lax.all_to_all(far, OUTER, 0, 0, tiled=True)  9.26 us
    pallas_call x1, Pallas kernels, per_device(): pl.pallas_call(local_kernel, name='local', in_specs=[SMEM, SMEM] + [HBM]...  9.16 us
    all_gather x1, blocking collectives, per_device(): pair = lax.all_gather(send, 'c')  8.86 us
    all_gather x1, blocking collectives, per_device(): far = lax.all_gather(far.reshape(half, rhs), 'c', axis=0, tiled=True)  7.38 us
    all_to_all x1, waiting for transfers between devices, per_device(): rows = lax.all_to_all(rows, MIDDLE, 0, 0, tiled=True)  5.02 us
    pallas_call x1, Pallas kernels, per_device(): pl.pallas_call(coef_kernel, name='coef', in_specs=[SMEM, HBM, HBM, HBM],...  2.97 us
  transfers between devices with their start and end apart: 1, of which 1 were waited for; matrix products, arithmetic and copies ran while one was open for 0% of the time, Pallas kernels for 13%

profile of v7, /device:TPU:1, one launch (start us, length us, event | category | flops | bytes accessed | tf_op | source)
XLA Modules:
  0.0 69.0 jit_solution(4956693992693983509)
XLA Ops:
  0.0 3.0 %coef.1 = (f32[128,640]{1,0:T(8,128)S(1)}, f32[160,640]{1,0:T(8,128)S(1)}) custom-call(s32[1]{0:T(128)} %bitcast.1.core, s32[1,1024]{1,0:T(1,128)} %bitcast.10, bf16[10,32,1024]{2,1,0:T(8,128)(2,1)} %v_hbm.3, bf16[1024,640]{1,0:T(8,128)(2,1)} %s_hbm.3), custom_call_target="tpu_custom_call" | custom-call | tf_op jit(solution)/shard_map/coef/pallas_call | solution.py:241
  3.0 8.9 %all-gather = f32[320,640]{1,0:T(8,128)S(1)} all-gather(f32[160,640]{1,0:T(8,128)S(1)} %get-tuple-element.15), channel_id=2, replica_groups=mesh['y'=4,'zh'=4,'z1'=2,'z0'=2,'x'=4,'c'=2] {'c'}, dimensions={0}, use_global_device_ids=true | all-gather | bytes 1228800 | tf_op jit(solution)/shard_map/all_gather | solution.py:258
  11.8 0.0 copy-start.1
  11.9 9.9 %all_to_all.15.got_ref = f32[8,16,640]{2,1,0:T(8,128)S(1)} all-to-all(f32[8,16,640]{2,1,0:T(8,128)S(1)} %bitcast.8), channel_id=1, replica_groups=mesh['y'=4,'zh'=4,'z1'=2,'z0'=2,'x'=4,'c'=2] {'z0','x'}, dimensions={0} | all-to-all | bytes 655360 | tf_op jit(solution)/shard_map/all_to_all | solution.py:267
  21.8 0.7 %middle.1 = (f32[32,2,640]{2,1,0:T(2,128)}, f32[8,8,640]{2,1,0:T(8,128)S(1)}, f32[8,128]{1,0:T(8,128)S(1)}) custom-call(s32[1]{0:T(128)} %bitcast._.me, f32[8,16,640]{2,1,0:T(8,128)S(1)} %all_to_all.15.got_ref), custom_call_target="tpu_custom_call" | custom-call | tf_op jit(solution)/shard_map/middle/pallas_call | solution.py:268
  22.5 14.2 %all-to-all-start.1 = ((f32[32,2,640]{2,1,0:T(2,128)}), f32[32,2,640]{2,1,0:T(2,128)S(1)}, u32[]{:S(2)}, u32[]{:S(2)}) async-start(f32[32,2,640]{2,1,0:T(2,128)} %get-tuple-element.16), calls=%async_computation.1 | async-start | bytes 327680 | tf_op jit(solution)/shard_map/all_to_all | solution.py:307
  36.7 0.0 copy-done.1
  36.7 9.2 %local.1 = (f32[256,640]{1,0:T(8,128)S(1)}, f32[768,640]{1,0:T(8,128)}, bf16[1024,256]{1,0:T(8,128)(2,1)S(1)}, f32[8,128]{1,0:T(8,128)S(1)}) custom-call(s32[10]{0:T(128)S(1)} %copy-done.1, s32[1]{0:T(128)} %bitcast.1.core, s32[1,1024]{1,0:T(1,128)} %bitcast.11, bf16[1024,640]{1,0:T(8,128)(2,1)} %s_hbm.3, bf16[1024,512]{1,0:T(8,128)(2,1)} %leaf_hbm.1, ...), custom_call_target="tpu_custom_call" | custom-call | flops 4700000256 | bytes 8000000 | tf_op jit(solution)/shard_map/local/pallas_call | solution.py:276
  45.9 0.0 copy-start
  45.9 5.0 %all-to-all-done.1.got_ref = f32[32,2,640]{2,1,0:T(2,128)S(1)} async-done(((f32[32,2,640]{2,1,0:T(2,128)}), f32[32,2,640]{2,1,0:T(2,128)S(1)}, u32[]{:S(2)}, u32[]{:S(2)}) %all-to-all-start.1) | async-done | bytes 163872 | tf_op jit(solution)/shard_map/all_to_all | solution.py:307
  50.9 0.1 far.1
  51.0 9.3 %all_to_all.16 = f32[8,16,640]{2,1,0:T(8,128)S(1)} all-to-all(f32[8,16,640]{2,1,0:T(8,128)S(1)} %far.1), channel_id=1, replica_groups=mesh['y'=4,'zh'=4,'z1'=2,'z0'=2,'x'=4,'c'=2] {'z0','x'}, dimensions={0} | all-to-all | bytes 655360 | tf_op jit(solution)/shard_map/all_to_all | solution.py:317
  60.3 7.4 %all_gather.11.far_ref = f32[256,640]{1,0:T(8,128)S(1)} all-gather(f32[128,640]{1,0:T(8,128)S(1)} %bitcast.9), channel_id=1, replica_groups=mesh['y'=4,'zh'=4,'z1'=2,'z0'=2,'x'=4,'c'=2] {'c'}, dimensions={0}, use_global_device_ids=true | all-gather | bytes 983040 | tf_op jit(solution)/shard_map/all_gather | solution.py:318
  67.7 0.0 copy-done
  67.7 1.4 %last.1 = bf16[1024,640]{1,0:T(8,128)(2,1)} custom-call(f32[256,640]{1,0:T(8,128)S(1)} %all_gather.11.far_ref, bf16[1024,256]{1,0:T(8,128)(2,1)S(1)} %get-tuple-element.20.ut_ref, f32[256,640]{1,0:T(8,128)S(1)} %get-tuple-element.21.top_ref, f32[768,640]{1,0:T(8,128)S(1)} %copy-done), custom_call_target="tpu_custom_call" | custom-call | tf_op jit(solution)/shard_map/last/pallas_call | solution.py:319
  (1 shorter events, 0.0 us)
Async XLA Ops:
  11.8 24.9 %copy-start.1 = (s32[10]{0:T(128)S(1)}, s32[10]{0:T(128)}, u32[]{:S(2)}) copy-start(s32[10]{0:T(128)} %ranks.1) | copy-start | bytes 124
  22.5 28.4 %all-to-all-start.1 = ((f32[32,2,640]{2,1,0:T(2,128)}), f32[32,2,640]{2,1,0:T(2,128)S(1)}, u32[]{:S(2)}, u32[]{:S(2)}) async-start(f32[32,2,640]{2,1,0:T(2,128)} %get-tuple-element.16), calls=%async_computation.1 | async-start | bytes 327680 | tf_op jit(solution)/shard_map/all_to_all | solution.py:307
  45.9 21.8 %copy-start = (f32[768,640]{1,0:T(8,128)S(1)}, f32[768,640]{1,0:T(8,128)}, u32[]{:S(2)}) copy-start(f32[768,640]{1,0:T(8,128)} %get-tuple-element.22.low_ref) | copy-start | bytes 5898244

commit v8 on v7

--- a/solution.py
+++ b/solution.py
@@ -8,7 +8,7 @@
 
 AXES = ("y", "zh", "z1", "z0", "x", "c")
 OUTER = ("z0", "x")
-MIDDLE = ("y", "zh", "z1")
+MIDDLE = ("zh", "y", "z1")
 F32 = jnp.float32
 BF16 = jnp.bfloat16
 NN = (((1,), (0,)), ((), ()))
@@ -151,7 +151,7 @@
 
 
 def level_at(apart):
-    for bit, row in ((16, 0), (8, 1), (4, 2), (2, 3)):
+    for bit, row in ((4, 0), (2, 1), (16, 2), (8, 3)):
         if apart & bit:
             return row
     return 4

time: 69.3 us -> 69.9 us (level)
    all_to_all x1, blocking collectives: 9.26 us -> 9.99 us  [per_device(): far = lax.all_to_all(far, OUTER, 0, 0, tiled=True)]
where the time goes in v8:
time: 69.9 us; the launch traced here: 69.6 us
  blocking collectives  35.7 us (51%)
  Pallas kernels  14.3 us (20%)
  starting transfers between devices  14.2 us (20%)
  waiting for transfers between devices  5.31 us (8%)
    all_to_all x1, starting transfers between devices, per_device(): rows = lax.all_to_all(rows, MIDDLE, 0, 0, tiled=True)  14.2 us
    all_to_all x1, blocking collectives, per_device(): far = lax.all_to_all(far, OUTER, 0, 0, tiled=True)  9.99 us
    all_to_all x1, blocking collectives, per_device(): got = lax.all_to_all(partial, OUTER, 0, 0, tiled=True)  9.93 us
    pallas_call x1, Pallas kernels, per_device(): pl.pallas_call(local_kernel, name='local', in_specs=[SMEM, SMEM] + [HBM]...  9.16 us
    all_gather x1, blocking collectives, per_device(): pair = lax.all_gather(send, 'c')  8.86 us
    all_gather x1, blocking collectives, per_device(): far = lax.all_gather(far.reshape(half, rhs), 'c', axis=0, tiled=True)  6.91 us
    all_to_all x1, waiting for transfers between devices, per_device(): rows = lax.all_to_all(rows, MIDDLE, 0, 0, tiled=True)  5.31 us
    pallas_call x1, Pallas kernels, per_device(): pl.pallas_call(coef_kernel, name='coef', in_specs=[SMEM, HBM, HBM, HBM],...  2.97 us
  transfers between devices with their start and end apart: 1, of which 1 were waited for; matrix products, arithmetic and copies ran while one was open for 0% of the time, Pallas kernels for 13%

profile of v8, /device:TPU:1, one launch (start us, length us, event | category | flops | bytes accessed | tf_op | source)
XLA Modules:
  0.0 69.6 jit_solution(3455362186577058)
XLA Ops:
  0.0 3.0 %coef.1 = (f32[128,640]{1,0:T(8,128)S(1)}, f32[160,640]{1,0:T(8,128)S(1)}) custom-call(s32[1]{0:T(128)} %bitcast.1.core, s32[1,1024]{1,0:T(1,128)} %bitcast.10, bf16[10,32,1024]{2,1,0:T(8,128)(2,1)} %v_hbm.3, bf16[1024,640]{1,0:T(8,128)(2,1)} %s_hbm.3), custom_call_target="tpu_custom_call" | custom-call | tf_op jit(solution)/shard_map/coef/pallas_call | solution.py:241
  3.0 8.9 %all-gather = f32[320,640]{1,0:T(8,128)S(1)} all-gather(f32[160,640]{1,0:T(8,128)S(1)} %get-tuple-element.15), channel_id=2, replica_groups=mesh['y'=4,'zh'=4,'z1'=2,'z0'=2,'x'=4,'c'=2] {'c'}, dimensions={0}, use_global_device_ids=true | all-gather | bytes 1228800 | tf_op jit(solution)/shard_map/all_gather | solution.py:258
  11.8 0.0 copy-start.1
  11.9 9.9 %all_to_all.15.got_ref = f32[8,16,640]{2,1,0:T(8,128)S(1)} all-to-all(f32[8,16,640]{2,1,0:T(8,128)S(1)} %bitcast.8), channel_id=1, replica_groups=mesh['y'=4,'zh'=4,'z1'=2,'z0'=2,'x'=4,'c'=2] {'z0','x'}, dimensions={0} | all-to-all | bytes 655360 | tf_op jit(solution)/shard_map/all_to_all | solution.py:267
  21.8 0.7 %middle.1 = (f32[32,2,640]{2,1,0:T(2,128)}, f32[8,8,640]{2,1,0:T(8,128)S(1)}, f32[8,128]{1,0:T(8,128)S(1)}) custom-call(s32[1]{0:T(128)} %bitcast._.me, f32[8,16,640]{2,1,0:T(8,128)S(1)} %all_to_all.15.got_ref), custom_call_target="tpu_custom_call" | custom-call | tf_op jit(solution)/shard_map/middle/pallas_call | solution.py:268
  22.5 14.2 %all-to-all-start.1 = ((f32[32,2,640]{2,1,0:T(2,128)}), f32[32,2,640]{2,1,0:T(2,128)S(1)}, u32[]{:S(2)}, u32[]{:S(2)}) async-start(f32[32,2,640]{2,1,0:T(2,128)} %get-tuple-element.16), calls=%async_computation.1 | async-start | bytes 327680 | tf_op jit(solution)/shard_map/all_to_all | solution.py:307
  36.7 0.0 copy-done.1
  36.7 9.2 %local.1 = (f32[256,640]{1,0:T(8,128)S(1)}, f32[768,640]{1,0:T(8,128)}, bf16[1024,256]{1,0:T(8,128)(2,1)S(1)}, f32[8,128]{1,0:T(8,128)S(1)}) custom-call(s32[10]{0:T(128)S(1)} %copy-done.1, s32[1]{0:T(128)} %bitcast.1.core, s32[1,1024]{1,0:T(1,128)} %bitcast.11, bf16[1024,640]{1,0:T(8,128)(2,1)} %s_hbm.3, bf16[1024,512]{1,0:T(8,128)(2,1)} %leaf_hbm.1, ...), custom_call_target="tpu_custom_call" | custom-call | flops 4700000256 | bytes 8000000 | tf_op jit(solution)/shard_map/local/pallas_call | solution.py:276
  45.9 0.0 copy-start
  45.9 5.3 %all-to-all-done.1.got_ref = f32[32,2,640]{2,1,0:T(2,128)S(1)} async-done(((f32[32,2,640]{2,1,0:T(2,128)}), f32[32,2,640]{2,1,0:T(2,128)S(1)}, u32[]{:S(2)}, u32[]{:S(2)}) %all-to-all-start.1) | async-done | bytes 163872 | tf_op jit(solution)/shard_map/all_to_all | solution.py:307
  51.2 0.1 far.1
  51.3 10.0 %all_to_all.16 = f32[8,16,640]{2,1,0:T(8,128)S(1)} all-to-all(f32[8,16,640]{2,1,0:T(8,128)S(1)} %far.1), channel_id=1, replica_groups=mesh['y'=4,'zh'=4,'z1'=2,'z0'=2,'x'=4,'c'=2] {'z0','x'}, dimensions={0} | all-to-all | bytes 655360 | tf_op jit(solution)/shard_map/all_to_all | solution.py:317
  61.3 6.9 %all_gather.11.far_ref = f32[256,640]{1,0:T(8,128)S(1)} all-gather(f32[128,640]{1,0:T(8,128)S(1)} %bitcast.9), channel_id=1, replica_groups=mesh['y'=4,'zh'=4,'z1'=2,'z0'=2,'x'=4,'c'=2] {'c'}, dimensions={0}, use_global_device_ids=true | all-gather | bytes 983040 | tf_op jit(solution)/shard_map/all_gather | solution.py:318
  68.2 0.0 copy-done
  68.2 1.4 %last.1 = bf16[1024,640]{1,0:T(8,128)(2,1)} custom-call(f32[256,640]{1,0:T(8,128)S(1)} %all_gather.11.far_ref, bf16[1024,256]{1,0:T(8,128)(2,1)S(1)} %get-tuple-element.20.ut_ref, f32[256,640]{1,0:T(8,128)S(1)} %get-tuple-element.21.top_ref, f32[768,640]{1,0:T(8,128)S(1)} %copy-done), custom_call_target="tpu_custom_call" | custom-call | tf_op jit(solution)/shard_map/last/pallas_call | solution.py:319
  (1 shorter events, 0.0 us)
Async XLA Ops:
  11.8 24.9 %copy-start.1 = (s32[10]{0:T(128)S(1)}, s32[10]{0:T(128)}, u32[]{:S(2)}) copy-start(s32[10]{0:T(128)} %ranks.1) | copy-start | bytes 124
  22.5 28.7 %all-to-all-start.1 = ((f32[32,2,640]{2,1,0:T(2,128)}), f32[32,2,640]{2,1,0:T(2,128)S(1)}, u32[]{:S(2)}, u32[]{:S(2)}) async-start(f32[32,2,640]{2,1,0:T(2,128)} %get-tuple-element.16), calls=%async_computation.1 | async-start | bytes 327680 | tf_op jit(solution)/shard_map/all_to_all | solution.py:307
  45.9 22.3 %copy-start = (f32[768,640]{1,0:T(8,128)S(1)}, f32[768,640]{1,0:T(8,128)}, u32[]{:S(2)}) copy-start(f32[768,640]{1,0:T(8,128)} %get-tuple-element.22.low_ref) | copy-start | bytes 5898244

commit v9 on v7

--- a/solution.py
+++ b/solution.py
@@ -70,34 +70,58 @@
 
 
 def local_kernel(
-    ranks, core, perm_hbm, s_hbm, leaf_hbm, u_hbm, v_hbm, pair_ref, _,
+    ranks, core, perm_ref, s_hbm, leaf_hbm, u_hbm, v_hbm, pair_ref, _,
     top_ref, low_hbm, ut_ref, token_ref,
-    perm_ref, s_ref, leaf_ref, u_ref, v_ref, ord_ref, uf_ref, us_ref, ue_ref, fe_ref, low_ref, sems, s_sem, leaf_sem, low_sem,
+    s_ref, leaf_ref, u_ref, v_ref, ord_ref, uf_ref, us_ref, ue_ref, fe_ref, low_ref, sems, s_sem, leaf_sem, low_sem,
 ):
     n, leaf = leaf_ref.shape
     rank = v_ref.shape[0]
     step = 256
-    pairs = ((perm_hbm, perm_ref), (u_hbm, u_ref), (v_hbm.at[9], v_ref))
-    copies = [pltpu.make_async_copy(a, b, sems.at[k]) for k, (a, b) in enumerate(pairs)]
-    for copy in copies:
-        copy.start()
-
-    def tall_copies(k):
+    u_copy = pltpu.make_async_copy(u_hbm, u_ref, sems.at[0])
+    v_copy = pltpu.make_async_copy(v_hbm.at[9], v_ref, sems.at[1])
+
+    def s_copy(k):
         rows = pl.ds(pl.multiple_of(k * step, step), step)
-        return (
-            pltpu.make_async_copy(s_hbm.at[rows], s_ref.at[rows], s_sem.at[k]),
-            pltpu.make_async_copy(leaf_hbm.at[rows], leaf_ref.at[rows], leaf_sem.at[k]),
-        )
-
-    def start(k, _):
-        for copy in tall_copies(k):
-            copy.start()
+        return pltpu.make_async_copy(s_hbm.at[rows], s_ref.at[rows], s_sem.at[k])
+
+    def leaf_copy(k):
+        rows = pl.ds(pl.multiple_of(k * step, step), step)
+        return pltpu.make_async_copy(leaf_hbm.at[rows], leaf_ref.at[rows], leaf_sem.at[k])
+
+    def start_s(k, _):
+        s_copy(k).start()
         return 0
 
-    lax.fori_loop(0, n // step, start, 0)
-    copies[0].wait()
+    def start_leaf(k, _):
+        leaf_copy(k).start()
+        return 0
+
+    lax.fori_loop(0, n // step, start_s, 0)
+    v_copy.start()
+    u_copy.start()
+    lax.fori_loop(0, n // step, start_leaf, 0)
     perm = perm_ref[...] & (n - 1)
-    copies[1].wait()
+    lane = lax.broadcasted_iota(jnp.int32, (128, 128), 1)
+
+    def one_hot(i):
+        hot = []
+        for h in range(i, i + step, 128):
+            column = jnp.broadcast_to(perm[:, h : h + 128], (128, 128)).T
+            hot.append(
+                jnp.concatenate(
+                    [jnp.where(column == lane + j, 1.0, 0.0).astype(BF16) for j in range(0, n, 128)], axis=1
+                )
+            )
+        return jnp.concatenate(hot, axis=0)
+
+    hot = one_hot(0)
+    for k in range(n // step):
+        s_copy(k).wait()
+    for i in range(0, n, step):
+        ord_ref[i : i + step, :] = dot(hot, s_ref[...]).astype(BF16)
+        if i + step < n:
+            hot = one_hot(i + step)
+    u_copy.wait()
     row = lax.broadcasted_iota(jnp.int32, (rank, n), 0)
     lane_n = lax.broadcasted_iota(jnp.int32, (rank, n), 1)
     for level in range(8):
@@ -111,21 +135,9 @@
     ue_ref[rank : 2 * rank, :] = jnp.where(lane_n < leaf, last, 0.0).astype(BF16)
     ue_ref[2 * rank : 3 * rank, :] = jnp.where(lane_n < leaf, 0.0, last).astype(BF16)
 
-    copies[2].wait()
+    v_copy.wait()
     for k in range(n // step):
-        for copy in tall_copies(k):
-            copy.wait()
-    lane = lax.broadcasted_iota(jnp.int32, (128, 128), 1)
-    for i in range(0, n, step):
-        hot = []
-        for h in range(i, i + step, 128):
-            column = jnp.broadcast_to(perm[:, h : h + 128], (128, 128)).T
-            hot.append(
-                jnp.concatenate(
-                    [jnp.where(column == lane + j, 1.0, 0.0).astype(BF16) for j in range(0, n, 128)], axis=1
-                )
-            )
-        ord_ref[i : i + step, :] = dot(jnp.concatenate(hot, axis=0), s_ref[...]).astype(BF16)
+        leaf_copy(k).wait()
     fe_ref[0:rank, :] = pair_ref[1 - core[0], 4 * rank :, :].astype(BF16)
     fe_ref[rank : 2 * rank, :] = dot(v_ref[:, leaf:], ord_ref[leaf:, :]).astype(BF16)
     fe_ref[2 * rank : 3 * rank, :] = dot(v_ref[:, :leaf], ord_ref[:leaf, :]).astype(BF16)
@@ -276,7 +288,7 @@
     top, low, ut, token = pl.pallas_call(
         local_kernel,
         name="local",
-        in_specs=[SMEM, SMEM] + [HBM] * 5 + [VMEM, ANY],
+        in_specs=[SMEM, SMEM, VMEM] + [HBM] * 4 + [VMEM, ANY],
         out_specs=[VMEM, HBM, VMEM, VMEM],
         out_shape=[
             pltpu.VMEM((n - low_rows, rhs), F32),
@@ -285,7 +297,6 @@
             shape((8, 128)),
         ],
         scratch_shapes=[
-            pltpu.VMEM((1, n), jnp.int32),
             pltpu.VMEM((n, rhs), BF16),
             pltpu.VMEM(leaf_blocks.shape, BF16),
             pltpu.VMEM(u_factors.shape, BF16),
@@ -296,14 +307,14 @@
             pltpu.VMEM((3 * rank, n), BF16),
             pltpu.VMEM((3 * rank, rhs), BF16),
             pltpu.VMEM((low_rows, rhs), F32),
-            pltpu.SemaphoreType.DMA((3,)),
+            pltpu.SemaphoreType.DMA((2,)),
             pltpu.SemaphoreType.DMA((n // 256,)),
             pltpu.SemaphoreType.DMA((n // 256,)),
             pltpu.SemaphoreType.DMA((low_rows // 256,)),
         ],
         compiler_params=grant(12),
         cost_estimate=pl.CostEstimate(flops=4_700_000_000, bytes_accessed=8_000_000, transcendentals=0),
-    )(level_ranks, core, *in_hbm(perm, sources, leaf_blocks, u_factors, v_factors), *in_vmem(pair), token)
+    )(level_ranks, core, *in_vmem(perm), *in_hbm(sources, leaf_blocks, u_factors, v_factors), *in_vmem(pair), token)
     rows = lax.all_to_all(rows, MIDDLE, 0, 0, tiled=True)
     far = pl.pallas_call(
         far_kernel,

time: 69.3 us -> 69.3 us (level)
  no operation moved by 1% of the time
where the time goes in v9:
time: 69.3 us; the launch traced here: 69 us
  blocking collectives  35.4 us (51%)
  Pallas kernels  14.4 us (21%)
  starting transfers between devices  14.2 us (20%)
  waiting for transfers between devices  4.98 us (7%)
    all_to_all x1, starting transfers between devices, per_device(): rows = lax.all_to_all(rows, MIDDLE, 0, 0, tiled=True)  14.2 us
    all_to_all x1, blocking collectives, per_device(): got = lax.all_to_all(partial, OUTER, 0, 0, tiled=True)  9.93 us
    all_to_all x1, blocking collectives, per_device(): far = lax.all_to_all(far, OUTER, 0, 0, tiled=True)  9.26 us
    pallas_call x1, Pallas kernels, per_device(): pl.pallas_call(local_kernel, name='local', in_specs=[SMEM, SMEM, VMEM] +...  9.19 us
    all_gather x1, blocking collectives, per_device(): pair = lax.all_gather(send, 'c')  8.86 us
    all_gather x1, blocking collectives, per_device(): far = lax.all_gather(far.reshape(half, rhs), 'c', axis=0, tiled=True)  7.38 us
    all_to_all x1, waiting for transfers between devices, per_device(): rows = lax.all_to_all(rows, MIDDLE, 0, 0, tiled=True)  4.98 us
    pallas_call x1, Pallas kernels, per_device(): pl.pallas_call(coef_kernel, name='coef', in_specs=[SMEM, HBM, HBM, HBM],...  2.97 us
  transfers between devices with their start and end apart: 1, of which 1 were waited for; matrix products, arithmetic and copies ran while one was open for 0% of the time, Pallas kernels for 13%

profile of v9, /device:TPU:1, one launch (start us, length us, event | category | flops | bytes accessed | tf_op | source)
XLA Modules:
  0.0 69.0 jit_solution(11718109013786609763)
XLA Ops:
  0.0 3.0 %coef.1 = (f32[128,640]{1,0:T(8,128)S(1)}, f32[160,640]{1,0:T(8,128)S(1)}) custom-call(s32[1]{0:T(128)} %bitcast.1.core, s32[1,1024]{1,0:T(1,128)} %bitcast.9, bf16[10,32,1024]{2,1,0:T(8,128)(2,1)} %v_hbm.3, bf16[1024,640]{1,0:T(8,128)(2,1)} %s_hbm.3), custom_call_target="tpu_custom_call" | custom-call | tf_op jit(solution)/shard_map/coef/pallas_call | solution.py:253
  3.0 8.9 %all-gather = f32[320,640]{1,0:T(8,128)S(1)} all-gather(f32[160,640]{1,0:T(8,128)S(1)} %get-tuple-element.15), channel_id=2, replica_groups=mesh['y'=4,'zh'=4,'z1'=2,'z0'=2,'x'=4,'c'=2] {'c'}, dimensions={0}, use_global_device_ids=true | all-gather | bytes 1228800 | tf_op jit(solution)/shard_map/all_gather | solution.py:270
  11.8 0.0 copy-start.1
  11.8 0.0 copy-start.2
  11.9 9.9 %all_to_all.15.got_ref = f32[8,16,640]{2,1,0:T(8,128)S(1)} all-to-all(f32[8,16,640]{2,1,0:T(8,128)S(1)} %bitcast.8), channel_id=1, replica_groups=mesh['y'=4,'zh'=4,'z1'=2,'z0'=2,'x'=4,'c'=2] {'z0','x'}, dimensions={0} | all-to-all | bytes 655360 | tf_op jit(solution)/shard_map/all_to_all | solution.py:279
  21.8 0.7 %middle.1 = (f32[32,2,640]{2,1,0:T(2,128)}, f32[8,8,640]{2,1,0:T(8,128)S(1)}, f32[8,128]{1,0:T(8,128)S(1)}) custom-call(s32[1]{0:T(128)} %bitcast._.me, f32[8,16,640]{2,1,0:T(8,128)S(1)} %all_to_all.15.got_ref), custom_call_target="tpu_custom_call" | custom-call | tf_op jit(solution)/shard_map/middle/pallas_call | solution.py:280
  22.5 14.2 %all-to-all-start.1 = ((f32[32,2,640]{2,1,0:T(2,128)}), f32[32,2,640]{2,1,0:T(2,128)S(1)}, u32[]{:S(2)}, u32[]{:S(2)}) async-start(f32[32,2,640]{2,1,0:T(2,128)} %get-tuple-element.16), calls=%async_computation.1 | async-start | bytes 327680 | tf_op jit(solution)/shard_map/all_to_all | solution.py:318
  36.7 0.0 copy-done.1
  36.7 0.0 copy-done.2
  36.7 9.2 %local.1 = (f32[256,640]{1,0:T(8,128)S(1)}, f32[768,640]{1,0:T(8,128)}, bf16[1024,256]{1,0:T(8,128)(2,1)S(1)}, f32[8,128]{1,0:T(8,128)S(1)}) custom-call(s32[10]{0:T(128)S(1)} %copy-done.2, s32[1]{0:T(128)} %bitcast.1.core, s32[1,1024]{1,0:T(1,128)S(1)} %bitcast.10, bf16[1024,640]{1,0:T(8,128)(2,1)} %s_hbm.3, bf16[1024,512]{1,0:T(8,128)(2,1)} %leaf_hbm.1, ...), custom_call_target="tpu_custom_call" | custom-call | flops 4700000256 | bytes 8000000 | tf_op jit(solution)/shard_map/local/pallas_call | solution.py:288
  45.9 0.0 copy-start
  46.0 5.0 %all-to-all-done.1.got_ref = f32[32,2,640]{2,1,0:T(2,128)S(1)} async-done(((f32[32,2,640]{2,1,0:T(2,128)}), f32[32,2,640]{2,1,0:T(2,128)S(1)}, u32[]{:S(2)}, u32[]{:S(2)}) %all-to-all-start.1) | async-done | bytes 163872 | tf_op jit(solution)/shard_map/all_to_all | solution.py:318
  50.9 0.1 far.1
  51.0 9.3 %all_to_all.16 = f32[8,16,640]{2,1,0:T(8,128)S(1)} all-to-all(f32[8,16,640]{2,1,0:T(8,128)S(1)} %far.1), channel_id=1, replica_groups=mesh['y'=4,'zh'=4,'z1'=2,'z0'=2,'x'=4,'c'=2] {'z0','x'}, dimensions={0} | all-to-all | bytes 655360 | tf_op jit(solution)/shard_map/all_to_all | solution.py:328
  60.3 7.4 %all_gather.11.far_ref = f32[256,640]{1,0:T(8,128)S(1)} all-gather(f32[128,640]{1,0:T(8,128)S(1)} %bitcast.11), channel_id=1, replica_groups=mesh['y'=4,'zh'=4,'z1'=2,'z0'=2,'x'=4,'c'=2] {'c'}, dimensions={0}, use_global_device_ids=true | all-gather | bytes 983040 | tf_op jit(solution)/shard_map/all_gather | solution.py:329
  67.7 0.0 copy-done
  67.7 1.4 %last.1 = bf16[1024,640]{1,0:T(8,128)(2,1)} custom-call(f32[256,640]{1,0:T(8,128)S(1)} %all_gather.11.far_ref, bf16[1024,256]{1,0:T(8,128)(2,1)S(1)} %get-tuple-element.20.ut_ref, f32[256,640]{1,0:T(8,128)S(1)} %get-tuple-element.21.top_ref, f32[768,640]{1,0:T(8,128)S(1)} %copy-done), custom_call_target="tpu_custom_call" | custom-call | tf_op jit(solution)/shard_map/last/pallas_call | solution.py:330
  (1 shorter events, 0.0 us)
Async XLA Ops:
  11.8 24.9 %copy-start.1 = (s32[1024]{0:T(1024)S(1)}, s32[1024]{0:T(1024)}, u32[]{:S(2)}) copy-start(s32[1024]{0:T(1024)} %param.7) | copy-start | bytes 12292
  11.8 24.9 %copy-start.2 = (s32[10]{0:T(128)S(1)}, s32[10]{0:T(128)}, u32[]{:S(2)}) copy-start(s32[10]{0:T(128)} %ranks.1) | copy-start | bytes 124
  22.5 28.4 %all-to-all-start.1 = ((f32[32,2,640]{2,1,0:T(2,128)}), f32[32,2,640]{2,1,0:T(2,128)S(1)}, u32[]{:S(2)}, u32[]{:S(2)}) async-start(f32[32,2,640]{2,1,0:T(2,128)} %get-tuple-element.16), calls=%async_computation.1 | async-start | bytes 327680 | tf_op jit(solution)/shard_map/all_to_all | solution.py:318
  45.9 21.7 %copy-start = (f32[768,640]{1,0:T(8,128)S(1)}, f32[768,640]{1,0:T(8,128)}, u32[]{:S(2)}) copy-start(f32[768,640]{1,0:T(8,128)} %get-tuple-element.22.low_ref) | copy-start | bytes 5898244

commit v10 on v9

--- a/solution.py
+++ b/solution.py
@@ -103,9 +103,9 @@
     perm = perm_ref[...] & (n - 1)
     lane = lax.broadcasted_iota(jnp.int32, (128, 128), 1)
 
-    def one_hot(i):
+    def one_hot(i, count):
         hot = []
-        for h in range(i, i + step, 128):
+        for h in range(i, i + count, 128):
             column = jnp.broadcast_to(perm[:, h : h + 128], (128, 128)).T
             hot.append(
                 jnp.concatenate(
@@ -114,13 +114,14 @@
             )
         return jnp.concatenate(hot, axis=0)
 
-    hot = one_hot(0)
+    tall = 512
+    hot = one_hot(0, tall)
     for k in range(n // step):
         s_copy(k).wait()
-    for i in range(0, n, step):
-        ord_ref[i : i + step, :] = dot(hot, s_ref[...]).astype(BF16)
-        if i + step < n:
-            hot = one_hot(i + step)
+    for i in range(0, n, tall):
+        ord_ref[i : i + tall, :] = dot(hot, s_ref[...]).astype(BF16)
+        if i + tall < n:
+            hot = one_hot(i + tall, tall)
     u_copy.wait()
     row = lax.broadcasted_iota(jnp.int32, (rank, n), 0)
     lane_n = lax.broadcasted_iota(jnp.int32, (rank, n), 1)
@@ -143,9 +144,9 @@
     fe_ref[2 * rank : 3 * rank, :] = dot(v_ref[:, :leaf], ord_ref[:leaf, :]).astype(BF16)
     top = top_ref.shape[0]
     kept = []
-    for j in [*range(top, n, step), *range(0, top, step)]:
-        rows = slice(j, j + step)
-        hot = one_hot_t(perm, j, step)
+    for j, count in ((256, 512), (768, 256), (0, 256)):
+        rows = slice(j, j + count)
+        hot = one_hot_t(perm, j, count)
         leaves = [dot(hot[:, g : g + leaf], leaf_ref[g : g + leaf, :]).astype(BF16) for g in range(0, n, leaf)]
         ut_ref[rows, :] = dot(hot, us_ref[...], NT).astype(BF16)
         et = dot(hot, ue_ref[...], NT).astype(BF16)
@@ -153,7 +154,7 @@
         if j < top:
             top_ref[rows, :] = base
         else:
-            part = slice(j - top, j - top + step)
+            part = slice(j - top, j - top + count)
             low_ref[part, :] = base
             kept.append(pltpu.make_async_copy(low_ref.at[part], low_hbm.at[part], low_sem.at[len(kept)]))
             kept[-1].start()

time: 69.3 us -> 69.3 us (level)
  no operation moved by 1% of the time
where the time goes in v10:
time: 69.3 us; the launch traced here: 69 us
  blocking collectives  35.4 us (51%)
  Pallas kernels  14.2 us (20%)
  starting transfers between devices  14.2 us (20%)
  waiting for transfers between devices  5.19 us (7%)
    all_to_all x1, starting transfers between devices, per_device(): rows = lax.all_to_all(rows, MIDDLE, 0, 0, tiled=True)  14.2 us
    all_to_all x1, blocking collectives, per_device(): got = lax.all_to_all(partial, OUTER, 0, 0, tiled=True)  9.93 us
    all_to_all x1, blocking collectives, per_device(): far = lax.all_to_all(far, OUTER, 0, 0, tiled=True)  9.26 us
    pallas_call x1, Pallas kernels, per_device(): pl.pallas_call(local_kernel, name='local', in_specs=[SMEM, SMEM, VMEM] +...  8.99 us
    all_gather x1, blocking collectives, per_device(): pair = lax.all_gather(send, 'c')  8.86 us
    all_gather x1, blocking collectives, per_device(): far = lax.all_gather(far.reshape(half, rhs), 'c', axis=0, tiled=True)  7.38 us
    all_to_all x1, waiting for transfers between devices, per_device(): rows = lax.all_to_all(rows, MIDDLE, 0, 0, tiled=True)  5.19 us
    pallas_call x1, Pallas kernels, per_device(): pl.pallas_call(coef_kernel, name='coef', in_specs=[SMEM, HBM, HBM, HBM],...  2.97 us
  transfers between devices with their start and end apart: 1, of which 1 were waited for; matrix products, arithmetic and copies ran while one was open for 0% of the time, Pallas kernels for 13%

profile of v10, /device:TPU:1, one launch (start us, length us, event | category | flops | bytes accessed | tf_op | source)
XLA Modules:
  0.0 69.0 jit_solution(7264367081617840901)
XLA Ops:
  0.0 3.0 %coef.1 = (f32[128,640]{1,0:T(8,128)S(1)}, f32[160,640]{1,0:T(8,128)S(1)}) custom-call(s32[1]{0:T(128)} %bitcast.1.core, s32[1,1024]{1,0:T(1,128)} %bitcast.9, bf16[10,32,1024]{2,1,0:T(8,128)(2,1)} %v_hbm.3, bf16[1024,640]{1,0:T(8,128)(2,1)} %s_hbm.3), custom_call_target="tpu_custom_call" | custom-call | tf_op jit(solution)/shard_map/coef/pallas_call | solution.py:254
  3.0 8.9 %all-gather = f32[320,640]{1,0:T(8,128)S(1)} all-gather(f32[160,640]{1,0:T(8,128)S(1)} %get-tuple-element.15), channel_id=2, replica_groups=mesh['y'=4,'zh'=4,'z1'=2,'z0'=2,'x'=4,'c'=2] {'c'}, dimensions={0}, use_global_device_ids=true | all-gather | bytes 1228800 | tf_op jit(solution)/shard_map/all_gather | solution.py:271
  11.8 0.0 copy-start.1
  11.8 0.0 copy-start.2
  11.9 9.9 %all_to_all.15.got_ref = f32[8,16,640]{2,1,0:T(8,128)S(1)} all-to-all(f32[8,16,640]{2,1,0:T(8,128)S(1)} %bitcast.8), channel_id=1, replica_groups=mesh['y'=4,'zh'=4,'z1'=2,'z0'=2,'x'=4,'c'=2] {'z0','x'}, dimensions={0} | all-to-all | bytes 655360 | tf_op jit(solution)/shard_map/all_to_all | solution.py:280
  21.8 0.7 %middle.1 = (f32[32,2,640]{2,1,0:T(2,128)}, f32[8,8,640]{2,1,0:T(8,128)S(1)}, f32[8,128]{1,0:T(8,128)S(1)}) custom-call(s32[1]{0:T(128)} %bitcast._.me, f32[8,16,640]{2,1,0:T(8,128)S(1)} %all_to_all.15.got_ref), custom_call_target="tpu_custom_call" | custom-call | tf_op jit(solution)/shard_map/middle/pallas_call | solution.py:281
  22.5 14.2 %all-to-all-start.1 = ((f32[32,2,640]{2,1,0:T(2,128)}), f32[32,2,640]{2,1,0:T(2,128)S(1)}, u32[]{:S(2)}, u32[]{:S(2)}) async-start(f32[32,2,640]{2,1,0:T(2,128)} %get-tuple-element.16), calls=%async_computation.1 | async-start | bytes 327680 | tf_op jit(solution)/shard_map/all_to_all | solution.py:319
  36.7 0.0 copy-done.1
  36.7 0.0 copy-done.2
  36.7 9.0 %local.1 = (f32[256,640]{1,0:T(8,128)S(1)}, f32[768,640]{1,0:T(8,128)}, bf16[1024,256]{1,0:T(8,128)(2,1)S(1)}, f32[8,128]{1,0:T(8,128)S(1)}) custom-call(s32[10]{0:T(128)S(1)} %copy-done.2, s32[1]{0:T(128)} %bitcast.1.core, s32[1,1024]{1,0:T(1,128)S(1)} %bitcast.10, bf16[1024,640]{1,0:T(8,128)(2,1)} %s_hbm.3, bf16[1024,512]{1,0:T(8,128)(2,1)} %leaf_hbm.1, ...), custom_call_target="tpu_custom_call" | custom-call | flops 4700000256 | bytes 8000000 | tf_op jit(solution)/shard_map/local/pallas_call | solution.py:289
  45.7 0.0 copy-start
  45.8 5.2 %all-to-all-done.1.got_ref = f32[32,2,640]{2,1,0:T(2,128)S(1)} async-done(((f32[32,2,640]{2,1,0:T(2,128)}), f32[32,2,640]{2,1,0:T(2,128)S(1)}, u32[]{:S(2)}, u32[]{:S(2)}) %all-to-all-start.1) | async-done | bytes 163872 | tf_op jit(solution)/shard_map/all_to_all | solution.py:319
  50.9 0.1 far.1
  51.0 9.3 %all_to_all.16 = f32[8,16,640]{2,1,0:T(8,128)S(1)} all-to-all(f32[8,16,640]{2,1,0:T(8,128)S(1)} %far.1), channel_id=1, replica_groups=mesh['y'=4,'zh'=4,'z1'=2,'z0'=2,'x'=4,'c'=2] {'z0','x'}, dimensions={0} | all-to-all | bytes 655360 | tf_op jit(solution)/shard_map/all_to_all | solution.py:329
  60.3 7.4 %all_gather.11.far_ref = f32[256,640]{1,0:T(8,128)S(1)} all-gather(f32[128,640]{1,0:T(8,128)S(1)} %bitcast.11), channel_id=1, replica_groups=mesh['y'=4,'zh'=4,'z1'=2,'z0'=2,'x'=4,'c'=2] {'c'}, dimensions={0}, use_global_device_ids=true | all-gather | bytes 983040 | tf_op jit(solution)/shard_map/all_gather | solution.py:330
  67.7 0.0 copy-done
  67.7 1.4 %last.1 = bf16[1024,640]{1,0:T(8,128)(2,1)} custom-call(f32[256,640]{1,0:T(8,128)S(1)} %all_gather.11.far_ref, bf16[1024,256]{1,0:T(8,128)(2,1)S(1)} %get-tuple-element.20.ut_ref, f32[256,640]{1,0:T(8,128)S(1)} %get-tuple-element.21.top_ref, f32[768,640]{1,0:T(8,128)S(1)} %copy-done), custom_call_target="tpu_custom_call" | custom-call | tf_op jit(solution)/shard_map/last/pallas_call | solution.py:331
  (1 shorter events, 0.0 us)
Async XLA Ops:
  11.8 24.9 %copy-start.1 = (s32[1024]{0:T(1024)S(1)}, s32[1024]{0:T(1024)}, u32[]{:S(2)}) copy-start(s32[1024]{0:T(1024)} %param.7) | copy-start | bytes 12292
  11.8 24.9 %copy-start.2 = (s32[10]{0:T(128)S(1)}, s32[10]{0:T(128)}, u32[]{:S(2)}) copy-start(s32[10]{0:T(128)} %ranks.1) | copy-start | bytes 124
  22.5 28.4 %all-to-all-start.1 = ((f32[32,2,640]{2,1,0:T(2,128)}), f32[32,2,640]{2,1,0:T(2,128)S(1)}, u32[]{:S(2)}, u32[]{:S(2)}) async-start(f32[32,2,640]{2,1,0:T(2,128)} %get-tuple-element.16), calls=%async_computation.1 | async-start | bytes 327680 | tf_op jit(solution)/shard_map/all_to_all | solution.py:319
  45.7 21.9 %copy-start = (f32[768,640]{1,0:T(8,128)S(1)}, f32[768,640]{1,0:T(8,128)}, u32[]{:S(2)}) copy-start(f32[768,640]{1,0:T(8,128)} %get-tuple-element.22.low_ref) | copy-start | bytes 5898244

commit v11 on v9

--- a/solution.py
+++ b/solution.py
@@ -8,7 +8,7 @@
 
 AXES = ("y", "zh", "z1", "z0", "x", "c")
 OUTER = ("z0", "x")
-MIDDLE = ("y", "zh", "z1")
+MIDDLE = ("z1", "y", "zh")
 F32 = jnp.float32
 BF16 = jnp.bfloat16
 NN = (((1,), (0,)), ((), ()))
@@ -163,7 +163,7 @@
 
 
 def level_at(apart):
-    for bit, row in ((16, 0), (8, 1), (4, 2), (2, 3)):
+    for bit, row in ((8, 0), (4, 1), (2, 2), (1, 3)):
         if apart & bit:
             return row
     return 4

time: 69.3 us -> 70.8 us (1.022)
  blocking collectives: 35.4 us -> 36.2 us
    all_to_all x1, blocking collectives: 9.26 us -> 10.5 us  [per_device(): far = lax.all_to_all(far, OUTER, 0, 0, tiled=True)]
where the time goes in v11:
time: 70.8 us; the launch traced here: 70.5 us
  blocking collectives  36.2 us (51%)
  Pallas kernels  14.4 us (20%)
  starting transfers between devices  14.2 us (20%)
  waiting for transfers between devices  5.63 us (8%)
    all_to_all x1, starting transfers between devices, per_device(): rows = lax.all_to_all(rows, MIDDLE, 0, 0, tiled=True)  14.2 us
    all_to_all x1, blocking collectives, per_device(): far = lax.all_to_all(far, OUTER, 0, 0, tiled=True)  10.5 us
    all_to_all x1, blocking collectives, per_device(): got = lax.all_to_all(partial, OUTER, 0, 0, tiled=True)  9.93 us
    pallas_call x1, Pallas kernels, per_device(): pl.pallas_call(local_kernel, name='local', in_specs=[SMEM, SMEM, VMEM] +...  9.19 us
    all_gather x1, blocking collectives, per_device(): pair = lax.all_gather(send, 'c')  8.86 us
    all_gather x1, blocking collectives, per_device(): far = lax.all_gather(far.reshape(half, rhs), 'c', axis=0, tiled=True)  6.88 us
    all_to_all x1, waiting for transfers between devices, per_device(): rows = lax.all_to_all(rows, MIDDLE, 0, 0, tiled=True)  5.63 us
    pallas_call x1, Pallas kernels, per_device(): pl.pallas_call(coef_kernel, name='coef', in_specs=[SMEM, HBM, HBM, HBM],...  2.97 us
  transfers between devices with their start and end apart: 1, of which 1 were waited for; matrix products, arithmetic and copies ran while one was open for 0% of the time, Pallas kernels for 13%

profile of v11, /device:TPU:1, one launch (start us, length us, event | category | flops | bytes accessed | tf_op | source)
XLA Modules:
  0.0 70.5 jit_solution(15270487832269570423)
XLA Ops:
  0.0 3.0 %coef.1 = (f32[128,640]{1,0:T(8,128)S(1)}, f32[160,640]{1,0:T(8,128)S(1)}) custom-call(s32[1]{0:T(128)} %bitcast.1.core, s32[1,1024]{1,0:T(1,128)} %bitcast.9, bf16[10,32,1024]{2,1,0:T(8,128)(2,1)} %v_hbm.3, bf16[1024,640]{1,0:T(8,128)(2,1)} %s_hbm.3), custom_call_target="tpu_custom_call" | custom-call | tf_op jit(solution)/shard_map/coef/pallas_call | solution.py:253
  3.0 8.9 %all-gather = f32[320,640]{1,0:T(8,128)S(1)} all-gather(f32[160,640]{1,0:T(8,128)S(1)} %get-tuple-element.15), channel_id=2, replica_groups=mesh['y'=4,'zh'=4,'z1'=2,'z0'=2,'x'=4,'c'=2] {'c'}, dimensions={0}, use_global_device_ids=true | all-gather | bytes 1228800 | tf_op jit(solution)/shard_map/all_gather | solution.py:270
  11.8 0.0 copy-start.1
  11.8 0.0 copy-start.2
  11.9 9.9 %all_to_all.15.got_ref = f32[8,16,640]{2,1,0:T(8,128)S(1)} all-to-all(f32[8,16,640]{2,1,0:T(8,128)S(1)} %bitcast.8), channel_id=1, replica_groups=mesh['y'=4,'zh'=4,'z1'=2,'z0'=2,'x'=4,'c'=2] {'z0','x'}, dimensions={0} | all-to-all | bytes 655360 | tf_op jit(solution)/shard_map/all_to_all | solution.py:279
  21.8 0.7 %middle.1 = (f32[32,2,640]{2,1,0:T(2,128)}, f32[8,8,640]{2,1,0:T(8,128)S(1)}, f32[8,128]{1,0:T(8,128)S(1)}) custom-call(s32[1]{0:T(128)} %bitcast._.me, f32[8,16,640]{2,1,0:T(8,128)S(1)} %all_to_all.15.got_ref), custom_call_target="tpu_custom_call" | custom-call | tf_op jit(solution)/shard_map/middle/pallas_call | solution.py:280
  22.5 14.2 %all-to-all-start.1 = ((f32[32,2,640]{2,1,0:T(2,128)}), f32[32,2,640]{2,1,0:T(2,128)S(1)}, u32[]{:S(2)}, u32[]{:S(2)}) async-start(f32[32,2,640]{2,1,0:T(2,128)} %get-tuple-element.16), calls=%async_computation.1 | async-start | bytes 327680 | tf_op jit(solution)/shard_map/all_to_all | solution.py:318
  36.7 0.0 copy-done.1
  36.7 0.0 copy-done.2
  36.7 9.2 %local.1 = (f32[256,640]{1,0:T(8,128)S(1)}, f32[768,640]{1,0:T(8,128)}, bf16[1024,256]{1,0:T(8,128)(2,1)S(1)}, f32[8,128]{1,0:T(8,128)S(1)}) custom-call(s32[10]{0:T(128)S(1)} %copy-done.2, s32[1]{0:T(128)} %bitcast.1.core, s32[1,1024]{1,0:T(1,128)S(1)} %bitcast.10, bf16[1024,640]{1,0:T(8,128)(2,1)} %s_hbm.3, bf16[1024,512]{1,0:T(8,128)(2,1)} %leaf_hbm.1, ...), custom_call_target="tpu_custom_call" | custom-call | flops 4700000256 | bytes 8000000 | tf_op jit(solution)/shard_map/local/pallas_call | solution.py:288
  45.9 0.0 copy-start
  46.0 5.6 %all-to-all-done.1.got_ref = f32[32,2,640]{2,1,0:T(2,128)S(1)} async-done(((f32[32,2,640]{2,1,0:T(2,128)}), f32[32,2,640]{2,1,0:T(2,128)S(1)}, u32[]{:S(2)}, u32[]{:S(2)}) %all-to-all-start.1) | async-done | bytes 163872 | tf_op jit(solution)/shard_map/all_to_all | solution.py:318
  51.6 0.1 far.1
  51.7 10.5 %all_to_all.16 = f32[8,16,640]{2,1,0:T(8,128)S(1)} all-to-all(f32[8,16,640]{2,1,0:T(8,128)S(1)} %far.1), channel_id=1, replica_groups=mesh['y'=4,'zh'=4,'z1'=2,'z0'=2,'x'=4,'c'=2] {'z0','x'}, dimensions={0} | all-to-all | bytes 655360 | tf_op jit(solution)/shard_map/all_to_all | solution.py:328
  62.2 6.9 %all_gather.11.far_ref = f32[256,640]{1,0:T(8,128)S(1)} all-gather(f32[128,640]{1,0:T(8,128)S(1)} %bitcast.11), channel_id=1, replica_groups=mesh['y'=4,'zh'=4,'z1'=2,'z0'=2,'x'=4,'c'=2] {'c'}, dimensions={0}, use_global_device_ids=true | all-gather | bytes 983040 | tf_op jit(solution)/shard_map/all_gather | solution.py:329
  69.1 0.0 copy-done
  69.1 1.4 %last.1 = bf16[1024,640]{1,0:T(8,128)(2,1)} custom-call(f32[256,640]{1,0:T(8,128)S(1)} %all_gather.11.far_ref, bf16[1024,256]{1,0:T(8,128)(2,1)S(1)} %get-tuple-element.20.ut_ref, f32[256,640]{1,0:T(8,128)S(1)} %get-tuple-element.21.top_ref, f32[768,640]{1,0:T(8,128)S(1)} %copy-done), custom_call_target="tpu_custom_call" | custom-call | tf_op jit(solution)/shard_map/last/pallas_call | solution.py:330
  (1 shorter events, 0.0 us)
Async XLA Ops:
  11.8 24.9 %copy-start.1 = (s32[1024]{0:T(1024)S(1)}, s32[1024]{0:T(1024)}, u32[]{:S(2)}) copy-start(s32[1024]{0:T(1024)} %param.7) | copy-start | bytes 12292
  11.8 24.9 %copy-start.2 = (s32[10]{0:T(128)S(1)}, s32[10]{0:T(128)}, u32[]{:S(2)}) copy-start(s32[10]{0:T(128)} %ranks.1) | copy-start | bytes 124
  22.5 29.1 %all-to-all-start.1 = ((f32[32,2,640]{2,1,0:T(2,128)}), f32[32,2,640]{2,1,0:T(2,128)S(1)}, u32[]{:S(2)}, u32[]{:S(2)}) async-start(f32[32,2,640]{2,1,0:T(2,128)} %get-tuple-element.16), calls=%async_computation.1 | async-start | bytes 327680 | tf_op jit(solution)/shard_map/all_to_all | solution.py:318
  45.9 23.2 %copy-start = (f32[768,640]{1,0:T(8,128)S(1)}, f32[768,640]{1,0:T(8,128)}, u32[]{:S(2)}) copy-start(f32[768,640]{1,0:T(8,128)} %get-tuple-element.22.low_ref) | copy-start | bytes 5898244

commit v12 on v9

--- a/solution.py
+++ b/solution.py
@@ -7,7 +7,7 @@
 from jax.sharding import PartitionSpec as P
 
 AXES = ("y", "zh", "z1", "z0", "x", "c")
-OUTER = ("z0", "x")
+OUTER = ("x", "z0")
 MIDDLE = ("y", "zh", "z1")
 F32 = jnp.float32
 BF16 = jnp.bfloat16
@@ -172,16 +172,16 @@
 def middle_kernel(me, got_ref, out_ref, fine_ref, token_ref):
     token_ref[...] = jnp.zeros_like(token_ref)
     rows = got_ref.shape[1]
-    got = lambda z, x: got_ref[z * 4 + x]
+    got = lambda z, x: got_ref[x * 2 + z]
     sums = [(got(z, 0) + got(z, 1)) + (got(z, 2) + got(z, 3)) for z in range(2)]
     total = sums[0] + sums[1]
     for z in range(2):
         for x in range(4):
             for j in range(rows // 8):
                 at = lambda a, row: a[j * 8 + row : j * 8 + row + 1]
-                fine_ref[z * 4 + x, j * 4 : j * 4 + 1, :] = at(sums[z ^ 1], 5)
-                fine_ref[z * 4 + x, j * 4 + 1 : j * 4 + 2, :] = at(got(z, x ^ 2), 6) + at(got(z, x ^ 3), 6)
-                fine_ref[z * 4 + x, j * 4 + 2 : j * 4 + 3, :] = at(got(z, x ^ 1), 7)
+                fine_ref[x * 2 + z, j * 4 : j * 4 + 1, :] = at(sums[z ^ 1], 5)
+                fine_ref[x * 2 + z, j * 4 + 1 : j * 4 + 2, :] = at(got(z, x ^ 2), 6) + at(got(z, x ^ 3), 6)
+                fine_ref[x * 2 + z, j * 4 + 2 : j * 4 + 3, :] = at(got(z, x ^ 1), 7)
     for row in range(5):
         sent = jnp.concatenate([total[r + row : r + row + 1] for r in range(0, rows, 8)], axis=0)
         for apart in range(out_ref.shape[0]):

time: 69.3 us -> 69.7 us (level)
  no operation moved by 1% of the time
where the time goes in v12:
time: 69.7 us; the launch traced here: 69.4 us
  blocking collectives  35.6 us (51%)
  Pallas kernels  14.4 us (21%)
  starting transfers between devices  14.2 us (20%)
  waiting for transfers between devices  5.1 us (7%)
    all_to_all x1, starting transfers between devices, per_device(): rows = lax.all_to_all(rows, MIDDLE, 0, 0, tiled=True)  14.2 us
    all_to_all x1, blocking collectives, per_device(): got = lax.all_to_all(partial, OUTER, 0, 0, tiled=True)  9.93 us
    pallas_call x1, Pallas kernels, per_device(): pl.pallas_call(local_kernel, name='local', in_specs=[SMEM, SMEM, VMEM] +...  9.2 us
    all_to_all x1, blocking collectives, per_device(): far = lax.all_to_all(far, OUTER, 0, 0, tiled=True)  9.07 us
    all_gather x1, blocking collectives, per_device(): pair = lax.all_gather(send, 'c')  8.86 us
    all_gather x1, blocking collectives, per_device(): far = lax.all_gather(far.reshape(half, rhs), 'c', axis=0, tiled=True)  7.77 us
    all_to_all x1, waiting for transfers between devices, per_device(): rows = lax.all_to_all(rows, MIDDLE, 0, 0, tiled=True)  5.1 us
    pallas_call x1, Pallas kernels, per_device(): pl.pallas_call(coef_kernel, name='coef', in_specs=[SMEM, HBM, HBM, HBM],...  2.97 us
  transfers between devices with their start and end apart: 1, of which 1 were waited for; matrix products, arithmetic and copies ran while one was open for 0% of the time, Pallas kernels for 13%

profile of v12, /device:TPU:1, one launch (start us, length us, event | category | flops | bytes accessed | tf_op | source)
XLA Modules:
  0.0 69.4 jit_solution(12438326595845413355)
XLA Ops:
  0.0 3.0 %coef.1 = (f32[128,640]{1,0:T(8,128)S(1)}, f32[160,640]{1,0:T(8,128)S(1)}) custom-call(s32[1]{0:T(128)} %bitcast.1.core, s32[1,1024]{1,0:T(1,128)} %bitcast.9, bf16[10,32,1024]{2,1,0:T(8,128)(2,1)} %v_hbm.3, bf16[1024,640]{1,0:T(8,128)(2,1)} %s_hbm.3), custom_call_target="tpu_custom_call" | custom-call | tf_op jit(solution)/shard_map/coef/pallas_call | solution.py:253
  3.0 8.9 %all-gather = f32[320,640]{1,0:T(8,128)S(1)} all-gather(f32[160,640]{1,0:T(8,128)S(1)} %get-tuple-element.15), channel_id=2, replica_groups=mesh['y'=4,'zh'=4,'z1'=2,'z0'=2,'x'=4,'c'=2] {'c'}, dimensions={0}, use_global_device_ids=true | all-gather | bytes 1228800 | tf_op jit(solution)/shard_map/all_gather | solution.py:270
  11.8 0.0 copy-start.1
  11.8 0.0 copy-start.2
  11.9 9.9 %all_to_all.15.got_ref = f32[8,16,640]{2,1,0:T(8,128)S(1)} all-to-all(f32[8,16,640]{2,1,0:T(8,128)S(1)} %bitcast.8), channel_id=1, replica_groups=mesh['y'=4,'zh'=4,'z1'=2,'z0'=2,'x'=4,'c'=2] {'x','z0'}, dimensions={0} | all-to-all | bytes 655360 | tf_op jit(solution)/shard_map/all_to_all | solution.py:279
  21.8 0.7 %middle.1 = (f32[32,2,640]{2,1,0:T(2,128)}, f32[8,8,640]{2,1,0:T(8,128)S(1)}, f32[8,128]{1,0:T(8,128)S(1)}) custom-call(s32[1]{0:T(128)} %bitcast._.me, f32[8,16,640]{2,1,0:T(8,128)S(1)} %all_to_all.15.got_ref), custom_call_target="tpu_custom_call" | custom-call | tf_op jit(solution)/shard_map/middle/pallas_call | solution.py:280
  22.5 14.2 %all-to-all-start.1 = ((f32[32,2,640]{2,1,0:T(2,128)}), f32[32,2,640]{2,1,0:T(2,128)S(1)}, u32[]{:S(2)}, u32[]{:S(2)}) async-start(f32[32,2,640]{2,1,0:T(2,128)} %get-tuple-element.16), calls=%async_computation.1 | async-start | bytes 327680 | tf_op jit(solution)/shard_map/all_to_all | solution.py:318
  36.8 0.0 copy-done.1
  36.8 0.0 copy-done.2
  36.8 9.2 %local.1 = (f32[256,640]{1,0:T(8,128)S(1)}, f32[768,640]{1,0:T(8,128)}, bf16[1024,256]{1,0:T(8,128)(2,1)S(1)}, f32[8,128]{1,0:T(8,128)S(1)}) custom-call(s32[10]{0:T(128)S(1)} %copy-done.2, s32[1]{0:T(128)} %bitcast.1.core, s32[1,1024]{1,0:T(1,128)S(1)} %bitcast.10, bf16[1024,640]{1,0:T(8,128)(2,1)} %s_hbm.3, bf16[1024,512]{1,0:T(8,128)(2,1)} %leaf_hbm.1, ...), custom_call_target="tpu_custom_call" | custom-call | flops 4700000256 | bytes 8000000 | tf_op jit(solution)/shard_map/local/pallas_call | solution.py:288
  46.0 0.0 copy-start
  46.0 5.1 %all-to-all-done.1.got_ref = f32[32,2,640]{2,1,0:T(2,128)S(1)} async-done(((f32[32,2,640]{2,1,0:T(2,128)}), f32[32,2,640]{2,1,0:T(2,128)S(1)}, u32[]{:S(2)}, u32[]{:S(2)}) %all-to-all-start.1) | async-done | bytes 163872 | tf_op jit(solution)/shard_map/all_to_all | solution.py:318
  51.1 0.1 far.1
  51.2 9.1 %all_to_all.16 = f32[8,16,640]{2,1,0:T(8,128)S(1)} all-to-all(f32[8,16,640]{2,1,0:T(8,128)S(1)} %far.1), channel_id=1, replica_groups=mesh['y'=4,'zh'=4,'z1'=2,'z0'=2,'x'=4,'c'=2] {'x','z0'}, dimensions={0} | all-to-all | bytes 655360 | tf_op jit(solution)/shard_map/all_to_all | solution.py:328
  60.3 7.8 %all_gather.11.far_ref = f32[256,640]{1,0:T(8,128)S(1)} all-gather(f32[128,640]{1,0:T(8,128)S(1)} %bitcast.11), channel_id=1, replica_groups=mesh['y'=4,'zh'=4,'z1'=2,'z0'=2,'x'=4,'c'=2] {'c'}, dimensions={0}, use_global_device_ids=true | all-gather | bytes 983040 | tf_op jit(solution)/shard_map/all_gather | solution.py:329
  68.1 0.0 copy-done
  68.1 1.4 %last.1 = bf16[1024,640]{1,0:T(8,128)(2,1)} custom-call(f32[256,640]{1,0:T(8,128)S(1)} %all_gather.11.far_ref, bf16[1024,256]{1,0:T(8,128)(2,1)S(1)} %get-tuple-element.20.ut_ref, f32[256,640]{1,0:T(8,128)S(1)} %get-tuple-element.21.top_ref, f32[768,640]{1,0:T(8,128)S(1)} %copy-done), custom_call_target="tpu_custom_call" | custom-call | tf_op jit(solution)/shard_map/last/pallas_call | solution.py:330
  (1 shorter events, 0.0 us)
Async XLA Ops:
  11.8 25.0 %copy-start.1 = (s32[1024]{0:T(1024)S(1)}, s32[1024]{0:T(1024)}, u32[]{:S(2)}) copy-start(s32[1024]{0:T(1024)} %param.7) | copy-start | bytes 12292
  11.8 25.0 %copy-start.2 = (s32[10]{0:T(128)S(1)}, s32[10]{0:T(128)}, u32[]{:S(2)}) copy-start(s32[10]{0:T(128)} %ranks.1) | copy-start | bytes 124
  22.5 28.6 %all-to-all-start.1 = ((f32[32,2,640]{2,1,0:T(2,128)}), f32[32,2,640]{2,1,0:T(2,128)S(1)}, u32[]{:S(2)}, u32[]{:S(2)}) async-start(f32[32,2,640]{2,1,0:T(2,128)} %get-tuple-element.16), calls=%async_computation.1 | async-start | bytes 327680 | tf_op jit(solution)/shard_map/all_to_all | solution.py:318
  46.0 22.0 %copy-start = (f32[768,640]{1,0:T(8,128)S(1)}, f32[768,640]{1,0:T(8,128)}, u32[]{:S(2)}) copy-start(f32[768,640]{1,0:T(8,128)} %get-tuple-element.22.low_ref) | copy-start | bytes 5898244
